TPU v7x, 512 devices: a whole 4x4x16 slice. The times are simulated.
512 devices in a mesh: smp: 32 (over y, z_lo), var: 16 (over x, z_hi, core).
Axes of the slice: x: 4, y: 4, z: 16 (z_hi: 2, z_lo: 8; z = z_hi * 8 + z_lo), core: 2. Of those that a mesh axis runs over, the one named last changes fastest.
Arguments:
- dosage: int32 [2048, 8192], P('smp', 'var'), may hold values from -2147483648 to 2147483647, as said below
- shares_init: float32 [12, 32768], P(None, ('smp', 'var')), may hold values from 0.1 to 1
- freqs_init: float32 [12, 8192], P(None, ('var', 'smp')), may hold values from 0.019 to 0.981
Outputs:
- shares: float32 [12, 32768], P(None, ('smp', 'var'))
- freqs: float32 [12, 8192], P(None, ('var', 'smp'))
Inputs may be any that keep to these rules, and one draw needn't show every extreme that they name: Every 2-bit code in a word of dosage is 0, 1, 2 or 3, and 3 marks a missing genotype.
All inputs are finite; a program needn't handle non-finite values.
Results may differ from a plain program's by a relative error of at most 0.0003.
Values sent between devices are 32-bit elements; how exact they have to be, the bound alone decides.
No kernel may reach another device: no remote copies, remote signals or barrier semaphores. Data moves between devices by JAX's collectives and lax.ppermute only.
A program may use at most 64 MiB of HBM per device.

v0:
```python
import jax
import jax.numpy as jnp
from jax import lax
from jax.sharding import PartitionSpec as P

ITERS = 2


HIGH = lax.Precision.HIGHEST


def copy_for_each(shard, axis):
    peers = lax.axis_size(axis)
    return lax.all_to_all(
        jnp.broadcast_to(shard[None], (peers, *shard.shape)), axis, 0, 0, tiled=True
    )


def joined_along(pieces, dim):
    pieces = jnp.moveaxis(pieces, 0, dim)
    shape = pieces.shape
    return pieces.reshape(*shape[:dim], shape[dim] * shape[dim + 1], *shape[dim + 2 :])


def collect(shard, axis, dim):
    pieces = copy_for_each(shard, axis)
    return joined_along(pieces, dim)


def split_up(shard, dim, peers):
    shape = shard.shape
    pieces = shard.reshape(*shape[:dim], peers, shape[dim] // peers, *shape[dim + 1 :])
    return jnp.moveaxis(pieces, dim, 0)


def sum_at_owner(shard, axis, dim):
    peers = lax.axis_size(axis)
    pieces = lax.all_to_all(split_up(shard, dim, peers), axis, 0, 0, tiled=True)
    return jnp.sum(pieces, axis=0)


def side_by_side(arrays, axis, dim, along):
    both = jnp.concatenate(arrays, axis=along)
    result, at, finished = (sum_at_owner(both, axis, dim), 0, [])
    for a in arrays:
        finished.append(lax.slice_in_dim(result, at, at + a.shape[along], axis=along))
        at += a.shape[along]
    return tuple(finished)


def unpack_codes(packed):
    shifts = 2 * jnp.arange(16, dtype=jnp.int32)
    codes = jnp.bitwise_and(jnp.right_shift(packed[:, None, :], shifts[None, :, None]), 3)
    return codes.reshape(packed.shape[0] * 16, packed.shape[1])


def expect_sums(packed, shares_block, freqs_block):
    codes = unpack_codes(packed)
    live = (codes < 3).astype(jnp.float32)
    allele_f = live * codes.astype(jnp.float32)
    probs = jnp.einsum("kn,km->nm", shares_block, freqs_block, precision=HIGH)
    ratio_alt = allele_f / probs
    ratio_ref = (2.0 * live - allele_f) / (1.0 - probs)
    sum_q = jnp.einsum("km,nm->kn", freqs_block, ratio_alt, precision=HIGH) + jnp.einsum(
        "km,nm->kn", 1.0 - freqs_block, ratio_ref, precision=HIGH
    )
    sum_a = jnp.einsum("kn,nm->km", shares_block, ratio_alt, precision=HIGH)
    sum_b = jnp.einsum("kn,nm->km", shares_block, ratio_ref, precision=HIGH)
    return (sum_q, sum_a, sum_b)


def block_sums(packed, shares_block, freqs_block):
    word_rows = min(packed.shape[0], 16)
    blocks = packed.shape[0] // word_rows
    populations = shares_block.shape[0]
    packed_blocks = packed.reshape(blocks, word_rows, packed.shape[1])
    share_blocks = shares_block.reshape(populations, blocks, word_rows * 16).transpose(1, 0, 2)

    def one_block(carry, items):
        sum_q, sum_a, sum_b = expect_sums(items[0], items[1], freqs_block)
        return ((carry[0] + sum_a, carry[1] + sum_b), sum_q)

    start = (jnp.zeros(freqs_block.shape, jnp.float32), jnp.zeros(freqs_block.shape, jnp.float32))
    totals, sums_q = lax.scan(one_block, start, (packed_blocks, share_blocks))
    sum_q = sums_q.transpose(1, 0, 2).reshape(populations, shares_block.shape[1])
    return (sum_q, totals[0], totals[1])


def renew_shares(shares_block, sum_q):
    numer = shares_block * sum_q
    return (numer + 0.5) / (jnp.sum(numer, axis=0, keepdims=True) + 0.5 * shares_block.shape[0])


def renew_freqs(freqs_block, sum_a, sum_b):
    alt_part = freqs_block * sum_a
    ref_part = (1.0 - freqs_block) * sum_b
    return (alt_part + 0.5) / (alt_part + ref_part + 1.0)


def body(dosage, shares_init, freqs_init):
    own_shares = shares_init / jnp.sum(shares_init, axis=0, keepdims=True)
    own_freqs = freqs_init
    share_width = shares_init.shape[1]
    freq_width = freqs_init.shape[1]
    shares_block = collect(own_shares, "var", 1)
    freqs_block = collect(own_freqs, "smp", 1)
    for iteration in range(ITERS):
        part_q, part_a, part_b = block_sums(dosage, shares_block, freqs_block)
        sum_q = sum_at_owner(part_q, "var", 1)
        sum_a, sum_b = side_by_side((part_a, part_b), "smp", 1, 0)
        old_shares = lax.dynamic_slice_in_dim(
            shares_block, lax.axis_index("var") * share_width, share_width, 1
        )
        old_freqs = lax.dynamic_slice_in_dim(
            freqs_block, lax.axis_index("smp") * freq_width, freq_width, 1
        )
        own_shares = renew_shares(old_shares, sum_q)
        own_freqs = renew_freqs(old_freqs, sum_a, sum_b)
        if iteration + 1 < ITERS:
            shares_block = collect(own_shares, "var", 1)
            freqs_block = collect(own_freqs, "smp", 1)
    return (own_shares, own_freqs)


def solution(mesh):
    placed = (P("smp", "var"), P(None, ("smp", "var")), P(None, ("var", "smp")))
    return jax.shard_map(
        body,
        mesh=mesh,
        in_specs=placed,
        out_specs=(P(None, ("smp", "var")), P(None, ("var", "smp"))),
        check_vma=False,
    )
```

profile of v0, /device:TPU:1, one launch (start us, length us, event | category | flops | bytes accessed | tf_op | source)
XLA Modules:
  0.0 190.5 jit_solution(16468203960508968355)
XLA Ops:
  2.1 16.2 %all-to-all-start.1 = ((f32[32,1,192]{2,1,0:T(1,128)}), f32[32,1,192]{2,1,0:T(1,128)S(1)}, u32[]{:S(2)}, u32[]{:S(2)}) async-start(f32[32,1,192]{2,1,0:T(1,128)} %reshape.66), calls=%async_computation.1 | async-start | bytes 65536 | tf_op jit(solution)/shard_map/all_to_all | solution.py:14
  19.1 10.6 %all-to-all-done.1 = f32[32,1,192]{2,1,0:T(1,128)S(1)} async-done(((f32[32,1,192]{2,1,0:T(1,128)}), f32[32,1,192]{2,1,0:T(1,128)S(1)}, u32[]{:S(2)}, u32[]{:S(2)}) %all-to-all-start.1) | async-done | bytes 24608 | tf_op jit(solution)/shard_map/all_to_all | solution.py:14
  29.7 12.2 %all-to-all-start = ((f32[16,1,768]{2,1,0:T(1,128)}), f32[16,1,768]{2,1,0:T(1,128)S(1)}, u32[]{:S(2)}, u32[]{:S(2)}) async-start(f32[16,1,768]{2,1,0:T(1,128)} %reshape.64), calls=%async_computation | async-start | bytes 98304 | tf_op jit(solution)/shard_map/all_to_all | solution.py:14
  43.4 13.0 %all-to-all-done = f32[16,1,768]{2,1,0:T(1,128)S(1)} async-done(((f32[16,1,768]{2,1,0:T(1,128)}), f32[16,1,768]{2,1,0:T(1,128)S(1)}, u32[]{:S(2)}, u32[]{:S(2)}) %all-to-all-start) | async-done | bytes 49184 | tf_op jit(solution)/shard_map/all_to_all | solution.py:14
  57.4 0.8 copy-done
  58.2 10.9 %while.30 = (s32[]{:T(128)}, f32[12,512]{1,0:T(8,128)S(1)}, f32[12,512]{1,0:T(8,128)S(1)}, f32[4,12,256]{2,1,0:T(8,128)S(1)}, f32[4,12,256]{2,0,1:T(4,128)S(1)},...) while((s32[]{:T(128)}, f32[12,512]{1,0:T(8,128)S(1)}, ...), condition=%wide.region_2.3_spmd.clone, body=%wide.region_1.2_spmd.clone.sunk | while | flops 95716368 | bytes 3535092 | solution.py:84
  63.7 0.8 fusion.71
  70.0 3.7 %all-to-all-start.2 = ((f32[16,1,768]{2,1,0:T(1,128)}), f32[16,1,768]{2,1,0:T(1,128)S(1)}, u32[]{:S(2)}, u32[]{:S(2)}) async-start(f32[16,1,768]{2,1,0:T(1,128)} %reshape.68), calls=%async_computation.2 | async-start | bytes 98304 | tf_op jit(solution)/shard_map/all_to_all | solution.py:38
  74.3 0.8 reshape.72
  75.1 13.1 %all-to-all-done.2 = f32[16,1,768]{2,1,0:T(1,128)S(1)} async-done(((f32[16,1,768]{2,1,0:T(1,128)}), f32[16,1,768]{2,1,0:T(1,128)S(1)}, u32[]{:S(2)}, u32[]{:S(2)}) %all-to-all-start.2) | async-done | bytes 49184 | tf_op jit(solution)/shard_map/all_to_all | solution.py:38
  88.2 4.2 %all-to-all-start.4 = ((f32[32,1,384]{2,1,0:T(1,128)}), f32[32,1,384]{2,1,0:T(1,128)S(1)}, u32[]{:S(2)}, u32[]{:S(2)}) async-start(f32[32,1,384]{2,1,0:T(1,128)} %reshape.72), calls=%async_computation.4 | async-start | bytes 98304 | tf_op jit(solution)/shard_map/all_to_all | solution.py:38
  93.4 10.5 %all-to-all-done.4 = f32[32,1,384]{2,1,0:T(1,128)S(1)} async-done(((f32[32,1,384]{2,1,0:T(1,128)}), f32[32,1,384]{2,1,0:T(1,128)S(1)}, u32[]{:S(2)}, u32[]{:S(2)}) %all-to-all-start.4) | async-done | bytes 49184 | tf_op jit(solution)/shard_map/all_to_all | solution.py:38
  105.8 3.8 %all-to-all-start.5 = ((f32[32,1,192]{2,1,0:T(1,128)}), f32[32,1,192]{2,1,0:T(1,128)S(1)}, u32[]{:S(2)}, u32[]{:S(2)}) async-start(f32[32,1,192]{2,1,0:T(1,128)} %reshape.74), calls=%async_computation.5 | async-start | bytes 65536 | tf_op jit(solution)/shard_map/all_to_all | solution.py:14
  110.5 10.6 %all-to-all-done.5 = f32[32,1,192]{2,1,0:T(1,128)S(1)} async-done(((f32[32,1,192]{2,1,0:T(1,128)}), f32[32,1,192]{2,1,0:T(1,128)S(1)}, u32[]{:S(2)}, u32[]{:S(2)}) %all-to-all-start.5) | async-done | bytes 24608 | tf_op jit(solution)/shard_map/all_to_all | solution.py:14
  121.0 6.3 %all-to-all-start.3 = ((f32[16,1,768]{2,1,0:T(1,128)}), f32[16,1,768]{2,1,0:T(1,128)S(1)}, u32[]{:S(2)}, u32[]{:S(2)}) async-start(f32[16,1,768]{2,1,0:T(1,128)} %reshape.70), calls=%async_computation.3 | async-start | bytes 98304 | tf_op jit(solution)/shard_map/all_to_all | solution.py:14
  128.3 13.6 %all-to-all-done.3 = f32[16,1,768]{2,1,0:T(1,128)S(1)} async-done(((f32[16,1,768]{2,1,0:T(1,128)}), f32[16,1,768]{2,1,0:T(1,128)S(1)}, u32[]{:S(2)}, u32[]{:S(2)}) %all-to-all-start.3) | async-done | bytes 49184 | tf_op jit(solution)/shard_map/all_to_all | solution.py:14
  142.8 10.9 %while.31 = (s32[]{:T(128)}, f32[12,512]{1,0:T(8,128)S(1)}, f32[12,512]{1,0:T(8,128)S(1)}, f32[4,12,256]{2,1,0:T(8,128)S(1)}, f32[4,12,256]{2,0,1:T(4,128)S(1)},...) while((s32[]{:T(128)}, f32[12,512]{1,0:T(8,128)S(1)}, ...), condition=%wide.region_7.8_spmd.clone, body=%wide.region_6.7_spmd.clone.sunk | while | flops 95716368 | bytes 3535092 | solution.py:84
  145.7 0.8 fusion.80
  151.1 0.8 fusion.80
  154.6 3.7 %all-to-all-start.6 = ((f32[16,1,768]{2,1,0:T(1,128)}), f32[16,1,768]{2,1,0:T(1,128)S(1)}, u32[]{:S(2)}, u32[]{:S(2)}) async-start(f32[16,1,768]{2,1,0:T(1,128)} %reshape.76), calls=%async_computation.6 | async-start | bytes 98304 | tf_op jit(solution)/shard_map/all_to_all | solution.py:38
  159.0 0.8 reshape.78
  159.8 13.1 %all-to-all-done.6 = f32[16,1,768]{2,1,0:T(1,128)S(1)} async-done(((f32[16,1,768]{2,1,0:T(1,128)}), f32[16,1,768]{2,1,0:T(1,128)S(1)}, u32[]{:S(2)}, u32[]{:S(2)}) %all-to-all-start.6) | async-done | bytes 49184 | tf_op jit(solution)/shard_map/all_to_all | solution.py:38
  172.9 4.5 %all-to-all-start.7 = ((f32[32,1,384]{2,1,0:T(1,128)}), f32[32,1,384]{2,1,0:T(1,128)S(1)}, u32[]{:S(2)}, u32[]{:S(2)}) async-start(f32[32,1,384]{2,1,0:T(1,128)} %reshape.78), calls=%async_computation.7 | async-start | bytes 98304 | tf_op jit(solution)/shard_map/all_to_all | solution.py:38
  179.0 9.9 %all-to-all-done.7 = f32[32,1,384]{2,1,0:T(1,128)S(1)} async-done(((f32[32,1,384]{2,1,0:T(1,128)}), f32[32,1,384]{2,1,0:T(1,128)S(1)}, u32[]{:S(2)}, u32[]{:S(2)}) %all-to-all-start.7) | async-done | bytes 49184 | tf_op jit(solution)/shard_map/all_to_all | solution.py:38
  (155 shorter events, 35.5 us)
Async XLA Ops:
  2.1 16.2 %copy-start.1 = (f32[12,64]{1,0:T(8,128)S(1)}, f32[12,64]{1,0:T(8,128)}, u32[]{:S(2)}) copy-start(f32[12,64]{1,0:T(8,128)} %param.8) | copy-start | bytes 9220
  2.1 27.6 %all-to-all-start.1 = ((f32[32,1,192]{2,1,0:T(1,128)}), f32[32,1,192]{2,1,0:T(1,128)S(1)}, u32[]{:S(2)}, u32[]{:S(2)}) async-start(f32[32,1,192]{2,1,0:T(1,128)} %reshape.66), calls=%async_computation.1 | async-start | bytes 65536 | tf_op jit(solution)/shard_map/all_to_all | solution.py:14
  29.7 26.7 %all-to-all-start = ((f32[16,1,768]{2,1,0:T(1,128)}), f32[16,1,768]{2,1,0:T(1,128)S(1)}, u32[]{:S(2)}, u32[]{:S(2)}) async-start(f32[16,1,768]{2,1,0:T(1,128)} %reshape.64), calls=%async_computation | async-start | bytes 98304 | tf_op jit(solution)/shard_map/all_to_all | solution.py:14
  57.2 0.9 copy-start
  70.0 18.3 %all-to-all-start.2 = ((f32[16,1,768]{2,1,0:T(1,128)}), f32[16,1,768]{2,1,0:T(1,128)S(1)}, u32[]{:S(2)}, u32[]{:S(2)}) async-start(f32[16,1,768]{2,1,0:T(1,128)} %reshape.68), calls=%async_computation.2 | async-start | bytes 98304 | tf_op jit(solution)/shard_map/all_to_all | solution.py:38
  88.2 15.7 %all-to-all-start.4 = ((f32[32,1,384]{2,1,0:T(1,128)}), f32[32,1,384]{2,1,0:T(1,128)S(1)}, u32[]{:S(2)}, u32[]{:S(2)}) async-start(f32[32,1,384]{2,1,0:T(1,128)} %reshape.72), calls=%async_computation.4 | async-start | bytes 98304 | tf_op jit(solution)/shard_map/all_to_all | solution.py:38
  105.8 15.3 %all-to-all-start.5 = ((f32[32,1,192]{2,1,0:T(1,128)}), f32[32,1,192]{2,1,0:T(1,128)S(1)}, u32[]{:S(2)}, u32[]{:S(2)}) async-start(f32[32,1,192]{2,1,0:T(1,128)} %reshape.74), calls=%async_computation.5 | async-start | bytes 65536 | tf_op jit(solution)/shard_map/all_to_all | solution.py:14
  121.0 20.9 %all-to-all-start.3 = ((f32[16,1,768]{2,1,0:T(1,128)}), f32[16,1,768]{2,1,0:T(1,128)S(1)}, u32[]{:S(2)}, u32[]{:S(2)}) async-start(f32[16,1,768]{2,1,0:T(1,128)} %reshape.70), calls=%async_computation.3 | async-start | bytes 98304 | tf_op jit(solution)/shard_map/all_to_all | solution.py:14
  154.6 18.3 %all-to-all-start.6 = ((f32[16,1,768]{2,1,0:T(1,128)}), f32[16,1,768]{2,1,0:T(1,128)S(1)}, u32[]{:S(2)}, u32[]{:S(2)}) async-start(f32[16,1,768]{2,1,0:T(1,128)} %reshape.76), calls=%async_computation.6 | async-start | bytes 98304 | tf_op jit(solution)/shard_map/all_to_all | solution.py:38
  172.9 16.0 %all-to-all-start.7 = ((f32[32,1,384]{2,1,0:T(1,128)}), f32[32,1,384]{2,1,0:T(1,128)S(1)}, u32[]{:S(2)}, u32[]{:S(2)}) async-start(f32[32,1,384]{2,1,0:T(1,128)} %reshape.78), calls=%async_computation.7 | async-start | bytes 98304 | tf_op jit(solution)/shard_map/all_to_all | solution.py:38
where the time goes:
time: 191 us
  waiting for transfers between devices  94.4 us (49%)
  starting transfers between devices  54.6 us (29%)
  matrix products  20.6 us (11%)
  local copies, waits for them, and re-layouts  13 us (7%)
  other arithmetic  6.65 us (3%)
    all_to_all x4, waiting for transfers between devices, copy_for_each(): lax.all_to_all(jnp.broadcast_to(shard[None], (peers, *shard.shape)), axis...  47.8 us
    all_to_all x4, waiting for transfers between devices, sum_at_owner(): pieces = lax.all_to_all(split_up(shard, dim, peers), axis, 0, 0, tiled=True)  46.6 us
    all_to_all x4, starting transfers between devices, copy_for_each(): lax.all_to_all(jnp.broadcast_to(shard[None], (peers, *shard.shape)), axis...  38.5 us
    all_to_all x4, starting transfers between devices, sum_at_owner(): pieces = lax.all_to_all(split_up(shard, dim, peers), axis, 0, 0, tiled=True)  16.1 us
    unnamed x23, local copies, waits for them, and re-layouts  8.63 us
    dot_general x8, matrix products, expect_sums(): probs = jnp.einsum('kn,km->nm', shares_block, freqs_block, precision=HIGH)  6.2 us
    dot_general x8, matrix products, expect_sums(): jnp.einsum('km,nm->kn', 1.0 - freqs_block, ratio_ref, precision=HIGH)  4.22 us
    dot_general x8, matrix products, expect_sums(): jnp.einsum('km,nm->kn', freqs_block, ratio_alt, precision=HIGH)  4.12 us
  transfers between devices with their start and end apart: 8, of which 8 were waited for; matrix products, arithmetic and copies ran while one was open for 5% of the time, Pallas kernels for 0%

commit v1 on v0

v1 whole, which is shorter than its diff:
```python
import jax
import jax.numpy as jnp
from jax import lax
from jax.experimental import pallas as pl
from jax.experimental.pallas import tpu as pltpu
from jax.sharding import Mesh, PartitionSpec as P

K = 12
PAD = 16
LANES = 128
ROWS = 256

AXES = ("y", "zl", "x", "zh", "c")
SIZES = (4, 8, 4, 2, 2)
SMP = ("y", "zl")
VAR = ("x", "zh", "c")
NEAR = ("y", "x", "c")
FAR = ("zl", "zh")
N_SMP, N_VAR, N_NEAR, N_FAR = 32, 16, 32, 16
N_Y, N_XC, N_ZL, N_ZH = 4, 8, 8, 2

f32 = jnp.float32
bf16 = jnp.bfloat16


def tile(i):
    return slice(i * LANES, (i + 1) * LANES)


def lane():
    return lax.broadcasted_iota(jnp.int32, (8, LANES), 1)


def roll(x, shift):
    shift = shift % LANES
    return pltpu.roll(x, shift, 1) if shift else x


def two_parts(x):
    high = x.astype(bf16)
    return high, (x - high.astype(f32)).astype(bf16)


def three_parts(x):
    high = x.astype(bf16)
    return (high, *two_parts(x - high.astype(f32)))


def dot(a, b, over_a, over_b):
    return lax.dot_general(
        a, b, (((over_a,), (over_b,)), ((), ())), preferred_element_type=f32
    )


def fold(x):
    return x[:PAD] + x[PAD:]


def block_sums(dosage_ref, shares, freqs):
    qh, qm, ql = three_parts(shares)
    fh, fm, fl = three_parts(freqs)
    q_side = jnp.concatenate([qh, qh, qm, qh, ql, qm], 0)
    f_side = jnp.concatenate([fh, fm, fh, fl, fh, fm], 0)
    q_two = jnp.concatenate([qh, qm], 0)
    f_two = jnp.concatenate([fh, fm], 0)
    g_two = jnp.concatenate(two_parts(1.0 - freqs), 0)
    shift = 2 * lax.broadcasted_iota(jnp.int32, (16, freqs.shape[1]), 0)
    sums_q, sum_a, sum_b = [], None, None
    for at in range(0, shares.shape[1], ROWS):
        probs = dot(q_side[:, at : at + ROWS], f_side, 0, 0)
        codes = jnp.concatenate(
            [
                jnp.bitwise_and(
                    jnp.right_shift(jnp.broadcast_to(dosage_ref[w : w + 1, :], shift.shape), shift), 3
                )
                for w in range(at // 16, (at + ROWS) // 16)
            ],
            0,
        )
        rest = 1.0 - probs
        inverse = jnp.where(codes < 3, 1.0 / (probs * rest), 0.0)
        allele = codes.astype(f32)
        ah, al = two_parts(allele * (rest * inverse))
        bh, bl = two_parts((2.0 - allele) * (probs * inverse))
        sums_q.append(
            dot(f_two, ah, 1, 1) + dot(f_two, al, 1, 1) + dot(g_two, bh, 1, 1) + dot(g_two, bl, 1, 1)
        )
        q_part = q_two[:, at : at + ROWS]
        part_a = dot(q_part, ah, 1, 0) + dot(q_part, al, 1, 0)
        part_b = dot(q_part, bh, 1, 0) + dot(q_part, bl, 1, 0)
        sum_a = part_a if sum_a is None else sum_a + part_a
        sum_b = part_b if sum_b is None else sum_b + part_b
    return fold(jnp.concatenate(sums_q, 1)), fold(sum_a), fold(sum_b)


def first_kernel(shares_ref, freqs_ref, v_out, s_out, q_tmp, f_tmp):
    raw = shares_ref[...]
    own = raw / jnp.sum(raw, axis=0, keepdims=True)
    q_tmp[...] = jnp.zeros_like(q_tmp)
    f_tmp[...] = jnp.zeros_like(f_tmp)
    q_tmp[:, 0:64] = own[0:8]
    q_tmp[0:4, 64:128] = own[8:12]
    f_tmp[:, 0:16] = freqs_ref[0:8, :]
    f_tmp[0:4, 16:32] = freqs_ref[8:12, :]
    for i in range(N_VAR):
        v_out[i] = q_tmp[...]
    for i in range(N_SMP):
        s_out[i] = f_tmp[...]


def shares_of(v_in):
    low, high = [], []
    left = lane() < 64
    for t in range(8):
        a, b = v_in[2 * t], v_in[2 * t + 1]
        low.append(jnp.where(left, a, roll(b, 64)))
        high.append(jnp.where(left, roll(a, 64), b))
    return jnp.concatenate([jnp.concatenate(low, 1), jnp.concatenate(high, 1)], 0)


def freqs_of(s_in):
    low, high = [], []
    place = lane() // 16
    for t in range(4):
        lo = hi = jnp.zeros((8, LANES), f32)
        for i in range(8):
            a = s_in[8 * t + i]
            lo = jnp.where(place == i, roll(a, 16 * i), lo)
            hi = jnp.where(place == i, roll(a, 16 * i - 16), hi)
        low.append(lo)
        high.append(hi)
    return jnp.concatenate([jnp.concatenate(low, 1), jnp.concatenate(high, 1)], 0)


def one_kernel(dosage_ref, v_in, s_in, slots, q_out, f_out, sq_tmp, sa_tmp):
    shares = shares_of(v_in)
    freqs = freqs_of(s_in)
    q_out[...] = shares
    f_out[...] = freqs
    sum_q, sum_a, sum_b = block_sums(dosage_ref, shares, freqs)
    sq_tmp[...] = sum_q
    sa_tmp[0:12] = sum_a[0:12]
    sa_tmp[12:24] = sum_b[0:12]
    slots[...] = jnp.zeros_like(slots)
    for s in range(N_NEAR):
        t, q = divmod(s, 4)
        slots[s, 0:3] = sq_tmp[3 * q : 3 * q + 3, tile(t)]
        t, g = divmod(s, 8)
        slots[s, 3:6] = sa_tmp[3 * g : 3 * g + 3, tile(t)]


def near_sums_kernel(idx, near_in, far_out, q_out, a_tmp):
    for y in range(N_Y):
        q_out[3 * y : 3 * y + 3] = sum(near_in[y * N_XC + g] for g in range(N_XC))[0:3]
    q_out[12:24] = jnp.zeros((12, LANES), f32)
    for g in range(N_XC):
        a_tmp[3 * g : 3 * g + 3] = sum(near_in[y * N_XC + g] for y in range(N_Y))[3:6]
    for h in range(N_ZH):
        sent = jnp.where(idx[3] == h, a_tmp[...], q_out[...])
        for i in range(N_ZL):
            far_out[i * N_ZH + h] = sent


def far_sums_kernel(idx, far_in, q_in, near_out, q_tmp, a_tmp):
    zh = idx[3]
    a_tmp[...] = sum(far_in[i * N_ZH + zh] for i in range(N_ZL))
    q_tmp[...] = q_in[...] + far_in[idx[2] * N_ZH + 1 - zh]
    near_out[...] = jnp.zeros_like(near_out)
    for y in range(N_Y):
        for g in range(N_XC):
            near_out[y * N_XC + g, 0:3] = q_tmp[3 * y : 3 * y + 3]
            near_out[y * N_XC + g, 3:6] = a_tmp[3 * g : 3 * g + 3]


def two_kernel(idx, dosage_ref, near_in, q_in, f_in, v_out, s_out, own_q, own_f, sq_tmp, sa_tmp, q_tmp, f_tmp):
    for s in range(N_NEAR):
        t, q = divmod(s, 4)
        sq_tmp[3 * q : 3 * q + 3, tile(t)] = near_in[s, 0:3]
        t, g = divmod(s, 8)
        sa_tmp[3 * g : 3 * g + 3, tile(t)] = near_in[s, 3:6]
    q_tmp[...] = q_in[...]
    f_tmp[...] = f_in[...]
    numer = q_tmp[0:12] * sq_tmp[0:12]
    q_tmp[0:12] = (numer + 0.5) / (jnp.sum(numer, axis=0, keepdims=True) + 0.5 * K)
    old = f_tmp[0:12]
    alt_part = old * sa_tmp[0:12]
    f_tmp[0:12] = (alt_part + 0.5) / (alt_part + (1.0 - old) * sa_tmp[12:24] + 1.0)

    left = lane() < 64
    t = pl.multiple_of(idx[0] // 2 * LANES, LANES)
    a, b = q_tmp[0:8, pl.ds(t, LANES)], q_tmp[8:16, pl.ds(t, LANES)]
    own_q[...] = jnp.where(
        idx[0] % 2 == 0, jnp.where(left, a, roll(b, 64)), jnp.where(left, roll(a, 64), b)
    )
    t = pl.multiple_of(idx[1] // 8 * LANES, LANES)
    a, b = f_tmp[0:8, pl.ds(t, LANES)], f_tmp[8:16, pl.ds(t, LANES)]
    back = LANES - 16 * (idx[1] % 8)
    own_f[...] = jnp.where(lane() < 16, pltpu.roll(a, back, 1), pltpu.roll(b, back + 16, 1))

    sum_q, sum_a, sum_b = block_sums(dosage_ref, q_tmp[...], f_tmp[...])
    for t in range(8):
        a, b = sum_q[0:8, tile(t)], sum_q[8:16, tile(t)]
        v_out[2 * t] = jnp.where(left, a, roll(b, 64))
        v_out[2 * t + 1] = jnp.where(left, roll(a, 64), b)
    place = lane() // 16
    for t in range(4):
        for i in range(8):
            got = roll(sum_a[0:8, tile(t)], -16 * i)
            got = jnp.where(place == 1, roll(sum_a[8:16, tile(t)], 16 - 16 * i), got)
            got = jnp.where(place == 2, roll(sum_b[0:8, tile(t)], 32 - 16 * i), got)
            s_out[8 * t + i] = jnp.where(place == 3, roll(sum_b[8:16, tile(t)], 48 - 16 * i), got)


def last_kernel(v_in, s_in, own_q, own_f, shares_out, freqs_out):
    row = lax.broadcasted_iota(jnp.int32, (8, LANES), 0)
    held = (lane() < 64) | (row < 4)
    sum_q = sum(v_in[i] for i in range(N_VAR))
    numer = jnp.where(held, own_q[...] * sum_q, 0.0)
    total = jnp.sum(numer, axis=0, keepdims=True)
    total = total + pltpu.roll(total, 64, 1)
    new = (numer + 0.5) / (total + 0.5 * K)
    shares_out[0:8] = new[:, 0:64]
    shares_out[8:12] = new[0:4, 64:128]
    sums = sum(s_in[i] for i in range(N_SMP))
    alt_part = own_f[...] * sums
    ref_part = (1.0 - own_f[...]) * roll(sums, -32)
    new = (alt_part + 0.5) / (alt_part + ref_part + 1.0)
    freqs_out[0:8] = new[:, 0:16]
    freqs_out[8:12] = new[0:4, 16:32]


def f32s(*shape):
    return jax.ShapeDtypeStruct(shape, f32)


def vmem(*shape):
    return pltpu.VMEM(shape, f32)


def call(kernel, scalars, n_in, outs, scratch):
    spec = pl.BlockSpec(memory_space=pltpu.VMEM)
    return pl.pallas_call(
        kernel,
        in_specs=[pl.BlockSpec(memory_space=pltpu.SMEM)] * scalars + [spec] * n_in,
        out_specs=[spec] * len(outs),
        out_shape=outs,
        scratch_shapes=scratch,
    )


def exchange(x, axes):
    return lax.all_to_all(x, axes, 0, 0, tiled=True)


def body(dosage, shares_init, freqs_init):
    idx = jnp.stack(
        [lax.axis_index(VAR), lax.axis_index(SMP), lax.axis_index("zl"), lax.axis_index("zh")]
    ).astype(jnp.int32)
    samples, variants = 16 * dosage.shape[0], dosage.shape[1]
    tiles = lambda n: f32s(n, 8, LANES)
    v_slots, s_slots = call(
        first_kernel, 0, 2, [tiles(N_VAR), tiles(N_SMP)], [vmem(8, LANES), vmem(8, LANES)]
    )(shares_init, freqs_init)
    v_got = exchange(v_slots, VAR)
    s_got = exchange(s_slots, SMP)
    slots, shares, freqs = call(
        one_kernel, 0, 3, [tiles(N_NEAR), f32s(PAD, samples), f32s(PAD, variants)],
        [vmem(PAD, samples), vmem(24, variants)],
    )(dosage, v_got, s_got)
    near_got = exchange(slots, NEAR)
    far_slots, own_sum = call(
        near_sums_kernel, 1, 1, [f32s(N_FAR, 24, LANES), f32s(24, LANES)], [vmem(24, LANES)]
    )(idx, near_got)
    far_got = exchange(far_slots, FAR)
    (near_slots,) = call(
        far_sums_kernel, 1, 2, [tiles(N_NEAR)], [vmem(24, LANES), vmem(24, LANES)]
    )(idx, far_got, own_sum)
    near_got = exchange(near_slots, NEAR)
    v_slots, s_slots, own_q, own_f = call(
        two_kernel, 1, 4, [tiles(N_VAR), tiles(N_SMP), f32s(8, LANES), f32s(8, LANES)],
        [vmem(PAD, samples), vmem(24, variants), vmem(PAD, samples), vmem(PAD, variants)],
    )(idx, dosage, near_got, shares, freqs)
    v_got = exchange(v_slots, VAR)
    s_got = exchange(s_slots, SMP)
    return tuple(
        call(last_kernel, 0, 4, [f32s(*shares_init.shape), f32s(*freqs_init.shape)], [])(
            v_got, s_got, own_q, own_f
        )
    )


def solution(mesh):
    fine = Mesh(mesh.devices.reshape(SIZES), AXES)
    return jax.shard_map(
        body,
        mesh=fine,
        in_specs=(P(SMP, VAR), P(None, SMP + VAR), P(None, VAR + SMP)),
        out_specs=(P(None, SMP + VAR), P(None, VAR + SMP)),
        check_vma=False,
    )
```

time: 191 us -> 164 us (0.86)
  blocking collectives: 0 us -> 130 us
  waiting for transfers between devices: 94.4 us -> 7.05 us
  starting transfers between devices: 54.6 us -> 6.98 us
  matrix products: 20.6 us -> 0 us
  Pallas kernels: 0 us -> 17.2 us
  local copies, waits for them, and re-layouts: 13 us -> 0.66 us
  other arithmetic: 6.65 us -> 0.65 us
    all_to_all x0 -> x6, blocking collectives: none -> 130 us  [exchange(): return lax.all_to_all(x, axes, 0, 0, tiled=True)]
    all_to_all x8 -> x1, waiting for transfers between devices: 94.4 us -> 7.05 us  [exchange(): return lax.all_to_all(x, axes, 0, 0, tiled=True)]
    all_to_all x8 -> x1, starting transfers between devices: 54.6 us -> 6.98 us  [exchange(): return lax.all_to_all(x, axes, 0, 0, tiled=True)]
    dot_general x40 -> x0, matrix products: 20.6 us -> none  [the longest x8 6.2 us: expect_sums(): probs = jnp.einsum('kn,km->nm', shares_block, freqs_block, precision=HIGH)]
    pallas_call x0 -> x6, Pallas kernels: none -> 17.2 us  [the longest x1 5.39 us: body(): call(two_kernel, 1, 4, [tiles(N_VAR), tiles(N_SMP), f32s(8, LANES), f32s(...]
    unnamed x23 -> x6, local copies, waits for them, and re-layouts: 8.63 us -> 0.66 us
    all_to_all x8 -> x0, other arithmetic: 5.31 us -> none  [the longest x4 2.69 us: sum_at_owner(): pieces = lax.all_to_all(split_up(shard, dim, peers), axis, 0, 0, tiled=True)]
  transfers between devices with their start and end apart: 8 -> 1, of which waited for: 8 -> 1; matrix products, arithmetic and copies ran while one was open for 5% -> 0% of each run, Pallas kernels for 0% -> 0%
where the time goes in v1:
time: 164 us; the launch traced here: 163 us
  blocking collectives  130 us (79%)
  Pallas kernels  17.2 us (10%)
  waiting for transfers between devices  7.05 us (4%)
  starting transfers between devices  6.98 us (4%)
    all_to_all x6, blocking collectives, exchange(): return lax.all_to_all(x, axes, 0, 0, tiled=True)  130 us
    all_to_all x1, waiting for transfers between devices, exchange(): return lax.all_to_all(x, axes, 0, 0, tiled=True)  7.05 us
    all_to_all x1, starting transfers between devices, exchange(): return lax.all_to_all(x, axes, 0, 0, tiled=True)  6.98 us
    pallas_call x1, Pallas kernels, body(): call(two_kernel, 1, 4, [tiles(N_VAR), tiles(N_SMP), f32s(8, LANES), f32s(...  5.39 us
    pallas_call x1, Pallas kernels, body(): call(one_kernel, 0, 3, [tiles(N_NEAR), f32s(PAD, samples), f32s(PAD, vari...  5.38 us
  transfers between devices with their start and end apart: 1, of which 1 were waited for; matrix products, arithmetic and copies ran while one was open for 0% of the time, Pallas kernels for 0%

profile of v1, /device:TPU:1, one launch (start us, length us, event | category | flops | bytes accessed | tf_op | source)
XLA Modules:
  0.0 162.7 jit_solution(7462307915411364081)
XLA Ops:
  0.6 1.5 shard_map.50
  2.1 0.0 copy-start.2
  2.1 33.8 %all_to_all.35.v_in = f32[16,8,128]{2,1,0:T(8,128)} all-to-all(f32[16,8,128]{2,1,0:T(8,128)} %get-tuple-element.13), channel_id=1, replica_groups=mesh['y'=4,'zl'=8,'x'=4,'zh'=2,'c'=2] {'x','zh','c'}, dimensions={0} | all-to-all | bytes 131072 | tf_op jit(solution)/shard_map/all_to_all | solution.py:252
  35.9 0.0 copy-done.2
  35.9 19.4 %all_to_all.36.s_in = f32[32,8,128]{2,1,0:T(8,128)} all-to-all(f32[32,8,128]{2,1,0:T(8,128)S(1)} %copy-done.2), channel_id=1, replica_groups=mesh['y'=4,'zl'=8,'x'=4,'zh'=2,'c'=2] {'y','zl'}, dimensions={0} | all-to-all | bytes 262144 | tf_op jit(solution)/shard_map/all_to_all | solution.py:252
  55.4 5.4 %shard_map.51 = (f32[32,8,128]{2,1,0:T(8,128)}, f32[16,1024]{1,0:T(8,128)}, f32[16,512]{1,0:T(8,128)}) custom-call(s32[64,512]{1,0:T(8,128)} %dosage_ref.3, f32[16,8,128]{2,1,0:T(8,128)} %all_to_all.35.v_in, f32[32,8,128]{2,1,0:T(8,128)} %all_to_all.36.s_in), custom_call_target="tpu_custom_call" | custom-call | tf_op jit(solution)/shard_map/pallas_call | solution.py:266
  60.8 7.0 %all-to-all-start.2 = ((f32[32,8,128]{2,1,0:T(8,128)}), f32[32,8,128]{2,1,0:T(8,128)S(1)}, u32[]{:S(2)}, u32[]{:S(2)}) async-start(f32[32,8,128]{2,1,0:T(8,128)} %get-tuple-element.15), calls=%async_computation.2 | async-start | bytes 262144 | tf_op jit(solution)/shard_map/all_to_all | solution.py:252
  67.8 0.7 pad_add_fusion.idx
  68.4 7.0 %all-to-all-done.2.near_in = f32[32,8,128]{2,1,0:T(8,128)S(1)} async-done(((f32[32,8,128]{2,1,0:T(8,128)}), f32[32,8,128]{2,1,0:T(8,128)S(1)}, u32[]{:S(2)}, u32[]{:S(2)}) %all-to-all-start.2) | async-done | bytes 131104 | tf_op jit(solution)/shard_map/all_to_all | solution.py:252
  75.5 0.0 copy-start
  75.5 0.6 copy-done
  76.1 1.6 shard_map.52
  77.7 19.6 %all_to_all.37.far_in = f32[16,24,128]{2,1,0:T(8,128)} all-to-all(f32[16,24,128]{2,1,0:T(8,128)} %get-tuple-element.16), channel_id=1, replica_groups=mesh['y'=4,'zl'=8,'x'=4,'zh'=2,'c'=2] {'zl','zh'}, dimensions={0} | all-to-all | bytes 393216 | tf_op jit(solution)/shard_map/all_to_all | solution.py:252
  97.4 1.6 shard_map.53
  99.0 14.6 %all_to_all.38.near_in = f32[32,8,128]{2,1,0:T(8,128)} all-to-all(f32[32,8,128]{2,1,0:T(8,128)} %shard_map.53), channel_id=1, replica_groups=mesh['y'=4,'zl'=8,'x'=4,'zh'=2,'c'=2] {'y','x','c'}, dimensions={0} | all-to-all | bytes 262144 | tf_op jit(solution)/shard_map/all_to_all | solution.py:252
  113.6 5.4 %shard_map.54 = (f32[16,8,128]{2,1,0:T(8,128)}, f32[32,8,128]{2,1,0:T(8,128)}, f32[8,128]{1,0:T(8,128)}, f32[8,128]{1,0:T(8,128)}) custom-call(s32[4]{0:T(128)} %pad_add_fusion.idx, s32[64,512]{1,0:T(8,128)} %dosage_ref.3, f32[32,8,128]{2,1,0:T(8,128)} %all_to_all.38.near_in, f32[16,1024]{1,0:T(8,128)} %get-tuple-element.18.q_in, ...), custom_call_target="tpu_custom_call" | custom-call | tf_op jit(solution)/shard_map/pallas_call | solution.py:279
  119.0 0.0 copy-start.1
  119.0 19.2 %all_to_all.39.v_in = f32[16,8,128]{2,1,0:T(8,128)} all-to-all(f32[16,8,128]{2,1,0:T(8,128)} %get-tuple-element.20), channel_id=1, replica_groups=mesh['y'=4,'zl'=8,'x'=4,'zh'=2,'c'=2] {'x','zh','c'}, dimensions={0} | all-to-all | bytes 131072 | tf_op jit(solution)/shard_map/all_to_all | solution.py:252
  138.2 0.0 copy-done.1
  138.2 22.8 %all_to_all.40.s_in = f32[32,8,128]{2,1,0:T(8,128)} all-to-all(f32[32,8,128]{2,1,0:T(8,128)S(1)} %copy-done.1), channel_id=1, replica_groups=mesh['y'=4,'zl'=8,'x'=4,'zh'=2,'c'=2] {'y','zl'}, dimensions={0} | all-to-all | bytes 262144 | tf_op jit(solution)/shard_map/all_to_all | solution.py:252
  161.0 1.7 %shard_map.55 = (f32[12,64]{1,0:T(8,128)}, f32[12,16]{1,0:T(8,128)}) custom-call(f32[16,8,128]{2,1,0:T(8,128)} %all_to_all.39.v_in, f32[32,8,128]{2,1,0:T(8,128)} %all_to_all.40.s_in, f32[8,128]{1,0:T(8,128)} %get-tuple-element.22.own_q, f32[8,128]{1,0:T(8,128)} %get-tuple-element.23.own_f), custom_call_target="tpu_custom_call" | custom-call | tf_op jit(solution)/shard_map/pallas_call | solution.py:286
Async XLA Ops:
  2.1 33.8 %copy-start.2 = (f32[32,8,128]{2,1,0:T(8,128)S(1)}, f32[32,8,128]{2,1,0:T(8,128)}, u32[]{:S(2)}) copy-start(f32[32,8,128]{2,1,0:T(8,128)} %get-tuple-element.14) | copy-start | bytes 393220
  60.8 14.7 %all-to-all-start.2 = ((f32[32,8,128]{2,1,0:T(8,128)}), f32[32,8,128]{2,1,0:T(8,128)S(1)}, u32[]{:S(2)}, u32[]{:S(2)}) async-start(f32[32,8,128]{2,1,0:T(8,128)} %get-tuple-element.15), calls=%async_computation.2 | async-start | bytes 262144 | tf_op jit(solution)/shard_map/all_to_all | solution.py:252
  75.5 0.6 copy-start
  119.0 19.2 %copy-start.1 = (f32[32,8,128]{2,1,0:T(8,128)S(1)}, f32[32,8,128]{2,1,0:T(8,128)}, u32[]{:S(2)}) copy-start(f32[32,8,128]{2,1,0:T(8,128)} %get-tuple-element.21) | copy-start | bytes 393220

commit v2 on v1

--- a/solution.py
+++ b/solution.py
@@ -25,6 +25,22 @@
 
 def tile(i):
     return slice(i * LANES, (i + 1) * LANES)
+
+
+def var_of(idx):
+    return idx[0] & 15
+
+
+def smp_of(idx):
+    return idx[0] >> 4
+
+
+def zl_of(idx):
+    return (idx[0] >> 4) & 7
+
+
+def zh_of(idx):
+    return (idx[0] >> 1) & 1
 
 
 def lane():
@@ -93,19 +109,20 @@
     return fold(jnp.concatenate(sums_q, 1)), fold(sum_a), fold(sum_b)
 
 
-def first_kernel(shares_ref, freqs_ref, v_out, s_out, q_tmp, f_tmp):
+def first_kernel(idx, shares_ref, freqs_ref, v_out, s_out, q_tmp, f_tmp):
     raw = shares_ref[...]
     own = raw / jnp.sum(raw, axis=0, keepdims=True)
     q_tmp[...] = jnp.zeros_like(q_tmp)
     f_tmp[...] = jnp.zeros_like(f_tmp)
     q_tmp[:, 0:64] = own[0:8]
     q_tmp[0:4, 64:128] = own[8:12]
-    f_tmp[:, 0:16] = freqs_ref[0:8, :]
-    f_tmp[0:4, 16:32] = freqs_ref[8:12, :]
+    for j in range(3):
+        f_tmp[0:4, 16 * j : 16 * j + 16] = freqs_ref[4 * j : 4 * j + 4, :]
+    turned = pltpu.roll(f_tmp[...], 16 * zl_of(idx), 1)[0:4]
     for i in range(N_VAR):
         v_out[i] = q_tmp[...]
     for i in range(N_SMP):
-        s_out[i] = f_tmp[...]
+        s_out[i] = turned
 
 
 def shares_of(v_in):
@@ -118,18 +135,22 @@
     return jnp.concatenate([jnp.concatenate(low, 1), jnp.concatenate(high, 1)], 0)
 
 
+def block_of_lane():
+    return lax.broadcasted_iota(jnp.int32, (4, LANES), 1) // 16
+
+
 def freqs_of(s_in):
-    low, high = [], []
-    place = lane() // 16
+    tiles = []
+    block = block_of_lane()
     for t in range(4):
-        lo = hi = jnp.zeros((8, LANES), f32)
-        for i in range(8):
-            a = s_in[8 * t + i]
-            lo = jnp.where(place == i, roll(a, 16 * i), lo)
-            hi = jnp.where(place == i, roll(a, 16 * i - 16), hi)
-        low.append(lo)
-        high.append(hi)
-    return jnp.concatenate([jnp.concatenate(low, 1), jnp.concatenate(high, 1)], 0)
+        rows = []
+        for j in range(3):
+            got = s_in[8 * t]
+            for i in range(1, 8):
+                got = jnp.where(block == (i + j) % 8, s_in[8 * t + i], got)
+            rows.append(roll(got, -16 * j))
+        tiles.append(jnp.concatenate(rows + [jnp.zeros((4, LANES), f32)], 0))
+    return jnp.concatenate(tiles, 1)
 
 
 def one_kernel(dosage_ref, v_in, s_in, slots, q_out, f_out, sq_tmp, sa_tmp):
@@ -156,15 +177,15 @@
     for g in range(N_XC):
         a_tmp[3 * g : 3 * g + 3] = sum(near_in[y * N_XC + g] for y in range(N_Y))[3:6]
     for h in range(N_ZH):
-        sent = jnp.where(idx[3] == h, a_tmp[...], q_out[...])
+        sent = jnp.where(zh_of(idx) == h, a_tmp[...], q_out[...])
         for i in range(N_ZL):
             far_out[i * N_ZH + h] = sent
 
 
 def far_sums_kernel(idx, far_in, q_in, near_out, q_tmp, a_tmp):
-    zh = idx[3]
+    zh = zh_of(idx)
     a_tmp[...] = sum(far_in[i * N_ZH + zh] for i in range(N_ZL))
-    q_tmp[...] = q_in[...] + far_in[idx[2] * N_ZH + 1 - zh]
+    q_tmp[...] = q_in[...] + far_in[zl_of(idx) * N_ZH + 1 - zh]
     near_out[...] = jnp.zeros_like(near_out)
     for y in range(N_Y):
         for g in range(N_XC):
@@ -187,31 +208,39 @@
     f_tmp[0:12] = (alt_part + 0.5) / (alt_part + (1.0 - old) * sa_tmp[12:24] + 1.0)
 
     left = lane() < 64
-    t = pl.multiple_of(idx[0] // 2 * LANES, LANES)
+    t = pl.multiple_of((var_of(idx) >> 1) * LANES, LANES)
     a, b = q_tmp[0:8, pl.ds(t, LANES)], q_tmp[8:16, pl.ds(t, LANES)]
     own_q[...] = jnp.where(
-        idx[0] % 2 == 0, jnp.where(left, a, roll(b, 64)), jnp.where(left, roll(a, 64), b)
-    )
-    t = pl.multiple_of(idx[1] // 8 * LANES, LANES)
-    a, b = f_tmp[0:8, pl.ds(t, LANES)], f_tmp[8:16, pl.ds(t, LANES)]
-    back = LANES - 16 * (idx[1] % 8)
-    own_f[...] = jnp.where(lane() < 16, pltpu.roll(a, back, 1), pltpu.roll(b, back + 16, 1))
+        (var_of(idx) & 1) == 0, jnp.where(left, a, roll(b, 64)), jnp.where(left, roll(a, 64), b)
+    )
+    t = pl.multiple_of((smp_of(idx) >> 3) * LANES, LANES)
+    block = block_of_lane()
+    got = f_tmp[0:4, pl.ds(t, LANES)]
+    for j in range(1, 3):
+        got = jnp.where(
+            block == ((zl_of(idx) + j) & 7), roll(f_tmp[4 * j : 4 * j + 4, pl.ds(t, LANES)], 16 * j), got
+        )
+    own_f[...] = got
 
     sum_q, sum_a, sum_b = block_sums(dosage_ref, q_tmp[...], f_tmp[...])
     for t in range(8):
         a, b = sum_q[0:8, tile(t)], sum_q[8:16, tile(t)]
         v_out[2 * t] = jnp.where(left, a, roll(b, 64))
         v_out[2 * t + 1] = jnp.where(left, roll(a, 64), b)
-    place = lane() // 16
     for t in range(4):
+        turned = [
+            roll(sums[4 * j : 4 * j + 4, tile(t)], 16 * j + at)
+            for sums, at in ((sum_a, 0), (sum_b, 48))
+            for j in range(3)
+        ]
         for i in range(8):
-            got = roll(sum_a[0:8, tile(t)], -16 * i)
-            got = jnp.where(place == 1, roll(sum_a[8:16, tile(t)], 16 - 16 * i), got)
-            got = jnp.where(place == 2, roll(sum_b[0:8, tile(t)], 32 - 16 * i), got)
-            s_out[8 * t + i] = jnp.where(place == 3, roll(sum_b[8:16, tile(t)], 48 - 16 * i), got)
-
-
-def last_kernel(v_in, s_in, own_q, own_f, shares_out, freqs_out):
+            got = turned[0]
+            for j in range(1, 6):
+                got = jnp.where(block == (i + j) % 8, turned[j], got)
+            s_out[8 * t + i] = got
+
+
+def last_kernel(idx, v_in, s_in, own_q, own_f, shares_out, freqs_out):
     row = lax.broadcasted_iota(jnp.int32, (8, LANES), 0)
     held = (lane() < 64) | (row < 4)
     sum_q = sum(v_in[i] for i in range(N_VAR))
@@ -223,10 +252,11 @@
     shares_out[8:12] = new[0:4, 64:128]
     sums = sum(s_in[i] for i in range(N_SMP))
     alt_part = own_f[...] * sums
-    ref_part = (1.0 - own_f[...]) * roll(sums, -32)
+    ref_part = (1.0 - own_f[...]) * roll(sums, -48)
     new = (alt_part + 0.5) / (alt_part + ref_part + 1.0)
-    freqs_out[0:8] = new[:, 0:16]
-    freqs_out[8:12] = new[0:4, 16:32]
+    new = pltpu.roll(jnp.concatenate([new, new], 0), (LANES - 16 * zl_of(idx)) & (LANES - 1), 1)
+    for j in range(3):
+        freqs_out[4 * j : 4 * j + 4] = new[0:4, 16 * j : 16 * j + 16]
 
 
 def f32s(*shape):
@@ -237,15 +267,23 @@
     return pltpu.VMEM(shape, f32)
 
 
-def call(kernel, scalars, n_in, outs, scratch):
+def call(kernel, scalars, n_in, outs, scratch, kept=True):
     spec = pl.BlockSpec(memory_space=pltpu.VMEM)
-    return pl.pallas_call(
+    run = pl.pallas_call(
         kernel,
         in_specs=[pl.BlockSpec(memory_space=pltpu.SMEM)] * scalars + [spec] * n_in,
         out_specs=[spec] * len(outs),
-        out_shape=outs,
+        out_shape=[pltpu.VMEM(o.shape, o.dtype) for o in outs] if kept else outs,
         scratch_shapes=scratch,
     )
+
+    def placed(*args):
+        args = args[:scalars] + tuple(
+            pltpu.with_memory_space_constraint(a, pltpu.VMEM) for a in args[scalars:]
+        )
+        return run(*args)
+
+    return placed
 
 
 def exchange(x, axes):
@@ -253,14 +291,13 @@
 
 
 def body(dosage, shares_init, freqs_init):
-    idx = jnp.stack(
-        [lax.axis_index(VAR), lax.axis_index(SMP), lax.axis_index("zl"), lax.axis_index("zh")]
-    ).astype(jnp.int32)
+    idx = lax.axis_index(AXES).astype(jnp.int32).reshape(1)
     samples, variants = 16 * dosage.shape[0], dosage.shape[1]
     tiles = lambda n: f32s(n, 8, LANES)
+    fours = lambda n: f32s(n, 4, LANES)
     v_slots, s_slots = call(
-        first_kernel, 0, 2, [tiles(N_VAR), tiles(N_SMP)], [vmem(8, LANES), vmem(8, LANES)]
-    )(shares_init, freqs_init)
+        first_kernel, 1, 2, [tiles(N_VAR), fours(N_SMP)], [vmem(8, LANES), vmem(8, LANES)]
+    )(idx, shares_init, freqs_init)
     v_got = exchange(v_slots, VAR)
     s_got = exchange(s_slots, SMP)
     slots, shares, freqs = call(
@@ -277,14 +314,14 @@
     )(idx, far_got, own_sum)
     near_got = exchange(near_slots, NEAR)
     v_slots, s_slots, own_q, own_f = call(
-        two_kernel, 1, 4, [tiles(N_VAR), tiles(N_SMP), f32s(8, LANES), f32s(8, LANES)],
+        two_kernel, 1, 4, [tiles(N_VAR), fours(N_SMP), f32s(8, LANES), f32s(4, LANES)],
         [vmem(PAD, samples), vmem(24, variants), vmem(PAD, samples), vmem(PAD, variants)],
     )(idx, dosage, near_got, shares, freqs)
     v_got = exchange(v_slots, VAR)
     s_got = exchange(s_slots, SMP)
     return tuple(
-        call(last_kernel, 0, 4, [f32s(*shares_init.shape), f32s(*freqs_init.shape)], [])(
-            v_got, s_got, own_q, own_f
+        call(last_kernel, 1, 4, [f32s(*shares_init.shape), f32s(*freqs_init.shape)], [], False)(
+            idx, v_got, s_got, own_q, own_f
         )
     )
 

time: 164 us -> 148 us (0.902)
  Pallas kernels: 17.2 us -> 8.47 us
  blocking collectives: 130 us -> 138 us
  waiting for transfers between devices: 7.05 us -> 0 us
  starting transfers between devices: 6.98 us -> 0 us
    pallas_call x6, Pallas kernels: 17.2 us -> 8.47 us  [placed(): return run(*args)]
    all_to_all x6 -> x7, blocking collectives: 130 us -> 138 us  [exchange(): return lax.all_to_all(x, axes, 0, 0, tiled=True)]
    all_to_all x1 -> x0, waiting for transfers between devices: 7.05 us -> none  [exchange(): return lax.all_to_all(x, axes, 0, 0, tiled=True)]
    all_to_all x1 -> x0, starting transfers between devices: 6.98 us -> none  [exchange(): return lax.all_to_all(x, axes, 0, 0, tiled=True)]
  transfers between devices with their start and end apart: 1 -> 0, of which waited for: 1 -> 0; matrix products, arithmetic and copies ran while one was open for 0% -> 0% of each run, Pallas kernels for 0% -> 0%
where the time goes in v2:
time: 148 us
  blocking collectives  138 us (93%)
  Pallas kernels  8.47 us (6%)
    all_to_all x7, blocking collectives, exchange(): return lax.all_to_all(x, axes, 0, 0, tiled=True)  138 us
    pallas_call x6, Pallas kernels, placed(): return run(*args)  8.47 us

profile of v2, /device:TPU:1, one launch (start us, length us, event | category | flops | bytes accessed | tf_op | source)
XLA Modules:
  0.0 147.9 jit_solution(15114385733743094855)
XLA Ops:
  0.6 0.0 copy-start.2
  0.6 0.0 copy-start.1
  0.7 0.7 copy-done.2
  1.3 0.0 copy-done.1
  1.4 0.1 shard_map.50
  1.5 0.0 copy-start
  1.5 33.5 %all_to_all.35.v_in = f32[16,8,128]{2,1,0:T(8,128)S(1)} all-to-all(f32[16,8,128]{2,1,0:T(8,128)S(1)} %get-tuple-element.13), channel_id=1, replica_groups=mesh['y'=4,'zl'=8,'x'=4,'zh'=2,'c'=2] {'x','zh','c'}, dimensions={0} | all-to-all | bytes 131072 | tf_op jit(solution)/shard_map/all_to_all | solution.py:290
  35.0 19.0 %all_to_all.36.s_in = f32[32,4,128]{2,1,0:T(4,128)S(1)} all-to-all(f32[32,4,128]{2,1,0:T(4,128)S(1)} %get-tuple-element.14), channel_id=1, replica_groups=mesh['y'=4,'zl'=8,'x'=4,'zh'=2,'c'=2] {'y','zl'}, dimensions={0} | all-to-all | bytes 131072 | tf_op jit(solution)/shard_map/all_to_all | solution.py:290
  54.1 0.0 copy-done
  54.1 3.7 %shard_map.51 = (f32[32,8,128]{2,1,0:T(8,128)S(1)}, f32[16,1024]{1,0:T(8,128)S(1)}, f32[16,512]{1,0:T(8,128)S(1)}) custom-call(s32[64,512]{1,0:T(8,128)S(1)} %copy-done, f32[16,8,128]{2,1,0:T(8,128)S(1)} %all_to_all.35.v_in, f32[32,4,128]{2,1,0:T(4,128)S(1)} %all_to_all.36.s_in), custom_call_target="tpu_custom_call" | custom-call | tf_op jit(solution)/shard_map/pallas_call | solution.py:284
  57.8 12.6 %all_to_all.37.near_in = f32[32,8,128]{2,1,0:T(8,128)S(1)} all-to-all(f32[32,8,128]{2,1,0:T(8,128)S(1)} %get-tuple-element.15), channel_id=1, replica_groups=mesh['y'=4,'zl'=8,'x'=4,'zh'=2,'c'=2] {'y','x','c'}, dimensions={0} | all-to-all | bytes 262144 | tf_op jit(solution)/shard_map/all_to_all | solution.py:290
  70.4 18.2 %all_to_all.38.far_in = f32[16,24,128]{2,1,0:T(8,128)S(1)} all-to-all(f32[16,24,128]{2,1,0:T(8,128)S(1)} %get-tuple-element.16), channel_id=1, replica_groups=mesh['y'=4,'zl'=8,'x'=4,'zh'=2,'c'=2] {'zl','zh'}, dimensions={0} | all-to-all | bytes 393216 | tf_op jit(solution)/shard_map/all_to_all | solution.py:290
  88.6 13.8 %all_to_all.39.near_in = f32[32,8,128]{2,1,0:T(8,128)S(1)} all-to-all(f32[32,8,128]{2,1,0:T(8,128)S(1)} %shard_map.53), channel_id=1, replica_groups=mesh['y'=4,'zl'=8,'x'=4,'zh'=2,'c'=2] {'y','x','c'}, dimensions={0} | all-to-all | bytes 262144 | tf_op jit(solution)/shard_map/all_to_all | solution.py:290
  102.4 3.7 %shard_map.54 = (f32[16,8,128]{2,1,0:T(8,128)S(1)}, f32[32,4,128]{2,1,0:T(4,128)S(1)}, f32[8,128]{1,0:T(8,128)S(1)}, f32[4,128]{1,0:T(4,128)S(1)}) custom-call(s32[1]{0:T(128)} %bitcast.idx, s32[64,512]{1,0:T(8,128)S(1)} %copy-done, f32[32,8,128]{2,1,0:T(8,128)S(1)} %all_to_all.39.near_in, f32[16,1024]{1,0:T(8,128)S(1)} %get-tuple-element.18.q_in, ...), custom_call_target="tpu_custom_call" | custom-call | tf_op jit(solution)/shard_map/pallas_call | solution.py:284
  106.1 18.5 %all_to_all.40.v_in = f32[16,8,128]{2,1,0:T(8,128)S(1)} all-to-all(f32[16,8,128]{2,1,0:T(8,128)S(1)} %get-tuple-element.20), channel_id=1, replica_groups=mesh['y'=4,'zl'=8,'x'=4,'zh'=2,'c'=2] {'x','zh','c'}, dimensions={0} | all-to-all | bytes 131072 | tf_op jit(solution)/shard_map/all_to_all | solution.py:290
  124.6 22.4 %all_to_all.41.s_in = f32[32,4,128]{2,1,0:T(4,128)S(1)} all-to-all(f32[32,4,128]{2,1,0:T(4,128)S(1)} %get-tuple-element.21), channel_id=1, replica_groups=mesh['y'=4,'zl'=8,'x'=4,'zh'=2,'c'=2] {'y','zl'}, dimensions={0} | all-to-all | bytes 131072 | tf_op jit(solution)/shard_map/all_to_all | solution.py:290
  147.0 0.8 shard_map.55
  (2 shorter events, 0.1 us)
Async XLA Ops:
  0.6 0.7 copy-start.2
  0.6 0.7 copy-start.1
  1.5 52.6 %copy-start = (s32[64,512]{1,0:T(8,128)S(1)}, s32[64,512]{1,0:T(8,128)}, u32[]{:S(2)}) copy-start(s32[64,512]{1,0:T(8,128)} %dosage_ref.3) | copy-start | bytes 393220

commit v3 on v2

--- a/solution.py
+++ b/solution.py
@@ -16,7 +16,7 @@
 VAR = ("x", "zh", "c")
 NEAR = ("y", "x", "c")
 FAR = ("zl", "zh")
-N_SMP, N_VAR, N_NEAR, N_FAR = 32, 16, 32, 16
+N_NEAR, N_FAR = 32, 16
 N_Y, N_XC, N_ZL, N_ZH = 4, 8, 8, 2
 
 f32 = jnp.float32
@@ -109,53 +109,85 @@
     return fold(jnp.concatenate(sums_q, 1)), fold(sum_a), fold(sum_b)
 
 
-def first_kernel(idx, shares_ref, freqs_ref, v_out, s_out, q_tmp, f_tmp):
+def near_of(idx):
+    return ((idx[0] >> 1) & 6) | (idx[0] & 1)
+
+
+def y_of(idx):
+    return idx[0] >> 7
+
+
+def halves(a, b):
+    left = lax.broadcasted_iota(jnp.int32, a.shape, 1) < 64
+    return jnp.where(left, a, roll(b, 64)), jnp.where(left, roll(a, 64), b)
+
+
+def block_of_lane():
+    return lax.broadcasted_iota(jnp.int32, (4, LANES), 1) // 16
+
+
+def first_kernel(idx, shares_ref, freqs_ref, far_out, q_out, f_tmp):
     raw = shares_ref[...]
     own = raw / jnp.sum(raw, axis=0, keepdims=True)
-    q_tmp[...] = jnp.zeros_like(q_tmp)
+    q_out[...] = jnp.zeros_like(q_out)
     f_tmp[...] = jnp.zeros_like(f_tmp)
-    q_tmp[:, 0:64] = own[0:8]
-    q_tmp[0:4, 64:128] = own[8:12]
+    q_out[:, 0:64] = own[0:8]
+    q_out[0:4, 64:128] = own[8:12]
     for j in range(3):
         f_tmp[0:4, 16 * j : 16 * j + 16] = freqs_ref[4 * j : 4 * j + 4, :]
-    turned = pltpu.roll(f_tmp[...], 16 * zl_of(idx), 1)[0:4]
-    for i in range(N_VAR):
-        v_out[i] = q_tmp[...]
-    for i in range(N_SMP):
-        s_out[i] = turned
-
-
-def shares_of(v_in):
-    low, high = [], []
-    left = lane() < 64
-    for t in range(8):
-        a, b = v_in[2 * t], v_in[2 * t + 1]
-        low.append(jnp.where(left, a, roll(b, 64)))
-        high.append(jnp.where(left, roll(a, 64), b))
-    return jnp.concatenate([jnp.concatenate(low, 1), jnp.concatenate(high, 1)], 0)
-
-
-def block_of_lane():
-    return lax.broadcasted_iota(jnp.int32, (4, LANES), 1) // 16
-
-
-def freqs_of(s_in):
-    tiles = []
+    turned = pltpu.roll(f_tmp[...], 16 * zl_of(idx), 1)
+    for h in range(N_ZH):
+        sent = jnp.where(zh_of(idx) == h, turned, q_out[...])
+        for i in range(N_ZL):
+            far_out[i * N_ZH + h] = sent
+
+
+def first_near_kernel(idx, far_in, q_in, near_out, f_out):
+    zh = zh_of(idx)
     block = block_of_lane()
-    for t in range(4):
-        rows = []
+    freqs = [far_in[i * N_ZH + zh, 0:4] for i in range(N_ZL)]
+    for j in range(3):
+        got = freqs[0]
+        for i in range(1, N_ZL):
+            got = jnp.where(block == (i + j) % 8, freqs[i], got)
+        f_out[j] = roll(got, -16 * j)
+    own, other = q_in[...], far_in[zl_of(idx) * N_ZH + 1 - zh]
+    low, high = halves(jnp.where(zh == 0, own, other), jnp.where(zh == 0, other, own))
+    for s in range(N_NEAR):
+        near_out[3 * s : 3 * s + 3] = f_out[...]
+    for g in range(N_XC):
+        s = 3 * (y_of(idx) * N_XC + g)
+        near_out[s] = low[0:4]
+        near_out[s + 1] = low[4:8]
+        near_out[s + 2] = high[0:4]
+
+
+def shares_of(idx, near_in):
+    rows = [[], [], []]
+    for x in range(4):
         for j in range(3):
-            got = s_in[8 * t]
-            for i in range(1, 8):
-                got = jnp.where(block == (i + j) % 8, s_in[8 * t + i], got)
-            rows.append(roll(got, -16 * j))
-        tiles.append(jnp.concatenate(rows + [jnp.zeros((4, LANES), f32)], 0))
-    return jnp.concatenate(tiles, 1)
-
-
-def one_kernel(dosage_ref, v_in, s_in, slots, q_out, f_out, sq_tmp, sa_tmp):
-    shares = shares_of(v_in)
-    freqs = freqs_of(s_in)
+            s = 3 * (y_of(idx) * N_XC + 2 * x) + j
+            rows[j].extend(halves(near_in[s], near_in[s + 3]))
+    return padded(rows)
+
+
+def freqs_of(idx, near_in, f_in):
+    rows = [[], [], []]
+    for y in range(N_Y):
+        for j in range(3):
+            got = near_in[3 * (y * N_XC + near_of(idx)) + j]
+            rows[j].append(jnp.where(y_of(idx) == y, f_in[j], got))
+    return padded(rows)
+
+
+def padded(rows):
+    rows = [jnp.concatenate(row, 1) for row in rows]
+    return jnp.concatenate([*rows, jnp.zeros_like(rows[0])], 0)
+
+
+def one_kernel(idx, dosage_ref, near_in, own_f_in, slots, q_out, f_out, sq_tmp, sa_tmp):
+    shares = shares_of(idx, near_in)
+    freqs = freqs_of(idx, near_in, own_f_in)
     q_out[...] = shares
     f_out[...] = freqs
     sum_q, sum_a, sum_b = block_sums(dosage_ref, shares, freqs)
@@ -193,7 +225,7 @@
             near_out[y * N_XC + g, 3:6] = a_tmp[3 * g : 3 * g + 3]
 
 
-def two_kernel(idx, dosage_ref, near_in, q_in, f_in, v_out, s_out, own_q, own_f, sq_tmp, sa_tmp, q_tmp, f_tmp):
+def two_kernel(idx, dosage_ref, near_in, q_in, f_in, near_out, sq_out, own_q, own_f, sq_tmp, sa_tmp, q_tmp, f_tmp):
     for s in range(N_NEAR):
         t, q = divmod(s, 4)
         sq_tmp[3 * q : 3 * q + 3, tile(t)] = near_in[s, 0:3]
@@ -207,12 +239,9 @@
     alt_part = old * sa_tmp[0:12]
     f_tmp[0:12] = (alt_part + 0.5) / (alt_part + (1.0 - old) * sa_tmp[12:24] + 1.0)
 
-    left = lane() < 64
     t = pl.multiple_of((var_of(idx) >> 1) * LANES, LANES)
-    a, b = q_tmp[0:8, pl.ds(t, LANES)], q_tmp[8:16, pl.ds(t, LANES)]
-    own_q[...] = jnp.where(
-        (var_of(idx) & 1) == 0, jnp.where(left, a, roll(b, 64)), jnp.where(left, roll(a, 64), b)
-    )
+    even, odd = halves(q_tmp[0:8, pl.ds(t, LANES)], q_tmp[8:16, pl.ds(t, LANES)])
+    own_q[...] = jnp.where((var_of(idx) & 1) == 0, even, odd)
     t = pl.multiple_of((smp_of(idx) >> 3) * LANES, LANES)
     block = block_of_lane()
     got = f_tmp[0:4, pl.ds(t, LANES)]
@@ -223,34 +252,50 @@
     own_f[...] = got
 
     sum_q, sum_a, sum_b = block_sums(dosage_ref, q_tmp[...], f_tmp[...])
-    for t in range(8):
-        a, b = sum_q[0:8, tile(t)], sum_q[8:16, tile(t)]
-        v_out[2 * t] = jnp.where(left, a, roll(b, 64))
-        v_out[2 * t + 1] = jnp.where(left, roll(a, 64), b)
-    for t in range(4):
-        turned = [
-            roll(sums[4 * j : 4 * j + 4, tile(t)], 16 * j + at)
-            for sums, at in ((sum_a, 0), (sum_b, 48))
-            for j in range(3)
-        ]
-        for i in range(8):
-            got = turned[0]
-            for j in range(1, 6):
-                got = jnp.where(block == (i + j) % 8, turned[j], got)
-            s_out[8 * t + i] = got
-
-
-def last_kernel(idx, v_in, s_in, own_q, own_f, shares_out, freqs_out):
+    for x in range(4):
+        pair = halves(sum_q[:, tile(2 * x)], sum_q[:, tile(2 * x + 1)])
+        for c in range(2):
+            for y in range(N_Y):
+                near_out[y * N_XC + 2 * x + c, 0:16] = pair[c]
+    sq_out[...] = near_out[near_of(idx), 0:16]
+    sa_tmp[0:12] = sum_a[0:12]
+    sa_tmp[12:24] = sum_b[0:12]
+    for y in range(N_Y):
+        near_out[y * N_XC + near_of(idx)] = sa_tmp[:, tile(y)]
+
+
+def last_far_kernel(idx, near_in, sq_in, far_out, q_out):
+    zh, near = zh_of(idx), near_of(idx)
+    sum_q = sq_in[...]
+    for g in range(N_XC):
+        got = near_in[y_of(idx) * N_XC + g, 0:16]
+        sum_q = sum_q + jnp.where(near == g, 0.0, got)
+    sums = sum(near_in[y * N_XC + near] for y in range(N_Y))
+    parts = halves(sum_q[0:8], sum_q[8:16])
+    q_out[...] = jnp.where(zh == 0, parts[0], parts[1])
+    block = block_of_lane()
+    turned = [roll(sums[4 * j : 4 * j + 4], 16 * j) for j in range(6)]
+    for i in range(N_ZL):
+        got = turned[0]
+        for j in range(1, 6):
+            got = jnp.where(block == (i + j) % 8, turned[j], got)
+        got = jnp.concatenate([got, got], 0)
+        for h in range(N_ZH):
+            far_out[i * N_ZH + h] = jnp.where(zh == h, got, parts[h])
+
+
+def last_kernel(idx, far_in, sq_in, own_q, own_f, shares_out, freqs_out):
+    zh = zh_of(idx)
     row = lax.broadcasted_iota(jnp.int32, (8, LANES), 0)
     held = (lane() < 64) | (row < 4)
-    sum_q = sum(v_in[i] for i in range(N_VAR))
+    sum_q = sq_in[...] + far_in[zl_of(idx) * N_ZH + 1 - zh]
     numer = jnp.where(held, own_q[...] * sum_q, 0.0)
     total = jnp.sum(numer, axis=0, keepdims=True)
     total = total + pltpu.roll(total, 64, 1)
     new = (numer + 0.5) / (total + 0.5 * K)
     shares_out[0:8] = new[:, 0:64]
     shares_out[8:12] = new[0:4, 64:128]
-    sums = sum(s_in[i] for i in range(N_SMP))
+    sums = sum(far_in[i * N_ZH + zh, 0:4] for i in range(N_ZL))
     alt_part = own_f[...] * sums
     ref_part = (1.0 - own_f[...]) * roll(sums, -48)
     new = (alt_part + 0.5) / (alt_part + ref_part + 1.0)
@@ -294,16 +339,18 @@
     idx = lax.axis_index(AXES).astype(jnp.int32).reshape(1)
     samples, variants = 16 * dosage.shape[0], dosage.shape[1]
     tiles = lambda n: f32s(n, 8, LANES)
-    fours = lambda n: f32s(n, 4, LANES)
-    v_slots, s_slots = call(
-        first_kernel, 1, 2, [tiles(N_VAR), fours(N_SMP)], [vmem(8, LANES), vmem(8, LANES)]
-    )(idx, shares_init, freqs_init)
-    v_got = exchange(v_slots, VAR)
-    s_got = exchange(s_slots, SMP)
+    far_slots, own_q = call(first_kernel, 1, 2, [tiles(N_FAR), f32s(8, LANES)], [vmem(8, LANES)])(
+        idx, shares_init, freqs_init
+    )
+    far_got = exchange(far_slots, FAR)
+    near_slots, own_f = call(
+        first_near_kernel, 1, 2, [f32s(3 * N_NEAR, 4, LANES), f32s(3, 4, LANES)], []
+    )(idx, far_got, own_q)
+    near_got = exchange(near_slots, NEAR)
     slots, shares, freqs = call(
-        one_kernel, 0, 3, [tiles(N_NEAR), f32s(PAD, samples), f32s(PAD, variants)],
+        one_kernel, 1, 3, [tiles(N_NEAR), f32s(PAD, samples), f32s(PAD, variants)],
         [vmem(PAD, samples), vmem(24, variants)],
-    )(dosage, v_got, s_got)
+    )(idx, dosage, near_got, own_f)
     near_got = exchange(slots, NEAR)
     far_slots, own_sum = call(
         near_sums_kernel, 1, 1, [f32s(N_FAR, 24, LANES), f32s(24, LANES)], [vmem(24, LANES)]
@@ -313,15 +360,19 @@
         far_sums_kernel, 1, 2, [tiles(N_NEAR)], [vmem(24, LANES), vmem(24, LANES)]
     )(idx, far_got, own_sum)
     near_got = exchange(near_slots, NEAR)
-    v_slots, s_slots, own_q, own_f = call(
-        two_kernel, 1, 4, [tiles(N_VAR), fours(N_SMP), f32s(8, LANES), f32s(4, LANES)],
+    near_slots, own_sum, own_q, own_f = call(
+        two_kernel, 1, 4,
+        [f32s(N_NEAR, 24, LANES), f32s(PAD, LANES), f32s(8, LANES), f32s(4, LANES)],
         [vmem(PAD, samples), vmem(24, variants), vmem(PAD, samples), vmem(PAD, variants)],
     )(idx, dosage, near_got, shares, freqs)
-    v_got = exchange(v_slots, VAR)
-    s_got = exchange(s_slots, SMP)
+    near_got = exchange(near_slots, NEAR)
+    far_slots, own_sum = call(last_far_kernel, 1, 2, [tiles(N_FAR), f32s(8, LANES)], [])(
+        idx, near_got, own_sum
+    )
+    far_got = exchange(far_slots, FAR)
     return tuple(
         call(last_kernel, 1, 4, [f32s(*shares_init.shape), f32s(*freqs_init.shape)], [], False)(
-            idx, v_got, s_got, own_q, own_f
+            idx, far_got, own_sum, own_q, own_f
         )
     )
 

time: 148 us -> 128 us (0.86)
  blocking collectives: 138 us -> 117 us
    all_to_all x7, blocking collectives: 138 us -> 117 us  [exchange(): return lax.all_to_all(x, axes, 0, 0, tiled=True)]
    pallas_call x6 -> x8, Pallas kernels: 8.47 us -> 8.63 us  [placed(): return run(*args)]
where the time goes in v3:
time: 128 us; the launch traced here: 127 us
  blocking collectives  117 us (91%)
  Pallas kernels  8.63 us (7%)
    all_to_all x7, blocking collectives, exchange(): return lax.all_to_all(x, axes, 0, 0, tiled=True)  117 us
    pallas_call x8, Pallas kernels, placed(): return run(*args)  8.63 us

profile of v3, /device:TPU:1, one launch (start us, length us, event | category | flops | bytes accessed | tf_op | source)
XLA Modules:
  0.0 127.3 jit_solution(2411198259487598899)
XLA Ops:
  0.6 0.0 copy-start.2
  0.6 0.0 copy-start.1
  0.7 0.7 copy-done.2
  1.3 0.0 copy-done.1
  1.4 0.1 shard_map.50
  1.5 27.6 %all_to_all.35.far_in = f32[16,8,128]{2,1,0:T(8,128)S(1)} all-to-all(f32[16,8,128]{2,1,0:T(8,128)S(1)} %get-tuple-element.17), channel_id=1, replica_groups=mesh['y'=4,'zl'=8,'x'=4,'zh'=2,'c'=2] {'zl','zh'}, dimensions={0} | all-to-all | bytes 131072 | tf_op jit(solution)/shard_map/all_to_all | solution.py:335
  29.1 0.1 shard_map.51
  29.2 0.0 copy-start
  29.3 17.4 %all_to_all.36.near_in = f32[96,4,128]{2,1,0:T(4,128)S(1)} all-to-all(f32[96,4,128]{2,1,0:T(4,128)S(1)} %get-tuple-element.19), channel_id=1, replica_groups=mesh['y'=4,'zl'=8,'x'=4,'zh'=2,'c'=2] {'y','x','c'}, dimensions={0} | all-to-all | bytes 393216 | tf_op jit(solution)/shard_map/all_to_all | solution.py:335
  46.6 0.0 copy-done
  46.6 3.7 %shard_map.52 = (f32[32,8,128]{2,1,0:T(8,128)S(1)}, f32[16,1024]{1,0:T(8,128)S(1)}, f32[16,512]{1,0:T(8,128)S(1)}) custom-call(s32[1]{0:T(128)} %bitcast.idx, s32[64,512]{1,0:T(8,128)S(1)} %copy-done, f32[96,4,128]{2,1,0:T(4,128)S(1)} %all_to_all.36.near_in, f32[3,4,128]{2,1,0:T(4,128)S(1)} %get-tuple-element.20.own_f_in), custom_call_target="tpu_custom_call" | custom-call | tf_op jit(solution)/shard_map/pallas_call | solution.py:329
  50.3 11.2 %all_to_all.37.near_in = f32[32,8,128]{2,1,0:T(8,128)S(1)} all-to-all(f32[32,8,128]{2,1,0:T(8,128)S(1)} %get-tuple-element.21), channel_id=1, replica_groups=mesh['y'=4,'zl'=8,'x'=4,'zh'=2,'c'=2] {'y','x','c'}, dimensions={0} | all-to-all | bytes 262144 | tf_op jit(solution)/shard_map/all_to_all | solution.py:335
  61.6 18.0 %all_to_all.38.far_in = f32[16,24,128]{2,1,0:T(8,128)S(1)} all-to-all(f32[16,24,128]{2,1,0:T(8,128)S(1)} %get-tuple-element.22), channel_id=1, replica_groups=mesh['y'=4,'zl'=8,'x'=4,'zh'=2,'c'=2] {'zl','zh'}, dimensions={0} | all-to-all | bytes 393216 | tf_op jit(solution)/shard_map/all_to_all | solution.py:335
  79.6 13.5 %all_to_all.39.near_in = f32[32,8,128]{2,1,0:T(8,128)S(1)} all-to-all(f32[32,8,128]{2,1,0:T(8,128)S(1)} %shard_map.54), channel_id=1, replica_groups=mesh['y'=4,'zl'=8,'x'=4,'zh'=2,'c'=2] {'y','x','c'}, dimensions={0} | all-to-all | bytes 262144 | tf_op jit(solution)/shard_map/all_to_all | solution.py:335
  93.1 3.7 %shard_map.55 = (f32[32,24,128]{2,1,0:T(8,128)S(1)}, f32[16,128]{1,0:T(8,128)S(1)}, f32[8,128]{1,0:T(8,128)S(1)}, f32[4,128]{1,0:T(4,128)S(1)}) custom-call(s32[1]{0:T(128)} %bitcast.idx, s32[64,512]{1,0:T(8,128)S(1)} %copy-done, f32[32,8,128]{2,1,0:T(8,128)S(1)} %all_to_all.39.near_in, f32[16,1024]{1,0:T(8,128)S(1)} %get-tuple-element.24.q_in, ...), custom_call_target="tpu_custom_call" | custom-call | tf_op jit(solution)/shard_map/pallas_call | solution.py:329
  96.8 13.8 %all_to_all.40.near_in = f32[32,24,128]{2,1,0:T(8,128)S(1)} all-to-all(f32[32,24,128]{2,1,0:T(8,128)S(1)} %get-tuple-element.26), channel_id=1, replica_groups=mesh['y'=4,'zl'=8,'x'=4,'zh'=2,'c'=2] {'y','x','c'}, dimensions={0} | all-to-all | bytes 786432 | tf_op jit(solution)/shard_map/all_to_all | solution.py:335
  110.6 0.1 shard_map.56
  110.7 15.8 %all_to_all.41.far_in = f32[16,8,128]{2,1,0:T(8,128)S(1)} all-to-all(f32[16,8,128]{2,1,0:T(8,128)S(1)} %get-tuple-element.28), channel_id=1, replica_groups=mesh['y'=4,'zl'=8,'x'=4,'zh'=2,'c'=2] {'zl','zh'}, dimensions={0} | all-to-all | bytes 131072 | tf_op jit(solution)/shard_map/all_to_all | solution.py:335
  126.5 0.8 shard_map.57
  (2 shorter events, 0.1 us)
Async XLA Ops:
  0.6 0.7 copy-start.2
  0.6 0.7 copy-start.1
  29.2 17.4 %copy-start = (s32[64,512]{1,0:T(8,128)S(1)}, s32[64,512]{1,0:T(8,128)}, u32[]{:S(2)}) copy-start(s32[64,512]{1,0:T(8,128)} %dosage_ref.3) | copy-start | bytes 393220

commit v4 on v3

--- a/solution.py
+++ b/solution.py
@@ -81,8 +81,8 @@
     f_two = jnp.concatenate([fh, fm], 0)
     g_two = jnp.concatenate(two_parts(1.0 - freqs), 0)
     shift = 2 * lax.broadcasted_iota(jnp.int32, (16, freqs.shape[1]), 0)
-    sums_q, sum_a, sum_b = [], None, None
-    for at in range(0, shares.shape[1], ROWS):
+
+    def ratios(at):
         probs = dot(q_side[:, at : at + ROWS], f_side, 0, 0)
         codes = jnp.concatenate(
             [
@@ -93,19 +93,25 @@
             ],
             0,
         )
-        rest = 1.0 - probs
-        inverse = jnp.where(codes < 3, 1.0 / (probs * rest), 0.0)
+        live = codes < 3
         allele = codes.astype(f32)
-        ah, al = two_parts(allele * (rest * inverse))
-        bh, bl = two_parts((2.0 - allele) * (probs * inverse))
+        ratio_alt = jnp.where(live, allele, 0.0) * (1.0 / probs)
+        ratio_ref = jnp.where(live, 2.0 - allele, 0.0) * (1.0 / (1.0 - probs))
+        return two_parts(ratio_alt) + two_parts(ratio_ref)
+
+    sums_q, sum_a, sum_b = [], 0.0, 0.0
+    starts = range(0, shares.shape[1], ROWS)
+    ready = ratios(0)
+    for at in starts:
+        ah, al, bh, bl = ready
+        if at + ROWS in starts:
+            ready = ratios(at + ROWS)
         sums_q.append(
             dot(f_two, ah, 1, 1) + dot(f_two, al, 1, 1) + dot(g_two, bh, 1, 1) + dot(g_two, bl, 1, 1)
         )
         q_part = q_two[:, at : at + ROWS]
-        part_a = dot(q_part, ah, 1, 0) + dot(q_part, al, 1, 0)
-        part_b = dot(q_part, bh, 1, 0) + dot(q_part, bl, 1, 0)
-        sum_a = part_a if sum_a is None else sum_a + part_a
-        sum_b = part_b if sum_b is None else sum_b + part_b
+        sum_a = sum_a + (dot(q_part, ah, 1, 0) + dot(q_part, al, 1, 0))
+        sum_b = sum_b + (dot(q_part, bh, 1, 0) + dot(q_part, bl, 1, 0))
     return fold(jnp.concatenate(sums_q, 1)), fold(sum_a), fold(sum_b)
 
 

time: 128 us -> 125 us (0.977)
  Pallas kernels: 8.63 us -> 6.22 us
    pallas_call x8, Pallas kernels: 8.63 us -> 6.22 us  [placed(): return run(*args)]
where the time goes in v4:
time: 125 us
  blocking collectives  117 us (94%)
  Pallas kernels  6.22 us (5%)
    all_to_all x7, blocking collectives, exchange(): return lax.all_to_all(x, axes, 0, 0, tiled=True)  117 us
    pallas_call x8, Pallas kernels, placed(): return run(*args)  6.22 us

profile of v4, /device:TPU:1, one launch (start us, length us, event | category | flops | bytes accessed | tf_op | source)
XLA Modules:
  0.0 124.9 jit_solution(14944322637524138600)
XLA Ops:
  0.6 0.0 copy-start.2
  0.6 0.0 copy-start.1
  0.7 0.7 copy-done.2
  1.3 0.0 copy-done.1
  1.4 0.1 shard_map.50
  1.5 27.6 %all_to_all.35.far_in = f32[16,8,128]{2,1,0:T(8,128)S(1)} all-to-all(f32[16,8,128]{2,1,0:T(8,128)S(1)} %get-tuple-element.17), channel_id=1, replica_groups=mesh['y'=4,'zl'=8,'x'=4,'zh'=2,'c'=2] {'zl','zh'}, dimensions={0} | all-to-all | bytes 131072 | tf_op jit(solution)/shard_map/all_to_all | solution.py:341
  29.1 0.1 shard_map.51
  29.2 0.0 copy-start
  29.3 17.4 %all_to_all.36.near_in = f32[96,4,128]{2,1,0:T(4,128)S(1)} all-to-all(f32[96,4,128]{2,1,0:T(4,128)S(1)} %get-tuple-element.19), channel_id=1, replica_groups=mesh['y'=4,'zl'=8,'x'=4,'zh'=2,'c'=2] {'y','x','c'}, dimensions={0} | all-to-all | bytes 393216 | tf_op jit(solution)/shard_map/all_to_all | solution.py:341
  46.6 0.0 copy-done
  46.6 2.5 %shard_map.52 = (f32[32,8,128]{2,1,0:T(8,128)S(1)}, f32[16,1024]{1,0:T(8,128)S(1)}, f32[16,512]{1,0:T(8,128)S(1)}) custom-call(s32[1]{0:T(128)} %bitcast.idx, s32[64,512]{1,0:T(8,128)S(1)} %copy-done, f32[96,4,128]{2,1,0:T(4,128)S(1)} %all_to_all.36.near_in, f32[3,4,128]{2,1,0:T(4,128)S(1)} %get-tuple-element.20.own_f_in), custom_call_target="tpu_custom_call" | custom-call | tf_op jit(solution)/shard_map/pallas_call | solution.py:335
  49.1 11.2 %all_to_all.37.near_in = f32[32,8,128]{2,1,0:T(8,128)S(1)} all-to-all(f32[32,8,128]{2,1,0:T(8,128)S(1)} %get-tuple-element.21), channel_id=1, replica_groups=mesh['y'=4,'zl'=8,'x'=4,'zh'=2,'c'=2] {'y','x','c'}, dimensions={0} | all-to-all | bytes 262144 | tf_op jit(solution)/shard_map/all_to_all | solution.py:341
  60.3 18.0 %all_to_all.38.far_in = f32[16,24,128]{2,1,0:T(8,128)S(1)} all-to-all(f32[16,24,128]{2,1,0:T(8,128)S(1)} %get-tuple-element.22), channel_id=1, replica_groups=mesh['y'=4,'zl'=8,'x'=4,'zh'=2,'c'=2] {'zl','zh'}, dimensions={0} | all-to-all | bytes 393216 | tf_op jit(solution)/shard_map/all_to_all | solution.py:341
  78.4 13.5 %all_to_all.39.near_in = f32[32,8,128]{2,1,0:T(8,128)S(1)} all-to-all(f32[32,8,128]{2,1,0:T(8,128)S(1)} %shard_map.54), channel_id=1, replica_groups=mesh['y'=4,'zl'=8,'x'=4,'zh'=2,'c'=2] {'y','x','c'}, dimensions={0} | all-to-all | bytes 262144 | tf_op jit(solution)/shard_map/all_to_all | solution.py:341
  91.9 2.5 %shard_map.55 = (f32[32,24,128]{2,1,0:T(8,128)S(1)}, f32[16,128]{1,0:T(8,128)S(1)}, f32[8,128]{1,0:T(8,128)S(1)}, f32[4,128]{1,0:T(4,128)S(1)}) custom-call(s32[1]{0:T(128)} %bitcast.idx, s32[64,512]{1,0:T(8,128)S(1)} %copy-done, f32[32,8,128]{2,1,0:T(8,128)S(1)} %all_to_all.39.near_in, f32[16,1024]{1,0:T(8,128)S(1)} %get-tuple-element.24.q_in, ...), custom_call_target="tpu_custom_call" | custom-call | tf_op jit(solution)/shard_map/pallas_call | solution.py:335
  94.4 13.8 %all_to_all.40.near_in = f32[32,24,128]{2,1,0:T(8,128)S(1)} all-to-all(f32[32,24,128]{2,1,0:T(8,128)S(1)} %get-tuple-element.26), channel_id=1, replica_groups=mesh['y'=4,'zl'=8,'x'=4,'zh'=2,'c'=2] {'y','x','c'}, dimensions={0} | all-to-all | bytes 786432 | tf_op jit(solution)/shard_map/all_to_all | solution.py:341
  108.2 0.1 shard_map.56
  108.3 15.8 %all_to_all.41.far_in = f32[16,8,128]{2,1,0:T(8,128)S(1)} all-to-all(f32[16,8,128]{2,1,0:T(8,128)S(1)} %get-tuple-element.28), channel_id=1, replica_groups=mesh['y'=4,'zl'=8,'x'=4,'zh'=2,'c'=2] {'zl','zh'}, dimensions={0} | all-to-all | bytes 131072 | tf_op jit(solution)/shard_map/all_to_all | solution.py:341
  124.1 0.8 shard_map.57
  (2 shorter events, 0.1 us)
Async XLA Ops:
  0.6 0.7 copy-start.2
  0.6 0.7 copy-start.1
  29.2 17.4 %copy-start = (s32[64,512]{1,0:T(8,128)S(1)}, s32[64,512]{1,0:T(8,128)}, u32[]{:S(2)}) copy-start(s32[64,512]{1,0:T(8,128)} %dosage_ref.3) | copy-start | bytes 393220

commit v5 on v4

--- a/solution.py
+++ b/solution.py
@@ -18,6 +18,8 @@
 FAR = ("zl", "zh")
 N_NEAR, N_FAR = 32, 16
 N_Y, N_XC, N_ZL, N_ZH = 4, 8, 8, 2
+NEAR_FIRST = 21
+FAR_FIRST = 1
 
 f32 = jnp.float32
 bf16 = jnp.bfloat16
@@ -115,6 +117,14 @@
     return fold(jnp.concatenate(sums_q, 1)), fold(sum_a), fold(sum_b)
 
 
+def near_at(y, g):
+    return (y * N_XC + g) ^ NEAR_FIRST
+
+
+def far_at(i, h):
+    return (i * N_ZH + h) ^ FAR_FIRST
+
+
 def near_of(idx):
     return ((idx[0] >> 1) & 6) | (idx[0] & 1)
 
@@ -145,24 +155,24 @@
     for h in range(N_ZH):
         sent = jnp.where(zh_of(idx) == h, turned, q_out[...])
         for i in range(N_ZL):
-            far_out[i * N_ZH + h] = sent
+            far_out[far_at(i, h)] = sent
 
 
 def first_near_kernel(idx, far_in, q_in, near_out, f_out):
     zh = zh_of(idx)
     block = block_of_lane()
-    freqs = [far_in[i * N_ZH + zh, 0:4] for i in range(N_ZL)]
+    freqs = [far_in[far_at(i, zh), 0:4] for i in range(N_ZL)]
     for j in range(3):
         got = freqs[0]
         for i in range(1, N_ZL):
             got = jnp.where(block == (i + j) % 8, freqs[i], got)
         f_out[j] = roll(got, -16 * j)
-    own, other = q_in[...], far_in[zl_of(idx) * N_ZH + 1 - zh]
+    own, other = q_in[...], far_in[far_at(zl_of(idx), 1 - zh)]
     low, high = halves(jnp.where(zh == 0, own, other), jnp.where(zh == 0, other, own))
     for s in range(N_NEAR):
         near_out[3 * s : 3 * s + 3] = f_out[...]
     for g in range(N_XC):
-        s = 3 * (y_of(idx) * N_XC + g)
+        s = 3 * near_at(y_of(idx), g)
         near_out[s] = low[0:4]
         near_out[s + 1] = low[4:8]
         near_out[s + 2] = high[0:4]
@@ -172,8 +182,8 @@
     rows = [[], [], []]
     for x in range(4):
         for j in range(3):
-            s = 3 * (y_of(idx) * N_XC + 2 * x) + j
-            rows[j].extend(halves(near_in[s], near_in[s + 3]))
+            a, b = (near_in[3 * near_at(y_of(idx), 2 * x + c) + j] for c in range(2))
+            rows[j].extend(halves(a, b))
     return padded(rows)
 
 
@@ -181,7 +191,7 @@
     rows = [[], [], []]
     for y in range(N_Y):
         for j in range(3):
-            got = near_in[3 * (y * N_XC + near_of(idx)) + j]
+            got = near_in[3 * near_at(y, near_of(idx)) + j]
             rows[j].append(jnp.where(y_of(idx) == y, f_in[j], got))
     return padded(rows)
 
@@ -203,40 +213,40 @@
     slots[...] = jnp.zeros_like(slots)
     for s in range(N_NEAR):
         t, q = divmod(s, 4)
-        slots[s, 0:3] = sq_tmp[3 * q : 3 * q + 3, tile(t)]
+        slots[s ^ NEAR_FIRST, 0:3] = sq_tmp[3 * q : 3 * q + 3, tile(t)]
         t, g = divmod(s, 8)
-        slots[s, 3:6] = sa_tmp[3 * g : 3 * g + 3, tile(t)]
+        slots[s ^ NEAR_FIRST, 3:6] = sa_tmp[3 * g : 3 * g + 3, tile(t)]
 
 
 def near_sums_kernel(idx, near_in, far_out, q_out, a_tmp):
     for y in range(N_Y):
-        q_out[3 * y : 3 * y + 3] = sum(near_in[y * N_XC + g] for g in range(N_XC))[0:3]
+        q_out[3 * y : 3 * y + 3] = sum(near_in[near_at(y, g)] for g in range(N_XC))[0:3]
     q_out[12:24] = jnp.zeros((12, LANES), f32)
     for g in range(N_XC):
-        a_tmp[3 * g : 3 * g + 3] = sum(near_in[y * N_XC + g] for y in range(N_Y))[3:6]
+        a_tmp[3 * g : 3 * g + 3] = sum(near_in[near_at(y, g)] for y in range(N_Y))[3:6]
     for h in range(N_ZH):
         sent = jnp.where(zh_of(idx) == h, a_tmp[...], q_out[...])
         for i in range(N_ZL):
-            far_out[i * N_ZH + h] = sent
+            far_out[far_at(i, h)] = sent
 
 
 def far_sums_kernel(idx, far_in, q_in, near_out, q_tmp, a_tmp):
     zh = zh_of(idx)
-    a_tmp[...] = sum(far_in[i * N_ZH + zh] for i in range(N_ZL))
-    q_tmp[...] = q_in[...] + far_in[zl_of(idx) * N_ZH + 1 - zh]
+    a_tmp[...] = sum(far_in[far_at(i, zh)] for i in range(N_ZL))
+    q_tmp[...] = q_in[...] + far_in[far_at(zl_of(idx), 1 - zh)]
     near_out[...] = jnp.zeros_like(near_out)
     for y in range(N_Y):
         for g in range(N_XC):
-            near_out[y * N_XC + g, 0:3] = q_tmp[3 * y : 3 * y + 3]
-            near_out[y * N_XC + g, 3:6] = a_tmp[3 * g : 3 * g + 3]
+            near_out[near_at(y, g), 0:3] = q_tmp[3 * y : 3 * y + 3]
+            near_out[near_at(y, g), 3:6] = a_tmp[3 * g : 3 * g + 3]
 
 
 def two_kernel(idx, dosage_ref, near_in, q_in, f_in, near_out, sq_out, own_q, own_f, sq_tmp, sa_tmp, q_tmp, f_tmp):
     for s in range(N_NEAR):
         t, q = divmod(s, 4)
-        sq_tmp[3 * q : 3 * q + 3, tile(t)] = near_in[s, 0:3]
+        sq_tmp[3 * q : 3 * q + 3, tile(t)] = near_in[s ^ NEAR_FIRST, 0:3]
         t, g = divmod(s, 8)
-        sa_tmp[3 * g : 3 * g + 3, tile(t)] = near_in[s, 3:6]
+        sa_tmp[3 * g : 3 * g + 3, tile(t)] = near_in[s ^ NEAR_FIRST, 3:6]
     q_tmp[...] = q_in[...]
     f_tmp[...] = f_in[...]
     numer = q_tmp[0:12] * sq_tmp[0:12]
@@ -262,21 +272,21 @@
         pair = halves(sum_q[:, tile(2 * x)], sum_q[:, tile(2 * x + 1)])
         for c in range(2):
             for y in range(N_Y):
-                near_out[y * N_XC + 2 * x + c, 0:16] = pair[c]
-    sq_out[...] = near_out[near_of(idx), 0:16]
+                near_out[near_at(y, 2 * x + c), 0:16] = pair[c]
+    sq_out[...] = near_out[near_at(0, near_of(idx)), 0:16]
     sa_tmp[0:12] = sum_a[0:12]
     sa_tmp[12:24] = sum_b[0:12]
     for y in range(N_Y):
-        near_out[y * N_XC + near_of(idx)] = sa_tmp[:, tile(y)]
+        near_out[near_at(y, near_of(idx))] = sa_tmp[:, tile(y)]
 
 
 def last_far_kernel(idx, near_in, sq_in, far_out, q_out):
     zh, near = zh_of(idx), near_of(idx)
     sum_q = sq_in[...]
     for g in range(N_XC):
-        got = near_in[y_of(idx) * N_XC + g, 0:16]
+        got = near_in[near_at(y_of(idx), g), 0:16]
         sum_q = sum_q + jnp.where(near == g, 0.0, got)
-    sums = sum(near_in[y * N_XC + near] for y in range(N_Y))
+    sums = sum(near_in[near_at(y, near)] for y in range(N_Y))
     parts = halves(sum_q[0:8], sum_q[8:16])
     q_out[...] = jnp.where(zh == 0, parts[0], parts[1])
     block = block_of_lane()
@@ -287,21 +297,21 @@
             got = jnp.where(block == (i + j) % 8, turned[j], got)
         got = jnp.concatenate([got, got], 0)
         for h in range(N_ZH):
-            far_out[i * N_ZH + h] = jnp.where(zh == h, got, parts[h])
+            far_out[far_at(i, h)] = jnp.where(zh == h, got, parts[h])
 
 
 def last_kernel(idx, far_in, sq_in, own_q, own_f, shares_out, freqs_out):
     zh = zh_of(idx)
     row = lax.broadcasted_iota(jnp.int32, (8, LANES), 0)
     held = (lane() < 64) | (row < 4)
-    sum_q = sq_in[...] + far_in[zl_of(idx) * N_ZH + 1 - zh]
+    sum_q = sq_in[...] + far_in[far_at(zl_of(idx), 1 - zh)]
     numer = jnp.where(held, own_q[...] * sum_q, 0.0)
     total = jnp.sum(numer, axis=0, keepdims=True)
     total = total + pltpu.roll(total, 64, 1)
     new = (numer + 0.5) / (total + 0.5 * K)
     shares_out[0:8] = new[:, 0:64]
     shares_out[8:12] = new[0:4, 64:128]
-    sums = sum(far_in[i * N_ZH + zh, 0:4] for i in range(N_ZL))
+    sums = sum(far_in[far_at(i, zh), 0:4] for i in range(N_ZL))
     alt_part = own_f[...] * sums
     ref_part = (1.0 - own_f[...]) * roll(sums, -48)
     new = (alt_part + 0.5) / (alt_part + ref_part + 1.0)
@@ -338,7 +348,9 @@
 
 
 def exchange(x, axes):
-    return lax.all_to_all(x, axes, 0, 0, tiled=True)
+    members, first = (N_NEAR, NEAR_FIRST) if axes is NEAR else (N_FAR, FAR_FIRST)
+    order = [[i ^ first for i in range(members)]]
+    return lax.all_to_all(x, axes, 0, 0, tiled=True, axis_index_groups=order)
 
 
 def body(dosage, shares_init, freqs_init):

time: 125 us -> 115 us (0.920)
  blocking collectives: 117 us -> 106 us
    all_to_all x7, blocking collectives: 117 us -> 106 us  [exchange(): return lax.all_to_all(x, axes, 0, 0, tiled=True, axis_index_groups=order)]
where the time goes in v5:
time: 115 us; the launch traced here: 114 us
  blocking collectives  106 us (92%)
  Pallas kernels  6.25 us (5%)
    all_to_all x7, blocking collectives, exchange(): return lax.all_to_all(x, axes, 0, 0, tiled=True, axis_index_groups=order)  106 us
    pallas_call x8, Pallas kernels, placed(): return run(*args)  6.25 us

profile of v5, /device:TPU:1, one launch (start us, length us, event | category | flops | bytes accessed | tf_op | source)
XLA Modules:
  0.0 114.1 jit_solution(4905571453360682772)
XLA Ops:
  0.6 0.0 copy-start.2
  0.6 0.0 copy-start.1
  0.7 0.7 copy-done.2
  1.3 0.0 copy-done.1
  1.4 0.1 shard_map.50
  1.5 21.5 %all_to_all.35.far_in = f32[16,8,128]{2,1,0:T(8,128)S(1)} all-to-all(f32[16,8,128]{2,1,0:T(8,128)S(1)} %get-tuple-element.17), channel_id=1, replica_groups={{2,0,18,16,34,32,50,48,66,64,82,80,98,96,114,112},{3,1,19,17,35,33,51,4..., dimensions={0} | all-to-all | bytes 131072 | tf_op jit(solution)/shard_map/all_to_all | solution.py:353
  23.0 0.1 shard_map.51
  23.1 0.0 copy-start
  23.2 13.6 %all_to_all.36.near_in = f32[96,4,128]{2,1,0:T(4,128)S(1)} all-to-all(f32[96,4,128]{2,1,0:T(4,128)S(1)} %get-tuple-element.19), channel_id=1, replica_groups={{265,264,269,268,257,256,261,260,393,392,397,396,385,384,389,388,9,8,13..., dimensions={0} | all-to-all | bytes 393216 | tf_op jit(solution)/shard_map/all_to_all | solution.py:353
  36.8 0.0 copy-done
  36.8 2.5 %shard_map.52 = (f32[32,8,128]{2,1,0:T(8,128)S(1)}, f32[16,1024]{1,0:T(8,128)S(1)}, f32[16,512]{1,0:T(8,128)S(1)}) custom-call(s32[1]{0:T(128)} %bitcast.idx, s32[64,512]{1,0:T(8,128)S(1)} %copy-done, f32[96,4,128]{2,1,0:T(4,128)S(1)} %all_to_all.36.near_in, f32[3,4,128]{2,1,0:T(4,128)S(1)} %get-tuple-element.20.own_f_in), custom_call_target="tpu_custom_call" | custom-call | tf_op jit(solution)/shard_map/pallas_call | solution.py:345
  39.3 10.7 %all_to_all.37.near_in = f32[32,8,128]{2,1,0:T(8,128)S(1)} all-to-all(f32[32,8,128]{2,1,0:T(8,128)S(1)} %get-tuple-element.21), channel_id=1, replica_groups={{265,264,269,268,257,256,261,260,393,392,397,396,385,384,389,388,9,8,13..., dimensions={0} | all-to-all | bytes 262144 | tf_op jit(solution)/shard_map/all_to_all | solution.py:353
  50.0 21.7 %all_to_all.38.far_in = f32[16,24,128]{2,1,0:T(8,128)S(1)} all-to-all(f32[16,24,128]{2,1,0:T(8,128)S(1)} %get-tuple-element.22), channel_id=1, replica_groups={{2,0,18,16,34,32,50,48,66,64,82,80,98,96,114,112},{3,1,19,17,35,33,51,4..., dimensions={0} | all-to-all | bytes 393216 | tf_op jit(solution)/shard_map/all_to_all | solution.py:353
  71.8 10.8 %all_to_all.39.near_in = f32[32,8,128]{2,1,0:T(8,128)S(1)} all-to-all(f32[32,8,128]{2,1,0:T(8,128)S(1)} %shard_map.54), channel_id=1, replica_groups={{265,264,269,268,257,256,261,260,393,392,397,396,385,384,389,388,9,8,13..., dimensions={0} | all-to-all | bytes 262144 | tf_op jit(solution)/shard_map/all_to_all | solution.py:353
  82.6 2.5 %shard_map.55 = (f32[32,24,128]{2,1,0:T(8,128)S(1)}, f32[16,128]{1,0:T(8,128)S(1)}, f32[8,128]{1,0:T(8,128)S(1)}, f32[4,128]{1,0:T(4,128)S(1)}) custom-call(s32[1]{0:T(128)} %bitcast.idx, s32[64,512]{1,0:T(8,128)S(1)} %copy-done, f32[32,8,128]{2,1,0:T(8,128)S(1)} %all_to_all.39.near_in, f32[16,1024]{1,0:T(8,128)S(1)} %get-tuple-element.24.q_in, ...), custom_call_target="tpu_custom_call" | custom-call | tf_op jit(solution)/shard_map/pallas_call | solution.py:345
  85.1 13.3 %all_to_all.40.near_in = f32[32,24,128]{2,1,0:T(8,128)S(1)} all-to-all(f32[32,24,128]{2,1,0:T(8,128)S(1)} %get-tuple-element.26), channel_id=1, replica_groups={{265,264,269,268,257,256,261,260,393,392,397,396,385,384,389,388,9,8,13..., dimensions={0} | all-to-all | bytes 786432 | tf_op jit(solution)/shard_map/all_to_all | solution.py:353
  98.4 0.1 shard_map.56
  98.5 14.8 %all_to_all.41.far_in = f32[16,8,128]{2,1,0:T(8,128)S(1)} all-to-all(f32[16,8,128]{2,1,0:T(8,128)S(1)} %get-tuple-element.28), channel_id=1, replica_groups={{2,0,18,16,34,32,50,48,66,64,82,80,98,96,114,112},{3,1,19,17,35,33,51,4..., dimensions={0} | all-to-all | bytes 131072 | tf_op jit(solution)/shard_map/all_to_all | solution.py:353
  113.3 0.8 shard_map.57
  (2 shorter events, 0.1 us)
Async XLA Ops:
  0.6 0.7 copy-start.2
  0.6 0.7 copy-start.1
  23.1 13.7 %copy-start = (s32[64,512]{1,0:T(8,128)S(1)}, s32[64,512]{1,0:T(8,128)}, u32[]{:S(2)}) copy-start(s32[64,512]{1,0:T(8,128)} %dosage_ref.3) | copy-start | bytes 393220

commit v6 on v5

--- a/solution.py
+++ b/solution.py
@@ -10,16 +10,20 @@
 LANES = 128
 ROWS = 256
 
-AXES = ("y", "zl", "x", "zh", "c")
-SIZES = (4, 8, 4, 2, 2)
-SMP = ("y", "zl")
+AXES = ("y", "zq", "zp", "x", "zh", "c")
+SIZES = (4, 4, 2, 4, 2, 2)
+SMP = ("y", "zq", "zp")
 VAR = ("x", "zh", "c")
 NEAR = ("y", "x", "c")
-FAR = ("zl", "zh")
-N_NEAR, N_FAR = 32, 16
-N_Y, N_XC, N_ZL, N_ZH = 4, 8, 8, 2
+FAR = ("zq", "zp", "zh")
+WIDE = ("y", "zp", "x", "c")
+LINE = ("zq", "zh")
+N_NEAR, N_FAR, N_WIDE, N_LINE = 32, 16, 64, 8
+N_Y, N_XC, N_ZL, N_ZH, N_ZQ, N_ROW = 4, 8, 8, 2, 4, 8
 NEAR_FIRST = 21
 FAR_FIRST = 1
+WIDE_FIRST = 37
+LINE_FIRST = 1
 
 f32 = jnp.float32
 bf16 = jnp.bfloat16
@@ -123,6 +127,18 @@
 
 def far_at(i, h):
     return (i * N_ZH + h) ^ FAR_FIRST
+
+
+def wide_at(row, g):
+    return (row * N_XC + g) ^ WIDE_FIRST
+
+
+def line_at(q, h):
+    return (q * N_ZH + h) ^ LINE_FIRST
+
+
+def zq_of(idx):
+    return (idx[0] >> 5) & 3
 
 
 def near_of(idx):
@@ -201,7 +217,15 @@
     return jnp.concatenate([*rows, jnp.zeros_like(rows[0])], 0)
 
 
-def one_kernel(idx, dosage_ref, near_in, own_f_in, slots, q_out, f_out, sq_tmp, sa_tmp):
+def turned_tiles(x):
+    return jnp.concatenate([roll(x[:, tile(t)], 64) for t in range(x.shape[1] // LANES)], 1)
+
+
+def left_of(rows):
+    return lax.broadcasted_iota(jnp.int32, (rows, LANES), 1) < 64
+
+
+def one_kernel(idx, dosage_ref, near_in, own_f_in, slots, q_out, f_out, sq_tmp, sa_tmp, sq_turn, sa_turn):
     shares = shares_of(idx, near_in)
     freqs = freqs_of(idx, near_in, own_f_in)
     q_out[...] = shares
@@ -210,43 +234,62 @@
     sq_tmp[...] = sum_q
     sa_tmp[0:12] = sum_a[0:12]
     sa_tmp[12:24] = sum_b[0:12]
-    slots[...] = jnp.zeros_like(slots)
-    for s in range(N_NEAR):
-        t, q = divmod(s, 4)
-        slots[s ^ NEAR_FIRST, 0:3] = sq_tmp[3 * q : 3 * q + 3, tile(t)]
-        t, g = divmod(s, 8)
-        slots[s ^ NEAR_FIRST, 3:6] = sa_tmp[3 * g : 3 * g + 3, tile(t)]
-
-
-def near_sums_kernel(idx, near_in, far_out, q_out, a_tmp):
-    for y in range(N_Y):
-        q_out[3 * y : 3 * y + 3] = sum(near_in[near_at(y, g)] for g in range(N_XC))[0:3]
-    q_out[12:24] = jnp.zeros((12, LANES), f32)
-    for g in range(N_XC):
-        a_tmp[3 * g : 3 * g + 3] = sum(near_in[near_at(y, g)] for y in range(N_Y))[3:6]
+    sq_turn[...] = turned_tiles(sum_q)
+    sa_turn[...] = turned_tiles(sa_tmp[...])
+    left = left_of(3)
+    for w in range(N_WIDE):
+        t, q = divmod(w, 4)
+        a = (sq_turn if t % 2 else sq_tmp)[3 * q : 3 * q + 3, tile(t // 2)]
+        t, q = divmod(w, 8)
+        b = (sa_tmp if t % 2 else sa_turn)[3 * q : 3 * q + 3, tile(t // 2)]
+        slots[w ^ WIDE_FIRST, 0:3] = jnp.where(left, a, b)
+
+
+def put_line(line_out, at, rows):
+    for b in range(3):
+        line_out[3 * at + b] = rows[4 * b : 4 * b + 4]
+
+
+def wide_sums_kernel(idx, wide_in, line_out, q_out, a_tmp):
+    left = left_of(4)
+    row_sums = [sum(wide_in[wide_at(r, g)] for g in range(N_XC)) for r in range(N_ROW)]
+    col_sums = [sum(wide_in[wide_at(r, g)] for r in range(N_ROW)) for g in range(N_XC)]
+    for i in range(4):
+        q_out[3 * i : 3 * i + 3] = jnp.where(left, row_sums[i], roll(row_sums[i + 4], 64))[0:3]
+        a_tmp[3 * i : 3 * i + 3] = jnp.where(left, roll(col_sums[i], 64), col_sums[i + 4])[0:3]
     for h in range(N_ZH):
         sent = jnp.where(zh_of(idx) == h, a_tmp[...], q_out[...])
-        for i in range(N_ZL):
-            far_out[far_at(i, h)] = sent
-
-
-def far_sums_kernel(idx, far_in, q_in, near_out, q_tmp, a_tmp):
+        for i in range(N_ZQ):
+            put_line(line_out, line_at(i, h), sent)
+
+
+def line_sums_kernel(idx, line_in, q_in, wide_out, q_tmp, a_tmp):
     zh = zh_of(idx)
-    a_tmp[...] = sum(far_in[far_at(i, zh)] for i in range(N_ZL))
-    q_tmp[...] = q_in[...] + far_in[far_at(zl_of(idx), 1 - zh)]
-    near_out[...] = jnp.zeros_like(near_out)
-    for y in range(N_Y):
+    for b in range(3):
+        a_tmp[4 * b : 4 * b + 4] = sum(line_in[3 * line_at(i, zh) + b] for i in range(N_ZQ))
+        other = line_in[3 * line_at(zq_of(idx), 1 - zh) + b]
+        q_tmp[4 * b : 4 * b + 4] = q_in[4 * b : 4 * b + 4] + other
+    left = left_of(3)
+    row_sums, col_sums = [], []
+    for i in range(8):
+        at = 3 * (i % 4)
+        row_sums.append(roll(q_tmp[at : at + 3], 64 * (i // 4)))
+        col_sums.append(roll(a_tmp[at : at + 3], 64 * (1 - i // 4)))
+    for r in range(N_ROW):
         for g in range(N_XC):
-            near_out[near_at(y, g), 0:3] = q_tmp[3 * y : 3 * y + 3]
-            near_out[near_at(y, g), 3:6] = a_tmp[3 * g : 3 * g + 3]
-
-
-def two_kernel(idx, dosage_ref, near_in, q_in, f_in, near_out, sq_out, own_q, own_f, sq_tmp, sa_tmp, q_tmp, f_tmp):
-    for s in range(N_NEAR):
-        t, q = divmod(s, 4)
-        sq_tmp[3 * q : 3 * q + 3, tile(t)] = near_in[s ^ NEAR_FIRST, 0:3]
-        t, g = divmod(s, 8)
-        sa_tmp[3 * g : 3 * g + 3, tile(t)] = near_in[s ^ NEAR_FIRST, 3:6]
+            wide_out[wide_at(r, g), 0:3] = jnp.where(left, row_sums[r], col_sums[g])
+
+
+def two_kernel(idx, dosage_ref, wide_in, q_in, f_in, near_out, sq_out, own_q, own_f, sq_tmp, sa_tmp, q_tmp, f_tmp):
+    left = left_of(4)
+    for t in range(8):
+        for q in range(4):
+            a, b = (wide_in[(8 * t + 4 * half + q) ^ WIDE_FIRST] for half in range(2))
+            sq_tmp[3 * q : 3 * q + 3, tile(t)] = jnp.where(left, a, roll(b, 64))[0:3]
+    for t in range(4):
+        for q in range(8):
+            a, b = (wide_in[(16 * t + 8 * half + q) ^ WIDE_FIRST] for half in range(2))
+            sa_tmp[3 * q : 3 * q + 3, tile(t)] = jnp.where(left, roll(a, 64), b)[0:3]
     q_tmp[...] = q_in[...]
     f_tmp[...] = f_in[...]
     numer = q_tmp[0:12] * sq_tmp[0:12]
@@ -348,7 +391,12 @@
 
 
 def exchange(x, axes):
-    members, first = (N_NEAR, NEAR_FIRST) if axes is NEAR else (N_FAR, FAR_FIRST)
+    members, first = {
+        NEAR: (N_NEAR, NEAR_FIRST),
+        FAR: (N_FAR, FAR_FIRST),
+        WIDE: (N_WIDE, WIDE_FIRST),
+        LINE: (N_LINE, LINE_FIRST),
+    }[axes]
     order = [[i ^ first for i in range(members)]]
     return lax.all_to_all(x, axes, 0, 0, tiled=True, axis_index_groups=order)
 
@@ -366,23 +414,23 @@
     )(idx, far_got, own_q)
     near_got = exchange(near_slots, NEAR)
     slots, shares, freqs = call(
-        one_kernel, 1, 3, [tiles(N_NEAR), f32s(PAD, samples), f32s(PAD, variants)],
-        [vmem(PAD, samples), vmem(24, variants)],
+        one_kernel, 1, 3, [f32s(N_WIDE, 4, LANES), f32s(PAD, samples), f32s(PAD, variants)],
+        [vmem(PAD, samples), vmem(24, variants), vmem(PAD, samples), vmem(24, variants)],
     )(idx, dosage, near_got, own_f)
-    near_got = exchange(slots, NEAR)
-    far_slots, own_sum = call(
-        near_sums_kernel, 1, 1, [f32s(N_FAR, 24, LANES), f32s(24, LANES)], [vmem(24, LANES)]
-    )(idx, near_got)
-    far_got = exchange(far_slots, FAR)
-    (near_slots,) = call(
-        far_sums_kernel, 1, 2, [tiles(N_NEAR)], [vmem(24, LANES), vmem(24, LANES)]
-    )(idx, far_got, own_sum)
-    near_got = exchange(near_slots, NEAR)
+    wide_got = exchange(slots, WIDE)
+    line_slots, own_sum = call(
+        wide_sums_kernel, 1, 1, [f32s(3 * N_LINE, 4, LANES), f32s(12, LANES)], [vmem(12, LANES)]
+    )(idx, wide_got)
+    line_got = exchange(line_slots, LINE)
+    (wide_slots,) = call(
+        line_sums_kernel, 1, 2, [f32s(N_WIDE, 4, LANES)], [vmem(12, LANES), vmem(12, LANES)]
+    )(idx, line_got, own_sum)
+    wide_got = exchange(wide_slots, WIDE)
     near_slots, own_sum, own_q, own_f = call(
         two_kernel, 1, 4,
         [f32s(N_NEAR, 24, LANES), f32s(PAD, LANES), f32s(8, LANES), f32s(4, LANES)],
         [vmem(PAD, samples), vmem(24, variants), vmem(PAD, samples), vmem(PAD, variants)],
-    )(idx, dosage, near_got, shares, freqs)
+    )(idx, dosage, wide_got, shares, freqs)
     near_got = exchange(near_slots, NEAR)
     far_slots, own_sum = call(last_far_kernel, 1, 2, [tiles(N_FAR), f32s(8, LANES)], [])(
         idx, near_got, own_sum

time: 115 us -> 112 us (0.974)
  blocking collectives: 106 us -> 104 us
    all_to_all x7, blocking collectives: 106 us -> 104 us  [exchange(): return lax.all_to_all(x, axes, 0, 0, tiled=True, axis_index_groups=order)]
where the time goes in v6:
time: 112 us
  blocking collectives  104 us (93%)
  Pallas kernels  6.41 us (6%)
    all_to_all x7, blocking collectives, exchange(): return lax.all_to_all(x, axes, 0, 0, tiled=True, axis_index_groups=order)  104 us
    pallas_call x8, Pallas kernels, placed(): return run(*args)  6.41 us

profile of v6, /device:TPU:1, one launch (start us, length us, event | category | flops | bytes accessed | tf_op | source)
XLA Modules:
  0.0 111.6 jit_solution(13051786089695428457)
XLA Ops:
  0.6 0.0 copy-start.2
  0.7 0.0 copy-start.1
  0.7 0.7 copy-done.2
  1.3 0.0 copy-done.1
  1.4 0.1 shard_map.50
  1.5 21.5 %all_to_all.35.far_in = f32[16,8,128]{2,1,0:T(8,128)S(1)} all-to-all(f32[16,8,128]{2,1,0:T(8,128)S(1)} %get-tuple-element.17), channel_id=1, replica_groups={{2,0,18,16,34,32,50,48,66,64,82,80,98,96,114,112},{3,1,19,17,35,33,51,4..., dimensions={0} | all-to-all | bytes 131072 | tf_op jit(solution)/shard_map/all_to_all | solution.py:401
  23.0 0.1 shard_map.51
  23.1 0.0 copy-start
  23.2 13.6 %all_to_all.36.near_in = f32[96,4,128]{2,1,0:T(4,128)S(1)} all-to-all(f32[96,4,128]{2,1,0:T(4,128)S(1)} %get-tuple-element.19), channel_id=1, replica_groups={{265,264,269,268,257,256,261,260,393,392,397,396,385,384,389,388,9,8,13..., dimensions={0} | all-to-all | bytes 393216 | tf_op jit(solution)/shard_map/all_to_all | solution.py:401
  36.8 0.0 copy-done
  36.8 2.6 %shard_map.52 = (f32[64,4,128]{2,1,0:T(4,128)S(1)}, f32[16,1024]{1,0:T(8,128)S(1)}, f32[16,512]{1,0:T(8,128)S(1)}) custom-call(s32[1]{0:T(128)} %bitcast.idx, s32[64,512]{1,0:T(8,128)S(1)} %copy-done, f32[96,4,128]{2,1,0:T(4,128)S(1)} %all_to_all.36.near_in, f32[3,4,128]{2,1,0:T(4,128)S(1)} %get-tuple-element.20.own_f_in), custom_call_target="tpu_custom_call" | custom-call | tf_op jit(solution)/shard_map/pallas_call | solution.py:388
  39.4 13.1 %all_to_all.37.wide_in = f32[64,4,128]{2,1,0:T(4,128)S(1)} all-to-all(f32[64,4,128]{2,1,0:T(4,128)S(1)} %get-tuple-element.21), channel_id=1, replica_groups={{265,264,269,268,257,256,261,260,281,280,285,284,273,272,277,276,393,39..., dimensions={0} | all-to-all | bytes 262144 | tf_op jit(solution)/shard_map/all_to_all | solution.py:401
  52.5 0.1 shard_map.53
  52.6 14.2 %all_to_all.38.line_in = f32[24,4,128]{2,1,0:T(4,128)S(1)} all-to-all(f32[24,4,128]{2,1,0:T(4,128)S(1)} %get-tuple-element.22), channel_id=1, replica_groups={{2,0,34,32,66,64,98,96},{3,1,35,33,67,65,99,97},{6,4,38,36,70,68,102,10..., dimensions={0} | all-to-all | bytes 98304 | tf_op jit(solution)/shard_map/all_to_all | solution.py:401
  66.8 0.1 shard_map.54
  66.9 12.8 %all_to_all.39.wide_in = f32[64,4,128]{2,1,0:T(4,128)S(1)} all-to-all(f32[64,4,128]{2,1,0:T(4,128)S(1)} %shard_map.54), channel_id=1, replica_groups={{265,264,269,268,257,256,261,260,281,280,285,284,273,272,277,276,393,39..., dimensions={0} | all-to-all | bytes 262144 | tf_op jit(solution)/shard_map/all_to_all | solution.py:401
  79.6 2.5 %shard_map.55 = (f32[32,24,128]{2,1,0:T(8,128)S(1)}, f32[16,128]{1,0:T(8,128)S(1)}, f32[8,128]{1,0:T(8,128)S(1)}, f32[4,128]{1,0:T(4,128)S(1)}) custom-call(s32[1]{0:T(128)} %bitcast.idx, s32[64,512]{1,0:T(8,128)S(1)} %copy-done, f32[64,4,128]{2,1,0:T(4,128)S(1)} %all_to_all.39.wide_in, f32[16,1024]{1,0:T(8,128)S(1)} %get-tuple-element.24.q_in, ...), custom_call_target="tpu_custom_call" | custom-call | tf_op jit(solution)/shard_map/pallas_call | solution.py:388
  82.1 13.6 %all_to_all.40.near_in = f32[32,24,128]{2,1,0:T(8,128)S(1)} all-to-all(f32[32,24,128]{2,1,0:T(8,128)S(1)} %get-tuple-element.26), channel_id=1, replica_groups={{265,264,269,268,257,256,261,260,393,392,397,396,385,384,389,388,9,8,13..., dimensions={0} | all-to-all | bytes 786432 | tf_op jit(solution)/shard_map/all_to_all | solution.py:401
  95.7 0.1 shard_map.56
  95.8 14.9 %all_to_all.41.far_in = f32[16,8,128]{2,1,0:T(8,128)S(1)} all-to-all(f32[16,8,128]{2,1,0:T(8,128)S(1)} %get-tuple-element.28), channel_id=1, replica_groups={{2,0,18,16,34,32,50,48,66,64,82,80,98,96,114,112},{3,1,19,17,35,33,51,4..., dimensions={0} | all-to-all | bytes 131072 | tf_op jit(solution)/shard_map/all_to_all | solution.py:401
  110.7 0.8 shard_map.57
Async XLA Ops:
  0.6 0.7 copy-start.2
  0.7 0.7 copy-start.1
  23.1 13.7 %copy-start = (s32[64,512]{1,0:T(8,128)S(1)}, s32[64,512]{1,0:T(8,128)}, u32[]{:S(2)}) copy-start(s32[64,512]{1,0:T(8,128)} %dosage_ref.3) | copy-start | bytes 393220

commit v7 on v6

--- a/solution.py
+++ b/solution.py
@@ -20,10 +20,7 @@
 LINE = ("zq", "zh")
 N_NEAR, N_FAR, N_WIDE, N_LINE = 32, 16, 64, 8
 N_Y, N_XC, N_ZL, N_ZH, N_ZQ, N_ROW = 4, 8, 8, 2, 4, 8
-NEAR_FIRST = 21
-FAR_FIRST = 1
-WIDE_FIRST = 37
-LINE_FIRST = 1
+FAR_1, NEAR_1, WIDE_1, LINE_1, WIDE_2, NEAR_2, FAR_2 = 1, 21, 35, 1, 37, 19, 14
 
 f32 = jnp.float32
 bf16 = jnp.bfloat16
@@ -121,20 +118,12 @@
     return fold(jnp.concatenate(sums_q, 1)), fold(sum_a), fold(sum_b)
 
 
-def near_at(y, g):
-    return (y * N_XC + g) ^ NEAR_FIRST
-
-
-def far_at(i, h):
-    return (i * N_ZH + h) ^ FAR_FIRST
-
-
-def wide_at(row, g):
-    return (row * N_XC + g) ^ WIDE_FIRST
-
-
-def line_at(q, h):
-    return (q * N_ZH + h) ^ LINE_FIRST
+def in_plane(y, g):
+    return y * N_XC + g
+
+
+def in_line(i, h):
+    return i * N_ZH + h
 
 
 def zq_of(idx):
@@ -171,24 +160,24 @@
     for h in range(N_ZH):
         sent = jnp.where(zh_of(idx) == h, turned, q_out[...])
         for i in range(N_ZL):
-            far_out[far_at(i, h)] = sent
+            far_out[in_line(i, h) ^ FAR_1] = sent
 
 
 def first_near_kernel(idx, far_in, q_in, near_out, f_out):
     zh = zh_of(idx)
     block = block_of_lane()
-    freqs = [far_in[far_at(i, zh), 0:4] for i in range(N_ZL)]
+    freqs = [far_in[in_line(i, zh) ^ FAR_1, 0:4] for i in range(N_ZL)]
     for j in range(3):
         got = freqs[0]
         for i in range(1, N_ZL):
             got = jnp.where(block == (i + j) % 8, freqs[i], got)
         f_out[j] = roll(got, -16 * j)
-    own, other = q_in[...], far_in[far_at(zl_of(idx), 1 - zh)]
+    own, other = q_in[...], far_in[in_line(zl_of(idx), 1 - zh) ^ FAR_1]
     low, high = halves(jnp.where(zh == 0, own, other), jnp.where(zh == 0, other, own))
     for s in range(N_NEAR):
         near_out[3 * s : 3 * s + 3] = f_out[...]
     for g in range(N_XC):
-        s = 3 * near_at(y_of(idx), g)
+        s = 3 * (in_plane(y_of(idx), g) ^ NEAR_1)
         near_out[s] = low[0:4]
         near_out[s + 1] = low[4:8]
         near_out[s + 2] = high[0:4]
@@ -198,7 +187,7 @@
     rows = [[], [], []]
     for x in range(4):
         for j in range(3):
-            a, b = (near_in[3 * near_at(y_of(idx), 2 * x + c) + j] for c in range(2))
+            a, b = (near_in[3 * (in_plane(y_of(idx), 2 * x + c) ^ NEAR_1) + j] for c in range(2))
             rows[j].extend(halves(a, b))
     return padded(rows)
 
@@ -207,7 +196,7 @@
     rows = [[], [], []]
     for y in range(N_Y):
         for j in range(3):
-            got = near_in[3 * near_at(y, near_of(idx)) + j]
+            got = near_in[3 * (in_plane(y, near_of(idx)) ^ NEAR_1) + j]
             rows[j].append(jnp.where(y_of(idx) == y, f_in[j], got))
     return padded(rows)
 
@@ -242,7 +231,7 @@
         a = (sq_turn if t % 2 else sq_tmp)[3 * q : 3 * q + 3, tile(t // 2)]
         t, q = divmod(w, 8)
         b = (sa_tmp if t % 2 else sa_turn)[3 * q : 3 * q + 3, tile(t // 2)]
-        slots[w ^ WIDE_FIRST, 0:3] = jnp.where(left, a, b)
+        slots[w ^ WIDE_1, 0:3] = jnp.where(left, a, b)
 
 
 def put_line(line_out, at, rows):
@@ -252,22 +241,22 @@
 
 def wide_sums_kernel(idx, wide_in, line_out, q_out, a_tmp):
     left = left_of(4)
-    row_sums = [sum(wide_in[wide_at(r, g)] for g in range(N_XC)) for r in range(N_ROW)]
-    col_sums = [sum(wide_in[wide_at(r, g)] for r in range(N_ROW)) for g in range(N_XC)]
+    row_sums = [sum(wide_in[in_plane(r, g) ^ WIDE_1] for g in range(N_XC)) for r in range(N_ROW)]
+    col_sums = [sum(wide_in[in_plane(r, g) ^ WIDE_1] for r in range(N_ROW)) for g in range(N_XC)]
     for i in range(4):
         q_out[3 * i : 3 * i + 3] = jnp.where(left, row_sums[i], roll(row_sums[i + 4], 64))[0:3]
         a_tmp[3 * i : 3 * i + 3] = jnp.where(left, roll(col_sums[i], 64), col_sums[i + 4])[0:3]
     for h in range(N_ZH):
         sent = jnp.where(zh_of(idx) == h, a_tmp[...], q_out[...])
         for i in range(N_ZQ):
-            put_line(line_out, line_at(i, h), sent)
+            put_line(line_out, in_line(i, h) ^ LINE_1, sent)
 
 
 def line_sums_kernel(idx, line_in, q_in, wide_out, q_tmp, a_tmp):
     zh = zh_of(idx)
     for b in range(3):
-        a_tmp[4 * b : 4 * b + 4] = sum(line_in[3 * line_at(i, zh) + b] for i in range(N_ZQ))
-        other = line_in[3 * line_at(zq_of(idx), 1 - zh) + b]
+        a_tmp[4 * b : 4 * b + 4] = sum(line_in[3 * (in_line(i, zh) ^ LINE_1) + b] for i in range(N_ZQ))
+        other = line_in[3 * (in_line(zq_of(idx), 1 - zh) ^ LINE_1) + b]
         q_tmp[4 * b : 4 * b + 4] = q_in[4 * b : 4 * b + 4] + other
     left = left_of(3)
     row_sums, col_sums = [], []
@@ -277,18 +266,18 @@
         col_sums.append(roll(a_tmp[at : at + 3], 64 * (1 - i // 4)))
     for r in range(N_ROW):
         for g in range(N_XC):
-            wide_out[wide_at(r, g), 0:3] = jnp.where(left, row_sums[r], col_sums[g])
+            wide_out[in_plane(r, g) ^ WIDE_2, 0:3] = jnp.where(left, row_sums[r], col_sums[g])
 
 
 def two_kernel(idx, dosage_ref, wide_in, q_in, f_in, near_out, sq_out, own_q, own_f, sq_tmp, sa_tmp, q_tmp, f_tmp):
     left = left_of(4)
     for t in range(8):
         for q in range(4):
-            a, b = (wide_in[(8 * t + 4 * half + q) ^ WIDE_FIRST] for half in range(2))
+            a, b = (wide_in[(8 * t + 4 * half + q) ^ WIDE_2] for half in range(2))
             sq_tmp[3 * q : 3 * q + 3, tile(t)] = jnp.where(left, a, roll(b, 64))[0:3]
     for t in range(4):
         for q in range(8):
-            a, b = (wide_in[(16 * t + 8 * half + q) ^ WIDE_FIRST] for half in range(2))
+            a, b = (wide_in[(16 * t + 8 * half + q) ^ WIDE_2] for half in range(2))
             sa_tmp[3 * q : 3 * q + 3, tile(t)] = jnp.where(left, roll(a, 64), b)[0:3]
     q_tmp[...] = q_in[...]
     f_tmp[...] = f_in[...]
@@ -315,21 +304,21 @@
         pair = halves(sum_q[:, tile(2 * x)], sum_q[:, tile(2 * x + 1)])
         for c in range(2):
             for y in range(N_Y):
-                near_out[near_at(y, 2 * x + c), 0:16] = pair[c]
-    sq_out[...] = near_out[near_at(0, near_of(idx)), 0:16]
+                near_out[in_plane(y, 2 * x + c) ^ NEAR_2, 0:16] = pair[c]
+    sq_out[...] = near_out[in_plane(0, near_of(idx)) ^ NEAR_2, 0:16]
     sa_tmp[0:12] = sum_a[0:12]
     sa_tmp[12:24] = sum_b[0:12]
     for y in range(N_Y):
-        near_out[near_at(y, near_of(idx))] = sa_tmp[:, tile(y)]
+        near_out[in_plane(y, near_of(idx)) ^ NEAR_2] = sa_tmp[:, tile(y)]
 
 
 def last_far_kernel(idx, near_in, sq_in, far_out, q_out):
     zh, near = zh_of(idx), near_of(idx)
     sum_q = sq_in[...]
     for g in range(N_XC):
-        got = near_in[near_at(y_of(idx), g), 0:16]
+        got = near_in[in_plane(y_of(idx), g) ^ NEAR_2, 0:16]
         sum_q = sum_q + jnp.where(near == g, 0.0, got)
-    sums = sum(near_in[near_at(y, near)] for y in range(N_Y))
+    sums = sum(near_in[in_plane(y, near) ^ NEAR_2] for y in range(N_Y))
     parts = halves(sum_q[0:8], sum_q[8:16])
     q_out[...] = jnp.where(zh == 0, parts[0], parts[1])
     block = block_of_lane()
@@ -340,21 +329,21 @@
             got = jnp.where(block == (i + j) % 8, turned[j], got)
         got = jnp.concatenate([got, got], 0)
         for h in range(N_ZH):
-            far_out[far_at(i, h)] = jnp.where(zh == h, got, parts[h])
+            far_out[in_line(i, h) ^ FAR_2] = jnp.where(zh == h, got, parts[h])
 
 
 def last_kernel(idx, far_in, sq_in, own_q, own_f, shares_out, freqs_out):
     zh = zh_of(idx)
     row = lax.broadcasted_iota(jnp.int32, (8, LANES), 0)
     held = (lane() < 64) | (row < 4)
-    sum_q = sq_in[...] + far_in[far_at(zl_of(idx), 1 - zh)]
+    sum_q = sq_in[...] + far_in[in_line(zl_of(idx), 1 - zh) ^ FAR_2]
     numer = jnp.where(held, own_q[...] * sum_q, 0.0)
     total = jnp.sum(numer, axis=0, keepdims=True)
     total = total + pltpu.roll(total, 64, 1)
     new = (numer + 0.5) / (total + 0.5 * K)
     shares_out[0:8] = new[:, 0:64]
     shares_out[8:12] = new[0:4, 64:128]
-    sums = sum(far_in[far_at(i, zh), 0:4] for i in range(N_ZL))
+    sums = sum(far_in[in_line(i, zh) ^ FAR_2, 0:4] for i in range(N_ZL))
     alt_part = own_f[...] * sums
     ref_part = (1.0 - own_f[...]) * roll(sums, -48)
     new = (alt_part + 0.5) / (alt_part + ref_part + 1.0)
@@ -390,13 +379,10 @@
     return placed
 
 
-def exchange(x, axes):
-    members, first = {
-        NEAR: (N_NEAR, NEAR_FIRST),
-        FAR: (N_FAR, FAR_FIRST),
-        WIDE: (N_WIDE, WIDE_FIRST),
-        LINE: (N_LINE, LINE_FIRST),
-    }[axes]
+def exchange(x, axes, first):
+    members = 1
+    for axis in axes:
+        members *= SIZES[AXES.index(axis)]
     order = [[i ^ first for i in range(members)]]
     return lax.all_to_all(x, axes, 0, 0, tiled=True, axis_index_groups=order)
 
@@ -408,34 +394,34 @@
     far_slots, own_q = call(first_kernel, 1, 2, [tiles(N_FAR), f32s(8, LANES)], [vmem(8, LANES)])(
         idx, shares_init, freqs_init
     )
-    far_got = exchange(far_slots, FAR)
+    far_got = exchange(far_slots, FAR, FAR_1)
     near_slots, own_f = call(
         first_near_kernel, 1, 2, [f32s(3 * N_NEAR, 4, LANES), f32s(3, 4, LANES)], []
     )(idx, far_got, own_q)
-    near_got = exchange(near_slots, NEAR)
+    near_got = exchange(near_slots, NEAR, NEAR_1)
     slots, shares, freqs = call(
         one_kernel, 1, 3, [f32s(N_WIDE, 4, LANES), f32s(PAD, samples), f32s(PAD, variants)],
         [vmem(PAD, samples), vmem(24, variants), vmem(PAD, samples), vmem(24, variants)],
     )(idx, dosage, near_got, own_f)
-    wide_got = exchange(slots, WIDE)
+    wide_got = exchange(slots, WIDE, WIDE_1)
     line_slots, own_sum = call(
         wide_sums_kernel, 1, 1, [f32s(3 * N_LINE, 4, LANES), f32s(12, LANES)], [vmem(12, LANES)]
     )(idx, wide_got)
-    line_got = exchange(line_slots, LINE)
+    line_got = exchange(line_slots, LINE, LINE_1)
     (wide_slots,) = call(
         line_sums_kernel, 1, 2, [f32s(N_WIDE, 4, LANES)], [vmem(12, LANES), vmem(12, LANES)]
     )(idx, line_got, own_sum)
-    wide_got = exchange(wide_slots, WIDE)
+    wide_got = exchange(wide_slots, WIDE, WIDE_2)
     near_slots, own_sum, own_q, own_f = call(
         two_kernel, 1, 4,
         [f32s(N_NEAR, 24, LANES), f32s(PAD, LANES), f32s(8, LANES), f32s(4, LANES)],
         [vmem(PAD, samples), vmem(24, variants), vmem(PAD, samples), vmem(PAD, variants)],
     )(idx, dosage, wide_got, shares, freqs)
-    near_got = exchange(near_slots, NEAR)
+    near_got = exchange(near_slots, NEAR, NEAR_2)
     far_slots, own_sum = call(last_far_kernel, 1, 2, [tiles(N_FAR), f32s(8, LANES)], [])(
         idx, near_got, own_sum
     )
-    far_got = exchange(far_slots, FAR)
+    far_got = exchange(far_slots, FAR, FAR_2)
     return tuple(
         call(last_kernel, 1, 4, [f32s(*shares_init.shape), f32s(*freqs_init.shape)], [], False)(
             idx, far_got, own_sum, own_q, own_f

time: 112 us -> 117 us (1.045)
  blocking collectives: 104 us -> 108 us
    all_to_all x7, blocking collectives: 104 us -> 108 us  [exchange(): return lax.all_to_all(x, axes, 0, 0, tiled=True, axis_index_groups=order)]
where the time goes in v7:
time: 117 us; the launch traced here: 116 us
  blocking collectives  108 us (92%)
  Pallas kernels  6.41 us (5%)
    all_to_all x7, blocking collectives, exchange(): return lax.all_to_all(x, axes, 0, 0, tiled=True, axis_index_groups=order)  108 us
    pallas_call x8, Pallas kernels, placed(): return run(*args)  6.41 us

profile of v7, /device:TPU:1, one launch (start us, length us, event | category | flops | bytes accessed | tf_op | source)
XLA Modules:
  0.0 116.2 jit_solution(9581811387612644195)
XLA Ops:
  0.6 0.0 copy-start.2
  0.7 0.0 copy-start.1
  0.7 0.7 copy-done.2
  1.3 0.0 copy-done.1
  1.4 0.1 shard_map.50
  1.5 21.5 %all_to_all.35.far_in = f32[16,8,128]{2,1,0:T(8,128)S(1)} all-to-all(f32[16,8,128]{2,1,0:T(8,128)S(1)} %get-tuple-element.17), channel_id=1, replica_groups={{2,0,18,16,34,32,50,48,66,64,82,80,98,96,114,112},{3,1,19,17,35,33,51,4..., dimensions={0} | all-to-all | bytes 131072 | tf_op jit(solution)/shard_map/all_to_all | solution.py:387
  23.0 0.1 shard_map.51
  23.1 0.0 copy-start
  23.2 13.6 %all_to_all.36.near_in = f32[96,4,128]{2,1,0:T(4,128)S(1)} all-to-all(f32[96,4,128]{2,1,0:T(4,128)S(1)} %get-tuple-element.19), channel_id=1, replica_groups={{265,264,269,268,257,256,261,260,393,392,397,396,385,384,389,388,9,8,13..., dimensions={0} | all-to-all | bytes 393216 | tf_op jit(solution)/shard_map/all_to_all | solution.py:387
  36.8 0.0 copy-done
  36.8 2.6 %shard_map.52 = (f32[64,4,128]{2,1,0:T(4,128)S(1)}, f32[16,1024]{1,0:T(8,128)S(1)}, f32[16,512]{1,0:T(8,128)S(1)}) custom-call(s32[1]{0:T(128)} %bitcast.idx, s32[64,512]{1,0:T(8,128)S(1)} %copy-done, f32[96,4,128]{2,1,0:T(4,128)S(1)} %all_to_all.36.near_in, f32[3,4,128]{2,1,0:T(4,128)S(1)} %get-tuple-element.20.own_f_in), custom_call_target="tpu_custom_call" | custom-call | tf_op jit(solution)/shard_map/pallas_call | solution.py:377
  39.4 14.7 %all_to_all.37.wide_in = f32[64,4,128]{2,1,0:T(4,128)S(1)} all-to-all(f32[64,4,128]{2,1,0:T(4,128)S(1)} %get-tuple-element.21), channel_id=1, replica_groups={{261,260,257,256,269,268,265,264,277,276,273,272,285,284,281,280,389,38..., dimensions={0} | all-to-all | bytes 262144 | tf_op jit(solution)/shard_map/all_to_all | solution.py:387
  54.1 0.1 shard_map.53
  54.2 13.9 %all_to_all.38.line_in = f32[24,4,128]{2,1,0:T(4,128)S(1)} all-to-all(f32[24,4,128]{2,1,0:T(4,128)S(1)} %get-tuple-element.22), channel_id=1, replica_groups={{2,0,34,32,66,64,98,96},{3,1,35,33,67,65,99,97},{6,4,38,36,70,68,102,10..., dimensions={0} | all-to-all | bytes 98304 | tf_op jit(solution)/shard_map/all_to_all | solution.py:387
  68.1 0.1 shard_map.54
  68.2 12.4 %all_to_all.39.wide_in = f32[64,4,128]{2,1,0:T(4,128)S(1)} all-to-all(f32[64,4,128]{2,1,0:T(4,128)S(1)} %shard_map.54), channel_id=1, replica_groups={{265,264,269,268,257,256,261,260,281,280,285,284,273,272,277,276,393,39..., dimensions={0} | all-to-all | bytes 262144 | tf_op jit(solution)/shard_map/all_to_all | solution.py:387
  80.5 2.5 %shard_map.55 = (f32[32,24,128]{2,1,0:T(8,128)S(1)}, f32[16,128]{1,0:T(8,128)S(1)}, f32[8,128]{1,0:T(8,128)S(1)}, f32[4,128]{1,0:T(4,128)S(1)}) custom-call(s32[1]{0:T(128)} %bitcast.idx, s32[64,512]{1,0:T(8,128)S(1)} %copy-done, f32[64,4,128]{2,1,0:T(4,128)S(1)} %all_to_all.39.wide_in, f32[16,1024]{1,0:T(8,128)S(1)} %get-tuple-element.24.q_in, ...), custom_call_target="tpu_custom_call" | custom-call | tf_op jit(solution)/shard_map/pallas_call | solution.py:377
  83.0 14.8 %all_to_all.40.near_in = f32[32,24,128]{2,1,0:T(8,128)S(1)} all-to-all(f32[32,24,128]{2,1,0:T(8,128)S(1)} %get-tuple-element.26), channel_id=1, replica_groups={{261,260,257,256,269,268,265,264,389,388,385,384,397,396,393,392,5,4,1,..., dimensions={0} | all-to-all | bytes 786432 | tf_op jit(solution)/shard_map/all_to_all | solution.py:387
  97.8 0.1 shard_map.56
  97.9 17.5 %all_to_all.41.far_in = f32[16,8,128]{2,1,0:T(8,128)S(1)} all-to-all(f32[16,8,128]{2,1,0:T(8,128)S(1)} %get-tuple-element.28), channel_id=1, replica_groups={{112,114,96,98,80,82,64,66,48,50,32,34,16,18,0,2},{113,115,97,99,81,83,..., dimensions={0} | all-to-all | bytes 131072 | tf_op jit(solution)/shard_map/all_to_all | solution.py:387
  115.4 0.8 shard_map.57
Async XLA Ops:
  0.6 0.7 copy-start.2
  0.7 0.7 copy-start.1
  23.1 13.7 %copy-start = (s32[64,512]{1,0:T(8,128)S(1)}, s32[64,512]{1,0:T(8,128)}, u32[]{:S(2)}) copy-start(s32[64,512]{1,0:T(8,128)} %dosage_ref.3) | copy-start | bytes 393220

commit v8 on v7

--- a/solution.py
+++ b/solution.py
@@ -20,7 +20,9 @@
 LINE = ("zq", "zh")
 N_NEAR, N_FAR, N_WIDE, N_LINE = 32, 16, 64, 8
 N_Y, N_XC, N_ZL, N_ZH, N_ZQ, N_ROW = 4, 8, 8, 2, 4, 8
-FAR_1, NEAR_1, WIDE_1, LINE_1, WIDE_2, NEAR_2, FAR_2 = 1, 21, 35, 1, 37, 19, 14
+FAR_1 = LINE_1 = FAR_2 = 1
+NEAR_1 = NEAR_2 = 21
+WIDE_1 = WIDE_2 = 37
 
 f32 = jnp.float32
 bf16 = jnp.bfloat16
@@ -147,40 +149,48 @@
     return lax.broadcasted_iota(jnp.int32, (4, LANES), 1) // 16
 
 
+def put_far(far_out, at, rows):
+    for b in range(3):
+        far_out[3 * at + b] = rows[2 * b : 2 * b + 2]
+
+
+def get_far(far_in, at, pairs):
+    return jnp.concatenate([far_in[3 * at + b] for b in range(pairs)], 0)
+
+
 def first_kernel(idx, shares_ref, freqs_ref, far_out, q_out, f_tmp):
     raw = shares_ref[...]
     own = raw / jnp.sum(raw, axis=0, keepdims=True)
     q_out[...] = jnp.zeros_like(q_out)
     f_tmp[...] = jnp.zeros_like(f_tmp)
-    q_out[:, 0:64] = own[0:8]
-    q_out[0:4, 64:128] = own[8:12]
+    q_out[0:6, 0:64] = own[0:6]
+    q_out[0:6, 64:128] = own[6:12]
     for j in range(3):
         f_tmp[0:4, 16 * j : 16 * j + 16] = freqs_ref[4 * j : 4 * j + 4, :]
     turned = pltpu.roll(f_tmp[...], 16 * zl_of(idx), 1)
     for h in range(N_ZH):
         sent = jnp.where(zh_of(idx) == h, turned, q_out[...])
         for i in range(N_ZL):
-            far_out[in_line(i, h) ^ FAR_1] = sent
-
-
-def first_near_kernel(idx, far_in, q_in, near_out, f_out):
+            put_far(far_out, in_line(i, h) ^ FAR_1, sent)
+
+
+def first_near_kernel(idx, far_in, q_in, near_out, f_out, q_tmp):
     zh = zh_of(idx)
     block = block_of_lane()
-    freqs = [far_in[in_line(i, zh) ^ FAR_1, 0:4] for i in range(N_ZL)]
+    freqs = [get_far(far_in, in_line(i, zh) ^ FAR_1, 2) for i in range(N_ZL)]
     for j in range(3):
         got = freqs[0]
         for i in range(1, N_ZL):
             got = jnp.where(block == (i + j) % 8, freqs[i], got)
         f_out[j] = roll(got, -16 * j)
-    own, other = q_in[...], far_in[in_line(zl_of(idx), 1 - zh) ^ FAR_1]
-    low, high = halves(jnp.where(zh == 0, own, other), jnp.where(zh == 0, other, own))
+    own, other = q_in[0:6], get_far(far_in, in_line(zl_of(idx), 1 - zh) ^ FAR_1, 3)
+    q_tmp[0:6], q_tmp[6:12] = halves(jnp.where(zh == 0, own, other), jnp.where(zh == 0, other, own))
     for s in range(N_NEAR):
         near_out[3 * s : 3 * s + 3] = f_out[...]
     for g in range(N_XC):
         s = 3 * (in_plane(y_of(idx), g) ^ NEAR_1)
-        near_out[s] = low[0:4]
-        near_out[s + 1] = low[4:8]
-        near_out[s + 2] = high[0:4]
+        for j in range(3):
+            near_out[s + j] = q_tmp[4 * j : 4 * j + 4]
 
 
 def shares_of(idx, near_in):
@@ -288,7 +298,7 @@
     f_tmp[0:12] = (alt_part + 0.5) / (alt_part + (1.0 - old) * sa_tmp[12:24] + 1.0)
 
     t = pl.multiple_of((var_of(idx) >> 1) * LANES, LANES)
-    even, odd = halves(q_tmp[0:8, pl.ds(t, LANES)], q_tmp[8:16, pl.ds(t, LANES)])
+    even, odd = halves(q_tmp[0:6, pl.ds(t, LANES)], q_tmp[6:12, pl.ds(t, LANES)])
     own_q[...] = jnp.where((var_of(idx) & 1) == 0, even, odd)
     t = pl.multiple_of((smp_of(idx) >> 3) * LANES, LANES)
     block = block_of_lane()
@@ -319,7 +329,7 @@
         got = near_in[in_plane(y_of(idx), g) ^ NEAR_2, 0:16]
         sum_q = sum_q + jnp.where(near == g, 0.0, got)
     sums = sum(near_in[in_plane(y, near) ^ NEAR_2] for y in range(N_Y))
-    parts = halves(sum_q[0:8], sum_q[8:16])
+    parts = halves(sum_q[0:6], sum_q[6:12])
     q_out[...] = jnp.where(zh == 0, parts[0], parts[1])
     block = block_of_lane()
     turned = [roll(sums[4 * j : 4 * j + 4], 16 * j) for j in range(6)]
@@ -327,23 +337,21 @@
         got = turned[0]
         for j in range(1, 6):
             got = jnp.where(block == (i + j) % 8, turned[j], got)
-        got = jnp.concatenate([got, got], 0)
+        got = jnp.concatenate([got, got[0:2]], 0)
         for h in range(N_ZH):
-            far_out[in_line(i, h) ^ FAR_2] = jnp.where(zh == h, got, parts[h])
+            put_far(far_out, in_line(i, h) ^ FAR_2, jnp.where(zh == h, got, parts[h]))
 
 
 def last_kernel(idx, far_in, sq_in, own_q, own_f, shares_out, freqs_out):
     zh = zh_of(idx)
-    row = lax.broadcasted_iota(jnp.int32, (8, LANES), 0)
-    held = (lane() < 64) | (row < 4)
-    sum_q = sq_in[...] + far_in[in_line(zl_of(idx), 1 - zh) ^ FAR_2]
-    numer = jnp.where(held, own_q[...] * sum_q, 0.0)
+    sum_q = sq_in[...] + get_far(far_in, in_line(zl_of(idx), 1 - zh) ^ FAR_2, 3)
+    numer = own_q[...] * sum_q
     total = jnp.sum(numer, axis=0, keepdims=True)
     total = total + pltpu.roll(total, 64, 1)
     new = (numer + 0.5) / (total + 0.5 * K)
-    shares_out[0:8] = new[:, 0:64]
-    shares_out[8:12] = new[0:4, 64:128]
-    sums = sum(far_in[in_line(i, zh) ^ FAR_2, 0:4] for i in range(N_ZL))
+    shares_out[0:6] = new[:, 0:64]
+    shares_out[6:12] = new[:, 64:128]
+    sums = sum(get_far(far_in, in_line(i, zh) ^ FAR_2, 2) for i in range(N_ZL))
     alt_part = own_f[...] * sums
     ref_part = (1.0 - own_f[...]) * roll(sums, -48)
     new = (alt_part + 0.5) / (alt_part + ref_part + 1.0)
@@ -390,13 +398,13 @@
 def body(dosage, shares_init, freqs_init):
     idx = lax.axis_index(AXES).astype(jnp.int32).reshape(1)
     samples, variants = 16 * dosage.shape[0], dosage.shape[1]
-    tiles = lambda n: f32s(n, 8, LANES)
-    far_slots, own_q = call(first_kernel, 1, 2, [tiles(N_FAR), f32s(8, LANES)], [vmem(8, LANES)])(
+    pairs = f32s(3 * N_FAR, 2, LANES)
+    far_slots, own_q = call(first_kernel, 1, 2, [pairs, f32s(8, LANES)], [vmem(8, LANES)])(
         idx, shares_init, freqs_init
     )
     far_got = exchange(far_slots, FAR, FAR_1)
     near_slots, own_f = call(
-        first_near_kernel, 1, 2, [f32s(3 * N_NEAR, 4, LANES), f32s(3, 4, LANES)], []
+        first_near_kernel, 1, 2, [f32s(3 * N_NEAR, 4, LANES), f32s(3, 4, LANES)], [vmem(12, LANES)]
     )(idx, far_got, own_q)
     near_got = exchange(near_slots, NEAR, NEAR_1)
     slots, shares, freqs = call(
@@ -414,11 +422,11 @@
     wide_got = exchange(wide_slots, WIDE, WIDE_2)
     near_slots, own_sum, own_q, own_f = call(
         two_kernel, 1, 4,
-        [f32s(N_NEAR, 24, LANES), f32s(PAD, LANES), f32s(8, LANES), f32s(4, LANES)],
+        [f32s(N_NEAR, 24, LANES), f32s(PAD, LANES), f32s(6, LANES), f32s(4, LANES)],
         [vmem(PAD, samples), vmem(24, variants), vmem(PAD, samples), vmem(PAD, variants)],
     )(idx, dosage, wide_got, shares, freqs)
     near_got = exchange(near_slots, NEAR, NEAR_2)
-    far_slots, own_sum = call(last_far_kernel, 1, 2, [tiles(N_FAR), f32s(8, LANES)], [])(
+    far_slots, own_sum = call(last_far_kernel, 1, 2, [pairs, f32s(6, LANES)], [])(
         idx, near_got, own_sum
     )
     far_got = exchange(far_slots, FAR, FAR_2)

time: 117 us -> 111 us (0.949)
  blocking collectives: 108 us -> 103 us
    all_to_all x7, blocking collectives: 108 us -> 103 us  [exchange(): return lax.all_to_all(x, axes, 0, 0, tiled=True, axis_index_groups=order)]
where the time goes in v8:
time: 111 us
  blocking collectives  103 us (93%)
  Pallas kernels  6.42 us (6%)
    all_to_all x7, blocking collectives, exchange(): return lax.all_to_all(x, axes, 0, 0, tiled=True, axis_index_groups=order)  103 us
    pallas_call x8, Pallas kernels, placed(): return run(*args)  6.42 us

profile of v8, /device:TPU:1, one launch (start us, length us, event | category | flops | bytes accessed | tf_op | source)
XLA Modules:
  0.0 110.6 jit_solution(16840783131821979771)
XLA Ops:
  0.6 0.0 copy-start.2
  0.7 0.0 copy-start.1
  0.7 0.7 copy-done.2
  1.3 0.0 copy-done.1
  1.4 0.1 shard_map.50
  1.5 21.3 %all_to_all.35.far_in = f32[48,2,128]{2,1,0:T(2,128)S(1)} all-to-all(f32[48,2,128]{2,1,0:T(2,128)S(1)} %get-tuple-element.17), channel_id=1, replica_groups={{2,0,18,16,34,32,50,48,66,64,82,80,98,96,114,112},{3,1,19,17,35,33,51,4..., dimensions={0} | all-to-all | bytes 98304 | tf_op jit(solution)/shard_map/all_to_all | solution.py:395
  22.8 0.1 shard_map.51
  22.9 0.0 copy-start
  22.9 13.7 %all_to_all.36.near_in = f32[96,4,128]{2,1,0:T(4,128)S(1)} all-to-all(f32[96,4,128]{2,1,0:T(4,128)S(1)} %get-tuple-element.19), channel_id=1, replica_groups={{265,264,269,268,257,256,261,260,393,392,397,396,385,384,389,388,9,8,13..., dimensions={0} | all-to-all | bytes 393216 | tf_op jit(solution)/shard_map/all_to_all | solution.py:395
  36.6 0.0 copy-done
  36.6 2.6 %shard_map.52 = (f32[64,4,128]{2,1,0:T(4,128)S(1)}, f32[16,1024]{1,0:T(8,128)S(1)}, f32[16,512]{1,0:T(8,128)S(1)}) custom-call(s32[1]{0:T(128)} %bitcast.idx, s32[64,512]{1,0:T(8,128)S(1)} %copy-done, f32[96,4,128]{2,1,0:T(4,128)S(1)} %all_to_all.36.near_in, f32[3,4,128]{2,1,0:T(4,128)S(1)} %get-tuple-element.20.own_f_in), custom_call_target="tpu_custom_call" | custom-call | tf_op jit(solution)/shard_map/pallas_call | solution.py:385
  39.2 13.0 %all_to_all.37.wide_in = f32[64,4,128]{2,1,0:T(4,128)S(1)} all-to-all(f32[64,4,128]{2,1,0:T(4,128)S(1)} %get-tuple-element.21), channel_id=1, replica_groups={{265,264,269,268,257,256,261,260,281,280,285,284,273,272,277,276,393,39..., dimensions={0} | all-to-all | bytes 262144 | tf_op jit(solution)/shard_map/all_to_all | solution.py:395
  52.1 0.1 shard_map.53
  52.2 14.2 %all_to_all.38.line_in = f32[24,4,128]{2,1,0:T(4,128)S(1)} all-to-all(f32[24,4,128]{2,1,0:T(4,128)S(1)} %get-tuple-element.22), channel_id=1, replica_groups={{2,0,34,32,66,64,98,96},{3,1,35,33,67,65,99,97},{6,4,38,36,70,68,102,10..., dimensions={0} | all-to-all | bytes 98304 | tf_op jit(solution)/shard_map/all_to_all | solution.py:395
  66.4 0.1 shard_map.54
  66.5 12.7 %all_to_all.39.wide_in = f32[64,4,128]{2,1,0:T(4,128)S(1)} all-to-all(f32[64,4,128]{2,1,0:T(4,128)S(1)} %shard_map.54), channel_id=1, replica_groups={{265,264,269,268,257,256,261,260,281,280,285,284,273,272,277,276,393,39..., dimensions={0} | all-to-all | bytes 262144 | tf_op jit(solution)/shard_map/all_to_all | solution.py:395
  79.3 2.5 %shard_map.55 = (f32[32,24,128]{2,1,0:T(8,128)S(1)}, f32[16,128]{1,0:T(8,128)S(1)}, f32[6,128]{1,0:T(8,128)S(1)}, f32[4,128]{1,0:T(4,128)S(1)}) custom-call(s32[1]{0:T(128)} %bitcast.idx, s32[64,512]{1,0:T(8,128)S(1)} %copy-done, f32[64,4,128]{2,1,0:T(4,128)S(1)} %all_to_all.39.wide_in, f32[16,1024]{1,0:T(8,128)S(1)} %get-tuple-element.24.q_in, ...), custom_call_target="tpu_custom_call" | custom-call | tf_op jit(solution)/shard_map/pallas_call | solution.py:385
  81.8 13.6 %all_to_all.40.near_in = f32[32,24,128]{2,1,0:T(8,128)S(1)} all-to-all(f32[32,24,128]{2,1,0:T(8,128)S(1)} %get-tuple-element.26), channel_id=1, replica_groups={{265,264,269,268,257,256,261,260,393,392,397,396,385,384,389,388,9,8,13..., dimensions={0} | all-to-all | bytes 786432 | tf_op jit(solution)/shard_map/all_to_all | solution.py:395
  95.4 0.1 shard_map.56
  95.5 14.4 %all_to_all.41.far_in = f32[48,2,128]{2,1,0:T(2,128)S(1)} all-to-all(f32[48,2,128]{2,1,0:T(2,128)S(1)} %get-tuple-element.28), channel_id=1, replica_groups={{2,0,18,16,34,32,50,48,66,64,82,80,98,96,114,112},{3,1,19,17,35,33,51,4..., dimensions={0} | all-to-all | bytes 98304 | tf_op jit(solution)/shard_map/all_to_all | solution.py:395
  109.8 0.8 shard_map.57
Async XLA Ops:
  0.6 0.7 copy-start.2
  0.7 0.7 copy-start.1
  22.9 13.7 %copy-start = (s32[64,512]{1,0:T(8,128)S(1)}, s32[64,512]{1,0:T(8,128)}, u32[]{:S(2)}) copy-start(s32[64,512]{1,0:T(8,128)} %dosage_ref.3) | copy-start | bytes 393220

commit v9 on v8

--- a/solution.py
+++ b/solution.py
@@ -21,8 +21,8 @@
 N_NEAR, N_FAR, N_WIDE, N_LINE = 32, 16, 64, 8
 N_Y, N_XC, N_ZL, N_ZH, N_ZQ, N_ROW = 4, 8, 8, 2, 4, 8
 FAR_1 = LINE_1 = FAR_2 = 1
-NEAR_1 = NEAR_2 = 21
-WIDE_1 = WIDE_2 = 37
+NEAR_1 = NEAR_2 = 20
+WIDE_1 = WIDE_2 = 36
 
 f32 = jnp.float32
 bf16 = jnp.bfloat16

time: 111 us -> 112 us (level)
    all_to_all x7, blocking collectives: 103 us -> 104 us  [exchange(): return lax.all_to_all(x, axes, 0, 0, tiled=True, axis_index_groups=order)]
where the time goes in v9:
time: 112 us
  blocking collectives  104 us (93%)
  Pallas kernels  6.41 us (6%)
    all_to_all x7, blocking collectives, exchange(): return lax.all_to_all(x, axes, 0, 0, tiled=True, axis_index_groups=order)  104 us
    pallas_call x8, Pallas kernels, placed(): return run(*args)  6.41 us

profile of v9, /device:TPU:1, one launch (start us, length us, event | category | flops | bytes accessed | tf_op | source)
XLA Modules:
  0.0 111.9 jit_solution(16914575999316551300)
XLA Ops:
  0.6 0.0 copy-start.2
  0.7 0.0 copy-start.1
  0.7 0.7 copy-done.2
  1.3 0.0 copy-done.1
  1.4 0.1 shard_map.50
  1.5 21.3 %all_to_all.35.far_in = f32[48,2,128]{2,1,0:T(2,128)S(1)} all-to-all(f32[48,2,128]{2,1,0:T(2,128)S(1)} %get-tuple-element.17), channel_id=1, replica_groups={{2,0,18,16,34,32,50,48,66,64,82,80,98,96,114,112},{3,1,19,17,35,33,51,4..., dimensions={0} | all-to-all | bytes 98304 | tf_op jit(solution)/shard_map/all_to_all | solution.py:395
  22.8 0.1 shard_map.51
  22.9 0.0 copy-start
  22.9 13.8 %all_to_all.36.near_in = f32[96,4,128]{2,1,0:T(4,128)S(1)} all-to-all(f32[96,4,128]{2,1,0:T(4,128)S(1)} %get-tuple-element.19), channel_id=1, replica_groups={{264,265,268,269,256,257,260,261,392,393,396,397,384,385,388,389,8,9,12..., dimensions={0} | all-to-all | bytes 393216 | tf_op jit(solution)/shard_map/all_to_all | solution.py:395
  36.7 0.0 copy-done
  36.7 2.6 %shard_map.52 = (f32[64,4,128]{2,1,0:T(4,128)S(1)}, f32[16,1024]{1,0:T(8,128)S(1)}, f32[16,512]{1,0:T(8,128)S(1)}) custom-call(s32[1]{0:T(128)} %bitcast.idx, s32[64,512]{1,0:T(8,128)S(1)} %copy-done, f32[96,4,128]{2,1,0:T(4,128)S(1)} %all_to_all.36.near_in, f32[3,4,128]{2,1,0:T(4,128)S(1)} %get-tuple-element.20.own_f_in), custom_call_target="tpu_custom_call" | custom-call | tf_op jit(solution)/shard_map/pallas_call | solution.py:385
  39.3 13.6 %all_to_all.37.wide_in = f32[64,4,128]{2,1,0:T(4,128)S(1)} all-to-all(f32[64,4,128]{2,1,0:T(4,128)S(1)} %get-tuple-element.21), channel_id=1, replica_groups={{264,265,268,269,256,257,260,261,280,281,284,285,272,273,276,277,392,39..., dimensions={0} | all-to-all | bytes 262144 | tf_op jit(solution)/shard_map/all_to_all | solution.py:395
  52.9 0.1 shard_map.53
  53.0 13.9 %all_to_all.38.line_in = f32[24,4,128]{2,1,0:T(4,128)S(1)} all-to-all(f32[24,4,128]{2,1,0:T(4,128)S(1)} %get-tuple-element.22), channel_id=1, replica_groups={{2,0,34,32,66,64,98,96},{3,1,35,33,67,65,99,97},{6,4,38,36,70,68,102,10..., dimensions={0} | all-to-all | bytes 98304 | tf_op jit(solution)/shard_map/all_to_all | solution.py:395
  67.0 0.1 shard_map.54
  67.1 13.5 %all_to_all.39.wide_in = f32[64,4,128]{2,1,0:T(4,128)S(1)} all-to-all(f32[64,4,128]{2,1,0:T(4,128)S(1)} %shard_map.54), channel_id=1, replica_groups={{264,265,268,269,256,257,260,261,280,281,284,285,272,273,276,277,392,39..., dimensions={0} | all-to-all | bytes 262144 | tf_op jit(solution)/shard_map/all_to_all | solution.py:395
  80.5 2.5 %shard_map.55 = (f32[32,24,128]{2,1,0:T(8,128)S(1)}, f32[16,128]{1,0:T(8,128)S(1)}, f32[6,128]{1,0:T(8,128)S(1)}, f32[4,128]{1,0:T(4,128)S(1)}) custom-call(s32[1]{0:T(128)} %bitcast.idx, s32[64,512]{1,0:T(8,128)S(1)} %copy-done, f32[64,4,128]{2,1,0:T(4,128)S(1)} %all_to_all.39.wide_in, f32[16,1024]{1,0:T(8,128)S(1)} %get-tuple-element.24.q_in, ...), custom_call_target="tpu_custom_call" | custom-call | tf_op jit(solution)/shard_map/pallas_call | solution.py:385
  83.0 13.6 %all_to_all.40.near_in = f32[32,24,128]{2,1,0:T(8,128)S(1)} all-to-all(f32[32,24,128]{2,1,0:T(8,128)S(1)} %get-tuple-element.26), channel_id=1, replica_groups={{264,265,268,269,256,257,260,261,392,393,396,397,384,385,388,389,8,9,12..., dimensions={0} | all-to-all | bytes 786432 | tf_op jit(solution)/shard_map/all_to_all | solution.py:395
  96.7 0.1 shard_map.56
  96.8 14.3 %all_to_all.41.far_in = f32[48,2,128]{2,1,0:T(2,128)S(1)} all-to-all(f32[48,2,128]{2,1,0:T(2,128)S(1)} %get-tuple-element.28), channel_id=1, replica_groups={{2,0,18,16,34,32,50,48,66,64,82,80,98,96,114,112},{3,1,19,17,35,33,51,4..., dimensions={0} | all-to-all | bytes 98304 | tf_op jit(solution)/shard_map/all_to_all | solution.py:395
  111.1 0.8 shard_map.57
Async XLA Ops:
  0.6 0.7 copy-start.2
  0.7 0.7 copy-start.1
  22.9 13.8 %copy-start = (s32[64,512]{1,0:T(8,128)S(1)}, s32[64,512]{1,0:T(8,128)}, u32[]{:S(2)}) copy-start(s32[64,512]{1,0:T(8,128)} %dosage_ref.3) | copy-start | bytes 393220

commit v10 on v9

--- a/solution.py
+++ b/solution.py
@@ -16,13 +16,12 @@
 VAR = ("x", "zh", "c")
 NEAR = ("y", "x", "c")
 FAR = ("zq", "zp", "zh")
-WIDE = ("y", "zp", "x", "c")
 LINE = ("zq", "zh")
 N_NEAR, N_FAR, N_WIDE, N_LINE = 32, 16, 64, 8
 N_Y, N_XC, N_ZL, N_ZH, N_ZQ, N_ROW = 4, 8, 8, 2, 4, 8
-FAR_1 = LINE_1 = FAR_2 = 1
-NEAR_1 = NEAR_2 = 20
-WIDE_1 = WIDE_2 = 36
+FAR_FIRST = 1
+NEAR_FIRST = 21
+WIDE_FIRST = 37
 
 f32 = jnp.float32
 bf16 = jnp.bfloat16
@@ -128,6 +127,10 @@
     return i * N_ZH + h
 
 
+def in_wide(idx, member):
+    return (member ^ WIDE_FIRST) ^ (8 - 8 * zh_of(idx))
+
+
 def zq_of(idx):
     return (idx[0] >> 5) & 3
 
@@ -171,24 +174,24 @@
     for h in range(N_ZH):
         sent = jnp.where(zh_of(idx) == h, turned, q_out[...])
         for i in range(N_ZL):
-            put_far(far_out, in_line(i, h) ^ FAR_1, sent)
+            put_far(far_out, in_line(i, h) ^ FAR_FIRST, sent)
 
 
 def first_near_kernel(idx, far_in, q_in, near_out, f_out, q_tmp):
     zh = zh_of(idx)
     block = block_of_lane()
-    freqs = [get_far(far_in, in_line(i, zh) ^ FAR_1, 2) for i in range(N_ZL)]
+    freqs = [get_far(far_in, in_line(i, zh) ^ FAR_FIRST, 2) for i in range(N_ZL)]
     for j in range(3):
         got = freqs[0]
         for i in range(1, N_ZL):
             got = jnp.where(block == (i + j) % 8, freqs[i], got)
         f_out[j] = roll(got, -16 * j)
-    own, other = q_in[0:6], get_far(far_in, in_line(zl_of(idx), 1 - zh) ^ FAR_1, 3)
+    own, other = q_in[0:6], get_far(far_in, in_line(zl_of(idx), 1 - zh) ^ FAR_FIRST, 3)
     q_tmp[0:6], q_tmp[6:12] = halves(jnp.where(zh == 0, own, other), jnp.where(zh == 0, other, own))
     for s in range(N_NEAR):
         near_out[3 * s : 3 * s + 3] = f_out[...]
     for g in range(N_XC):
-        s = 3 * (in_plane(y_of(idx), g) ^ NEAR_1)
+        s = 3 * (in_plane(y_of(idx), g) ^ NEAR_FIRST)
         for j in range(3):
             near_out[s + j] = q_tmp[4 * j : 4 * j + 4]
 
@@ -197,7 +200,7 @@
     rows = [[], [], []]
     for x in range(4):
         for j in range(3):
-            a, b = (near_in[3 * (in_plane(y_of(idx), 2 * x + c) ^ NEAR_1) + j] for c in range(2))
+            a, b = (near_in[3 * (in_plane(y_of(idx), 2 * x + c) ^ NEAR_FIRST) + j] for c in range(2))
             rows[j].extend(halves(a, b))
     return padded(rows)
 
@@ -206,7 +209,7 @@
     rows = [[], [], []]
     for y in range(N_Y):
         for j in range(3):
-            got = near_in[3 * (in_plane(y, near_of(idx)) ^ NEAR_1) + j]
+            got = near_in[3 * (in_plane(y, near_of(idx)) ^ NEAR_FIRST) + j]
             rows[j].append(jnp.where(y_of(idx) == y, f_in[j], got))
     return padded(rows)
 
@@ -241,7 +244,7 @@
         a = (sq_turn if t % 2 else sq_tmp)[3 * q : 3 * q + 3, tile(t // 2)]
         t, q = divmod(w, 8)
         b = (sa_tmp if t % 2 else sa_turn)[3 * q : 3 * q + 3, tile(t // 2)]
-        slots[w ^ WIDE_1, 0:3] = jnp.where(left, a, b)
+        slots[in_wide(idx, w), 0:3] = jnp.where(left, a, b)
 
 
 def put_line(line_out, at, rows):
@@ -251,22 +254,22 @@
 
 def wide_sums_kernel(idx, wide_in, line_out, q_out, a_tmp):
     left = left_of(4)
-    row_sums = [sum(wide_in[in_plane(r, g) ^ WIDE_1] for g in range(N_XC)) for r in range(N_ROW)]
-    col_sums = [sum(wide_in[in_plane(r, g) ^ WIDE_1] for r in range(N_ROW)) for g in range(N_XC)]
+    row_sums = [sum(wide_in[in_wide(idx, in_plane(r, g))] for g in range(N_XC)) for r in range(N_ROW)]
+    col_sums = [sum(wide_in[in_wide(idx, in_plane(r, g))] for r in range(N_ROW)) for g in range(N_XC)]
     for i in range(4):
         q_out[3 * i : 3 * i + 3] = jnp.where(left, row_sums[i], roll(row_sums[i + 4], 64))[0:3]
         a_tmp[3 * i : 3 * i + 3] = jnp.where(left, roll(col_sums[i], 64), col_sums[i + 4])[0:3]
     for h in range(N_ZH):
         sent = jnp.where(zh_of(idx) == h, a_tmp[...], q_out[...])
         for i in range(N_ZQ):
-            put_line(line_out, in_line(i, h) ^ LINE_1, sent)
+            put_line(line_out, in_line(i, h) ^ FAR_FIRST, sent)
 
 
 def line_sums_kernel(idx, line_in, q_in, wide_out, q_tmp, a_tmp):
     zh = zh_of(idx)
     for b in range(3):
-        a_tmp[4 * b : 4 * b + 4] = sum(line_in[3 * (in_line(i, zh) ^ LINE_1) + b] for i in range(N_ZQ))
-        other = line_in[3 * (in_line(zq_of(idx), 1 - zh) ^ LINE_1) + b]
+        a_tmp[4 * b : 4 * b + 4] = sum(line_in[3 * (in_line(i, zh) ^ FAR_FIRST) + b] for i in range(N_ZQ))
+        other = line_in[3 * (in_line(zq_of(idx), 1 - zh) ^ FAR_FIRST) + b]
         q_tmp[4 * b : 4 * b + 4] = q_in[4 * b : 4 * b + 4] + other
     left = left_of(3)
     row_sums, col_sums = [], []
@@ -276,18 +279,18 @@
         col_sums.append(roll(a_tmp[at : at + 3], 64 * (1 - i // 4)))
     for r in range(N_ROW):
         for g in range(N_XC):
-            wide_out[in_plane(r, g) ^ WIDE_2, 0:3] = jnp.where(left, row_sums[r], col_sums[g])
+            wide_out[in_wide(idx, in_plane(r, g)), 0:3] = jnp.where(left, row_sums[r], col_sums[g])
 
 
 def two_kernel(idx, dosage_ref, wide_in, q_in, f_in, near_out, sq_out, own_q, own_f, sq_tmp, sa_tmp, q_tmp, f_tmp):
     left = left_of(4)
     for t in range(8):
         for q in range(4):
-            a, b = (wide_in[(8 * t + 4 * half + q) ^ WIDE_2] for half in range(2))
+            a, b = (wide_in[in_wide(idx, 8 * t + 4 * half + q)] for half in range(2))
             sq_tmp[3 * q : 3 * q + 3, tile(t)] = jnp.where(left, a, roll(b, 64))[0:3]
     for t in range(4):
         for q in range(8):
-            a, b = (wide_in[(16 * t + 8 * half + q) ^ WIDE_2] for half in range(2))
+            a, b = (wide_in[in_wide(idx, 16 * t + 8 * half + q)] for half in range(2))
             sa_tmp[3 * q : 3 * q + 3, tile(t)] = jnp.where(left, roll(a, 64), b)[0:3]
     q_tmp[...] = q_in[...]
     f_tmp[...] = f_in[...]
@@ -314,21 +317,21 @@
         pair = halves(sum_q[:, tile(2 * x)], sum_q[:, tile(2 * x + 1)])
         for c in range(2):
             for y in range(N_Y):
-                near_out[in_plane(y, 2 * x + c) ^ NEAR_2, 0:16] = pair[c]
-    sq_out[...] = near_out[in_plane(0, near_of(idx)) ^ NEAR_2, 0:16]
+                near_out[in_plane(y, 2 * x + c) ^ NEAR_FIRST, 0:16] = pair[c]
+    sq_out[...] = near_out[in_plane(0, near_of(idx)) ^ NEAR_FIRST, 0:16]
     sa_tmp[0:12] = sum_a[0:12]
     sa_tmp[12:24] = sum_b[0:12]
     for y in range(N_Y):
-        near_out[in_plane(y, near_of(idx)) ^ NEAR_2] = sa_tmp[:, tile(y)]
+        near_out[in_plane(y, near_of(idx)) ^ NEAR_FIRST] = sa_tmp[:, tile(y)]
 
 
 def last_far_kernel(idx, near_in, sq_in, far_out, q_out):
     zh, near = zh_of(idx), near_of(idx)
     sum_q = sq_in[...]
     for g in range(N_XC):
-        got = near_in[in_plane(y_of(idx), g) ^ NEAR_2, 0:16]
+        got = near_in[in_plane(y_of(idx), g) ^ NEAR_FIRST, 0:16]
         sum_q = sum_q + jnp.where(near == g, 0.0, got)
-    sums = sum(near_in[in_plane(y, near) ^ NEAR_2] for y in range(N_Y))
+    sums = sum(near_in[in_plane(y, near) ^ NEAR_FIRST] for y in range(N_Y))
     parts = halves(sum_q[0:6], sum_q[6:12])
     q_out[...] = jnp.where(zh == 0, parts[0], parts[1])
     block = block_of_lane()
@@ -339,19 +342,19 @@
             got = jnp.where(block == (i + j) % 8, turned[j], got)
         got = jnp.concatenate([got, got[0:2]], 0)
         for h in range(N_ZH):
-            put_far(far_out, in_line(i, h) ^ FAR_2, jnp.where(zh == h, got, parts[h]))
+            put_far(far_out, in_line(i, h) ^ FAR_FIRST, jnp.where(zh == h, got, parts[h]))
 
 
 def last_kernel(idx, far_in, sq_in, own_q, own_f, shares_out, freqs_out):
     zh = zh_of(idx)
-    sum_q = sq_in[...] + get_far(far_in, in_line(zl_of(idx), 1 - zh) ^ FAR_2, 3)
+    sum_q = sq_in[...] + get_far(far_in, in_line(zl_of(idx), 1 - zh) ^ FAR_FIRST, 3)
     numer = own_q[...] * sum_q
     total = jnp.sum(numer, axis=0, keepdims=True)
     total = total + pltpu.roll(total, 64, 1)
     new = (numer + 0.5) / (total + 0.5 * K)
     shares_out[0:6] = new[:, 0:64]
     shares_out[6:12] = new[:, 64:128]
-    sums = sum(get_far(far_in, in_line(i, zh) ^ FAR_2, 2) for i in range(N_ZL))
+    sums = sum(get_far(far_in, in_line(i, zh) ^ FAR_FIRST, 2) for i in range(N_ZL))
     alt_part = own_f[...] * sums
     ref_part = (1.0 - own_f[...]) * roll(sums, -48)
     new = (alt_part + 0.5) / (alt_part + ref_part + 1.0)
@@ -395,6 +398,21 @@
     return lax.all_to_all(x, axes, 0, 0, tiled=True, axis_index_groups=order)
 
 
+def wide_exchange(x):
+    groups = []
+    for zq in range(N_ZQ):
+        for zh in range(N_ZH):
+            first = WIDE_FIRST ^ (8 - 8 * zh)
+            members = [i ^ first for i in range(N_WIDE)]
+            groups.append(
+                [
+                    (m >> 4) << 7 | zq << 5 | (m >> 3 & 1) << 4 | (m >> 1 & 3) << 2 | zh << 1 | (m & 1)
+                    for m in members
+                ]
+            )
+    return lax.all_to_all(x, AXES, 0, 0, tiled=True, axis_index_groups=groups)
+
+
 def body(dosage, shares_init, freqs_init):
     idx = lax.axis_index(AXES).astype(jnp.int32).reshape(1)
     samples, variants = 16 * dosage.shape[0], dosage.shape[1]
@@ -402,34 +420,34 @@
     far_slots, own_q = call(first_kernel, 1, 2, [pairs, f32s(8, LANES)], [vmem(8, LANES)])(
         idx, shares_init, freqs_init
     )
-    far_got = exchange(far_slots, FAR, FAR_1)
+    far_got = exchange(far_slots, FAR, FAR_FIRST)
     near_slots, own_f = call(
         first_near_kernel, 1, 2, [f32s(3 * N_NEAR, 4, LANES), f32s(3, 4, LANES)], [vmem(12, LANES)]
     )(idx, far_got, own_q)
-    near_got = exchange(near_slots, NEAR, NEAR_1)
+    near_got = exchange(near_slots, NEAR, NEAR_FIRST)
     slots, shares, freqs = call(
         one_kernel, 1, 3, [f32s(N_WIDE, 4, LANES), f32s(PAD, samples), f32s(PAD, variants)],
         [vmem(PAD, samples), vmem(24, variants), vmem(PAD, samples), vmem(24, variants)],
     )(idx, dosage, near_got, own_f)
-    wide_got = exchange(slots, WIDE, WIDE_1)
+    wide_got = wide_exchange(slots)
     line_slots, own_sum = call(
         wide_sums_kernel, 1, 1, [f32s(3 * N_LINE, 4, LANES), f32s(12, LANES)], [vmem(12, LANES)]
     )(idx, wide_got)
-    line_got = exchange(line_slots, LINE, LINE_1)
+    line_got = exchange(line_slots, LINE, FAR_FIRST)
     (wide_slots,) = call(
         line_sums_kernel, 1, 2, [f32s(N_WIDE, 4, LANES)], [vmem(12, LANES), vmem(12, LANES)]
     )(idx, line_got, own_sum)
-    wide_got = exchange(wide_slots, WIDE, WIDE_2)
+    wide_got = wide_exchange(wide_slots)
     near_slots, own_sum, own_q, own_f = call(
         two_kernel, 1, 4,
         [f32s(N_NEAR, 24, LANES), f32s(PAD, LANES), f32s(6, LANES), f32s(4, LANES)],
         [vmem(PAD, samples), vmem(24, variants), vmem(PAD, samples), vmem(PAD, variants)],
     )(idx, dosage, wide_got, shares, freqs)
-    near_got = exchange(near_slots, NEAR, NEAR_2)
+    near_got = exchange(near_slots, NEAR, NEAR_FIRST)
     far_slots, own_sum = call(last_far_kernel, 1, 2, [pairs, f32s(6, LANES)], [])(
         idx, near_got, own_sum
     )
-    far_got = exchange(far_slots, FAR, FAR_2)
+    far_got = exchange(far_slots, FAR, FAR_FIRST)
     return tuple(
         call(last_kernel, 1, 4, [f32s(*shares_init.shape), f32s(*freqs_init.shape)], [], False)(
             idx, far_got, own_sum, own_q, own_f

time: 112 us -> 111 us (level)
    all_to_all x7 -> x5, blocking collectives: 104 us -> 77.9 us  [exchange(): return lax.all_to_all(x, axes, 0, 0, tiled=True, axis_index_groups=order)]
    all_to_all x0 -> x2, blocking collectives: none -> 24.7 us  [wide_exchange(): return lax.all_to_all(x, AXES, 0, 0, tiled=True, axis_index_groups=groups)]
where the time goes in v10:
time: 111 us
  blocking collectives  103 us (93%)
  Pallas kernels  6.51 us (6%)
    all_to_all x5, blocking collectives, exchange(): return lax.all_to_all(x, axes, 0, 0, tiled=True, axis_index_groups=order)  77.9 us
    all_to_all x2, blocking collectives, wide_exchange(): return lax.all_to_all(x, AXES, 0, 0, tiled=True, axis_index_groups=groups)  24.7 us
    pallas_call x8, Pallas kernels, placed(): return run(*args)  6.51 us

profile of v10, /device:TPU:1, one launch (start us, length us, event | category | flops | bytes accessed | tf_op | source)
XLA Modules:
  0.0 110.6 jit_solution(17126025807032192074)
XLA Ops:
  0.6 0.0 copy-start.2
  0.7 0.0 copy-start.1
  0.7 0.7 copy-done.2
  1.3 0.0 copy-done.1
  1.4 0.1 shard_map.50
  1.5 21.3 %all_to_all.35.far_in = f32[48,2,128]{2,1,0:T(2,128)S(1)} all-to-all(f32[48,2,128]{2,1,0:T(2,128)S(1)} %get-tuple-element.17), channel_id=1, replica_groups={{2,0,18,16,34,32,50,48,66,64,82,80,98,96,114,112},{3,1,19,17,35,33,51,4..., dimensions={0} | all-to-all | bytes 98304 | tf_op jit(solution)/shard_map/all_to_all | solution.py:398
  22.8 0.1 shard_map.51
  22.9 0.0 copy-start
  22.9 13.7 %all_to_all.36.near_in = f32[96,4,128]{2,1,0:T(4,128)S(1)} all-to-all(f32[96,4,128]{2,1,0:T(4,128)S(1)} %get-tuple-element.19), channel_id=1, replica_groups={{265,264,269,268,257,256,261,260,393,392,397,396,385,384,389,388,9,8,13..., dimensions={0} | all-to-all | bytes 393216 | tf_op jit(solution)/shard_map/all_to_all | solution.py:398
  36.6 0.0 copy-done
  36.6 2.6 %shard_map.52 = (f32[64,4,128]{2,1,0:T(4,128)S(1)}, f32[16,1024]{1,0:T(8,128)S(1)}, f32[16,512]{1,0:T(8,128)S(1)}) custom-call(s32[1]{0:T(128)} %bitcast.idx, s32[64,512]{1,0:T(8,128)S(1)} %copy-done, f32[96,4,128]{2,1,0:T(4,128)S(1)} %all_to_all.36.near_in, f32[3,4,128]{2,1,0:T(4,128)S(1)} %get-tuple-element.20.own_f_in), custom_call_target="tpu_custom_call" | custom-call | tf_op jit(solution)/shard_map/pallas_call | solution.py:388
  39.2 12.2 %all_to_all.37.wide_in = f32[64,4,128]{2,1,0:T(4,128)S(1)} all-to-all(f32[64,4,128]{2,1,0:T(4,128)S(1)} %get-tuple-element.21), channel_id=1, replica_groups={{281,280,285,284,273,272,277,276,265,264,269,268,257,256,261,260,409,40..., dimensions={0} | all-to-all | bytes 262144 | tf_op jit(solution)/shard_map/all_to_all | solution.py:413
  51.3 0.1 shard_map.53
  51.5 15.0 %all_to_all.38.line_in = f32[24,4,128]{2,1,0:T(4,128)S(1)} all-to-all(f32[24,4,128]{2,1,0:T(4,128)S(1)} %get-tuple-element.22), channel_id=1, replica_groups={{2,0,34,32,66,64,98,96},{3,1,35,33,67,65,99,97},{6,4,38,36,70,68,102,10..., dimensions={0} | all-to-all | bytes 98304 | tf_op jit(solution)/shard_map/all_to_all | solution.py:398
  66.5 0.1 shard_map.54
  66.6 12.6 %all_to_all.39.wide_in = f32[64,4,128]{2,1,0:T(4,128)S(1)} all-to-all(f32[64,4,128]{2,1,0:T(4,128)S(1)} %shard_map.54), channel_id=1, replica_groups={{281,280,285,284,273,272,277,276,265,264,269,268,257,256,261,260,409,40..., dimensions={0} | all-to-all | bytes 262144 | tf_op jit(solution)/shard_map/all_to_all | solution.py:413
  79.2 2.5 %shard_map.55 = (f32[32,24,128]{2,1,0:T(8,128)S(1)}, f32[16,128]{1,0:T(8,128)S(1)}, f32[6,128]{1,0:T(8,128)S(1)}, f32[4,128]{1,0:T(4,128)S(1)}) custom-call(s32[1]{0:T(128)} %bitcast.idx, s32[64,512]{1,0:T(8,128)S(1)} %copy-done, f32[64,4,128]{2,1,0:T(4,128)S(1)} %all_to_all.39.wide_in, f32[16,1024]{1,0:T(8,128)S(1)} %get-tuple-element.24.q_in, ...), custom_call_target="tpu_custom_call" | custom-call | tf_op jit(solution)/shard_map/pallas_call | solution.py:388
  81.7 13.7 %all_to_all.40.near_in = f32[32,24,128]{2,1,0:T(8,128)S(1)} all-to-all(f32[32,24,128]{2,1,0:T(8,128)S(1)} %get-tuple-element.26), channel_id=1, replica_groups={{265,264,269,268,257,256,261,260,393,392,397,396,385,384,389,388,9,8,13..., dimensions={0} | all-to-all | bytes 786432 | tf_op jit(solution)/shard_map/all_to_all | solution.py:398
  95.4 0.1 shard_map.56
  95.5 14.3 %all_to_all.41.far_in = f32[48,2,128]{2,1,0:T(2,128)S(1)} all-to-all(f32[48,2,128]{2,1,0:T(2,128)S(1)} %get-tuple-element.28), channel_id=1, replica_groups={{2,0,18,16,34,32,50,48,66,64,82,80,98,96,114,112},{3,1,19,17,35,33,51,4..., dimensions={0} | all-to-all | bytes 98304 | tf_op jit(solution)/shard_map/all_to_all | solution.py:398
  109.8 0.8 shard_map.57
Async XLA Ops:
  0.6 0.7 copy-start.2
  0.7 0.7 copy-start.1
  22.9 13.7 %copy-start = (s32[64,512]{1,0:T(8,128)S(1)}, s32[64,512]{1,0:T(8,128)}, u32[]{:S(2)}) copy-start(s32[64,512]{1,0:T(8,128)} %dosage_ref.3) | copy-start | bytes 393220

commit v11 on v10

--- a/solution.py
+++ b/solution.py
@@ -127,6 +127,11 @@
     return i * N_ZH + h
 
 
+def near_slot(y, g):
+    m = in_plane(y, g) ^ NEAR_FIRST
+    return m & 1 | (m >> 4 & 1) << 1 | (m >> 2 & 1) << 2 | (m >> 3 & 1) << 3 | (m >> 1 & 1) << 4
+
+
 def in_wide(idx, member):
     return (member ^ WIDE_FIRST) ^ (8 - 8 * zh_of(idx))
 
@@ -191,7 +196,7 @@
     for s in range(N_NEAR):
         near_out[3 * s : 3 * s + 3] = f_out[...]
     for g in range(N_XC):
-        s = 3 * (in_plane(y_of(idx), g) ^ NEAR_FIRST)
+        s = 3 * near_slot(y_of(idx), g)
         for j in range(3):
             near_out[s + j] = q_tmp[4 * j : 4 * j + 4]
 
@@ -200,7 +205,7 @@
     rows = [[], [], []]
     for x in range(4):
         for j in range(3):
-            a, b = (near_in[3 * (in_plane(y_of(idx), 2 * x + c) ^ NEAR_FIRST) + j] for c in range(2))
+            a, b = (near_in[3 * near_slot(y_of(idx), 2 * x + c) + j] for c in range(2))
             rows[j].extend(halves(a, b))
     return padded(rows)
 
@@ -209,7 +214,7 @@
     rows = [[], [], []]
     for y in range(N_Y):
         for j in range(3):
-            got = near_in[3 * (in_plane(y, near_of(idx)) ^ NEAR_FIRST) + j]
+            got = near_in[3 * near_slot(y, near_of(idx)) + j]
             rows[j].append(jnp.where(y_of(idx) == y, f_in[j], got))
     return padded(rows)
 
@@ -317,21 +322,21 @@
         pair = halves(sum_q[:, tile(2 * x)], sum_q[:, tile(2 * x + 1)])
         for c in range(2):
             for y in range(N_Y):
-                near_out[in_plane(y, 2 * x + c) ^ NEAR_FIRST, 0:16] = pair[c]
-    sq_out[...] = near_out[in_plane(0, near_of(idx)) ^ NEAR_FIRST, 0:16]
+                near_out[near_slot(y, 2 * x + c), 0:16] = pair[c]
+    sq_out[...] = near_out[near_slot(0, near_of(idx)), 0:16]
     sa_tmp[0:12] = sum_a[0:12]
     sa_tmp[12:24] = sum_b[0:12]
     for y in range(N_Y):
-        near_out[in_plane(y, near_of(idx)) ^ NEAR_FIRST] = sa_tmp[:, tile(y)]
+        near_out[near_slot(y, near_of(idx))] = sa_tmp[:, tile(y)]
 
 
 def last_far_kernel(idx, near_in, sq_in, far_out, q_out):
     zh, near = zh_of(idx), near_of(idx)
     sum_q = sq_in[...]
     for g in range(N_XC):
-        got = near_in[in_plane(y_of(idx), g) ^ NEAR_FIRST, 0:16]
+        got = near_in[near_slot(y_of(idx), g), 0:16]
         sum_q = sum_q + jnp.where(near == g, 0.0, got)
-    sums = sum(near_in[in_plane(y, near) ^ NEAR_FIRST] for y in range(N_Y))
+    sums = sum(near_in[near_slot(y, near)] for y in range(N_Y))
     parts = halves(sum_q[0:6], sum_q[6:12])
     q_out[...] = jnp.where(zh == 0, parts[0], parts[1])
     block = block_of_lane()
@@ -390,12 +395,17 @@
     return placed
 
 
-def exchange(x, axes, first):
-    members = 1
-    for axis in axes:
-        members *= SIZES[AXES.index(axis)]
-    order = [[i ^ first for i in range(members)]]
-    return lax.all_to_all(x, axes, 0, 0, tiled=True, axis_index_groups=order)
+def exchange(x, axes, order):
+    return lax.all_to_all(x, axes, 0, 0, tiled=True, axis_index_groups=[order])
+
+
+def near_exchange(x):
+    slots = [near_slot(m // N_XC, m % N_XC) for m in range(N_NEAR)]
+    return exchange(x, NEAR, [slots.index(i) for i in range(N_NEAR)])
+
+
+def line_exchange(x, axes, members):
+    return exchange(x, axes, [i ^ FAR_FIRST for i in range(members)])
 
 
 def wide_exchange(x):
@@ -420,11 +430,11 @@
     far_slots, own_q = call(first_kernel, 1, 2, [pairs, f32s(8, LANES)], [vmem(8, LANES)])(
         idx, shares_init, freqs_init
     )
-    far_got = exchange(far_slots, FAR, FAR_FIRST)
+    far_got = line_exchange(far_slots, FAR, N_FAR)
     near_slots, own_f = call(
         first_near_kernel, 1, 2, [f32s(3 * N_NEAR, 4, LANES), f32s(3, 4, LANES)], [vmem(12, LANES)]
     )(idx, far_got, own_q)
-    near_got = exchange(near_slots, NEAR, NEAR_FIRST)
+    near_got = near_exchange(near_slots)
     slots, shares, freqs = call(
         one_kernel, 1, 3, [f32s(N_WIDE, 4, LANES), f32s(PAD, samples), f32s(PAD, variants)],
         [vmem(PAD, samples), vmem(24, variants), vmem(PAD, samples), vmem(24, variants)],
@@ -433,7 +443,7 @@
     line_slots, own_sum = call(
         wide_sums_kernel, 1, 1, [f32s(3 * N_LINE, 4, LANES), f32s(12, LANES)], [vmem(12, LANES)]
     )(idx, wide_got)
-    line_got = exchange(line_slots, LINE, FAR_FIRST)
+    line_got = line_exchange(line_slots, LINE, N_LINE)
     (wide_slots,) = call(
         line_sums_kernel, 1, 2, [f32s(N_WIDE, 4, LANES)], [vmem(12, LANES), vmem(12, LANES)]
     )(idx, line_got, own_sum)
@@ -443,11 +453,11 @@
         [f32s(N_NEAR, 24, LANES), f32s(PAD, LANES), f32s(6, LANES), f32s(4, LANES)],
         [vmem(PAD, samples), vmem(24, variants), vmem(PAD, samples), vmem(PAD, variants)],
     )(idx, dosage, wide_got, shares, freqs)
-    near_got = exchange(near_slots, NEAR, NEAR_FIRST)
+    near_got = near_exchange(near_slots)
     far_slots, own_sum = call(last_far_kernel, 1, 2, [pairs, f32s(6, LANES)], [])(
         idx, near_got, own_sum
     )
-    far_got = exchange(far_slots, FAR, FAR_FIRST)
+    far_got = line_exchange(far_slots, FAR, N_FAR)
     return tuple(
         call(last_kernel, 1, 4, [f32s(*shares_init.shape), f32s(*freqs_init.shape)], [], False)(
             idx, far_got, own_sum, own_q, own_f

time: 111 us -> 112 us (level)
  no operation moved by 1% of the time
where the time goes in v11:
time: 112 us; the launch traced here: 111 us
  blocking collectives  103 us (92%)
  Pallas kernels  6.55 us (6%)
    all_to_all x5, blocking collectives, exchange(): return lax.all_to_all(x, axes, 0, 0, tiled=True, axis_index_groups=[order])  78 us
    all_to_all x2, blocking collectives, wide_exchange(): return lax.all_to_all(x, AXES, 0, 0, tiled=True, axis_index_groups=groups)  25.2 us
    pallas_call x8, Pallas kernels, placed(): return run(*args)  6.55 us

profile of v11, /device:TPU:1, one launch (start us, length us, event | category | flops | bytes accessed | tf_op | source)
XLA Modules:
  0.0 111.1 jit_solution(10976665103088893584)
XLA Ops:
  0.6 0.0 copy-start.2
  0.7 0.0 copy-start.1
  0.7 0.7 copy-done.2
  1.3 0.0 copy-done.1
  1.4 0.1 shard_map.50
  1.5 21.3 %all_to_all.35.far_in = f32[48,2,128]{2,1,0:T(2,128)S(1)} all-to-all(f32[48,2,128]{2,1,0:T(2,128)S(1)} %get-tuple-element.17), channel_id=1, replica_groups={{2,0,18,16,34,32,50,48,66,64,82,80,98,96,114,112},{3,1,19,17,35,33,51,4..., dimensions={0} | all-to-all | bytes 98304 | tf_op jit(solution)/shard_map/all_to_all | solution.py:399
  22.8 0.1 shard_map.51
  22.9 0.0 copy-start
  22.9 13.4 %all_to_all.36.near_in = f32[96,4,128]{2,1,0:T(4,128)S(1)} all-to-all(f32[96,4,128]{2,1,0:T(4,128)S(1)} %get-tuple-element.19), channel_id=1, replica_groups={{265,264,9,8,257,256,1,0,393,392,137,136,385,384,129,128,269,268,13,12,..., dimensions={0} | all-to-all | bytes 393216 | tf_op jit(solution)/shard_map/all_to_all | solution.py:399
  36.4 0.0 copy-done
  36.4 2.6 %shard_map.52 = (f32[64,4,128]{2,1,0:T(4,128)S(1)}, f32[16,1024]{1,0:T(8,128)S(1)}, f32[16,512]{1,0:T(8,128)S(1)}) custom-call(s32[1]{0:T(128)} %bitcast.idx, s32[64,512]{1,0:T(8,128)S(1)} %copy-done, f32[96,4,128]{2,1,0:T(4,128)S(1)} %all_to_all.36.near_in, f32[3,4,128]{2,1,0:T(4,128)S(1)} %get-tuple-element.20.own_f_in), custom_call_target="tpu_custom_call" | custom-call | tf_op jit(solution)/shard_map/pallas_call | solution.py:393
  39.0 12.6 %all_to_all.37.wide_in = f32[64,4,128]{2,1,0:T(4,128)S(1)} all-to-all(f32[64,4,128]{2,1,0:T(4,128)S(1)} %get-tuple-element.21), channel_id=1, replica_groups={{281,280,285,284,273,272,277,276,265,264,269,268,257,256,261,260,409,40..., dimensions={0} | all-to-all | bytes 262144 | tf_op jit(solution)/shard_map/all_to_all | solution.py:423
  51.6 0.1 shard_map.53
  51.7 15.0 %all_to_all.38.line_in = f32[24,4,128]{2,1,0:T(4,128)S(1)} all-to-all(f32[24,4,128]{2,1,0:T(4,128)S(1)} %get-tuple-element.22), channel_id=1, replica_groups={{2,0,34,32,66,64,98,96},{3,1,35,33,67,65,99,97},{6,4,38,36,70,68,102,10..., dimensions={0} | all-to-all | bytes 98304 | tf_op jit(solution)/shard_map/all_to_all | solution.py:399
  66.8 0.1 shard_map.54
  66.9 12.6 %all_to_all.39.wide_in = f32[64,4,128]{2,1,0:T(4,128)S(1)} all-to-all(f32[64,4,128]{2,1,0:T(4,128)S(1)} %shard_map.54), channel_id=1, replica_groups={{281,280,285,284,273,272,277,276,265,264,269,268,257,256,261,260,409,40..., dimensions={0} | all-to-all | bytes 262144 | tf_op jit(solution)/shard_map/all_to_all | solution.py:423
  79.5 2.5 %shard_map.55 = (f32[32,24,128]{2,1,0:T(8,128)S(1)}, f32[16,128]{1,0:T(8,128)S(1)}, f32[6,128]{1,0:T(8,128)S(1)}, f32[4,128]{1,0:T(4,128)S(1)}) custom-call(s32[1]{0:T(128)} %bitcast.idx, s32[64,512]{1,0:T(8,128)S(1)} %copy-done, f32[64,4,128]{2,1,0:T(4,128)S(1)} %all_to_all.39.wide_in, f32[16,1024]{1,0:T(8,128)S(1)} %get-tuple-element.24.q_in, ...), custom_call_target="tpu_custom_call" | custom-call | tf_op jit(solution)/shard_map/pallas_call | solution.py:393
  82.0 13.6 %all_to_all.40.near_in = f32[32,24,128]{2,1,0:T(8,128)S(1)} all-to-all(f32[32,24,128]{2,1,0:T(8,128)S(1)} %get-tuple-element.26), channel_id=1, replica_groups={{265,264,9,8,257,256,1,0,393,392,137,136,385,384,129,128,269,268,13,12,..., dimensions={0} | all-to-all | bytes 786432 | tf_op jit(solution)/shard_map/all_to_all | solution.py:399
  95.6 0.1 shard_map.56
  95.7 14.6 %all_to_all.41.far_in = f32[48,2,128]{2,1,0:T(2,128)S(1)} all-to-all(f32[48,2,128]{2,1,0:T(2,128)S(1)} %get-tuple-element.28), channel_id=1, replica_groups={{2,0,18,16,34,32,50,48,66,64,82,80,98,96,114,112},{3,1,19,17,35,33,51,4..., dimensions={0} | all-to-all | bytes 98304 | tf_op jit(solution)/shard_map/all_to_all | solution.py:399
  110.3 0.8 shard_map.57
Async XLA Ops:
  0.6 0.7 copy-start.2
  0.7 0.7 copy-start.1
  22.9 13.5 %copy-start = (s32[64,512]{1,0:T(8,128)S(1)}, s32[64,512]{1,0:T(8,128)}, u32[]{:S(2)}) copy-start(s32[64,512]{1,0:T(8,128)} %dosage_ref.3) | copy-start | bytes 393220

commit v12 on v8

--- a/solution.py
+++ b/solution.py
@@ -241,7 +241,12 @@
         a = (sq_turn if t % 2 else sq_tmp)[3 * q : 3 * q + 3, tile(t // 2)]
         t, q = divmod(w, 8)
         b = (sa_tmp if t % 2 else sa_turn)[3 * q : 3 * q + 3, tile(t // 2)]
-        slots[w ^ WIDE_1, 0:3] = jnp.where(left, a, b)
+        put_wide(slots, w ^ WIDE_1, jnp.where(left, a, b))
+
+
+def put_wide(wide_out, at, rows):
+    for r in range(3):
+        wide_out[3 * at + r] = rows[r : r + 1]
 
 
 def put_line(line_out, at, rows):
@@ -250,12 +255,15 @@
 
 
 def wide_sums_kernel(idx, wide_in, line_out, q_out, a_tmp):
-    left = left_of(4)
-    row_sums = [sum(wide_in[in_plane(r, g) ^ WIDE_1] for g in range(N_XC)) for r in range(N_ROW)]
-    col_sums = [sum(wide_in[in_plane(r, g) ^ WIDE_1] for r in range(N_ROW)) for g in range(N_XC)]
-    for i in range(4):
-        q_out[3 * i : 3 * i + 3] = jnp.where(left, row_sums[i], roll(row_sums[i + 4], 64))[0:3]
-        a_tmp[3 * i : 3 * i + 3] = jnp.where(left, roll(col_sums[i], 64), col_sums[i + 4])[0:3]
+    left = left_of(1)
+    for r in range(3):
+        got = [[wide_in[3 * (in_plane(i, g) ^ WIDE_1) + r] for g in range(N_XC)] for i in range(N_ROW)]
+        row_sums = [sum(row) for row in got]
+        col_sums = [sum(row[g] for row in got) for g in range(N_XC)]
+        for i in range(4):
+            at = 3 * i + r
+            q_out[at : at + 1] = jnp.where(left, row_sums[i], roll(row_sums[i + 4], 64))
+            a_tmp[at : at + 1] = jnp.where(left, roll(col_sums[i], 64), col_sums[i + 4])
     for h in range(N_ZH):
         sent = jnp.where(zh_of(idx) == h, a_tmp[...], q_out[...])
         for i in range(N_ZQ):
@@ -276,19 +284,21 @@
         col_sums.append(roll(a_tmp[at : at + 3], 64 * (1 - i // 4)))
     for r in range(N_ROW):
         for g in range(N_XC):
-            wide_out[in_plane(r, g) ^ WIDE_2, 0:3] = jnp.where(left, row_sums[r], col_sums[g])
+            put_wide(wide_out, in_plane(r, g) ^ WIDE_2, jnp.where(left, row_sums[r], col_sums[g]))
 
 
 def two_kernel(idx, dosage_ref, wide_in, q_in, f_in, near_out, sq_out, own_q, own_f, sq_tmp, sa_tmp, q_tmp, f_tmp):
-    left = left_of(4)
+    left = left_of(1)
     for t in range(8):
         for q in range(4):
-            a, b = (wide_in[(8 * t + 4 * half + q) ^ WIDE_2] for half in range(2))
-            sq_tmp[3 * q : 3 * q + 3, tile(t)] = jnp.where(left, a, roll(b, 64))[0:3]
+            for r in range(3):
+                a, b = (wide_in[3 * ((8 * t + 4 * half + q) ^ WIDE_2) + r] for half in range(2))
+                sq_tmp[3 * q + r : 3 * q + r + 1, tile(t)] = jnp.where(left, a, roll(b, 64))
     for t in range(4):
         for q in range(8):
-            a, b = (wide_in[(16 * t + 8 * half + q) ^ WIDE_2] for half in range(2))
-            sa_tmp[3 * q : 3 * q + 3, tile(t)] = jnp.where(left, roll(a, 64), b)[0:3]
+            for r in range(3):
+                a, b = (wide_in[3 * ((16 * t + 8 * half + q) ^ WIDE_2) + r] for half in range(2))
+                sa_tmp[3 * q + r : 3 * q + r + 1, tile(t)] = jnp.where(left, roll(a, 64), b)
     q_tmp[...] = q_in[...]
     f_tmp[...] = f_in[...]
     numer = q_tmp[0:12] * sq_tmp[0:12]
@@ -408,7 +418,7 @@
     )(idx, far_got, own_q)
     near_got = exchange(near_slots, NEAR, NEAR_1)
     slots, shares, freqs = call(
-        one_kernel, 1, 3, [f32s(N_WIDE, 4, LANES), f32s(PAD, samples), f32s(PAD, variants)],
+        one_kernel, 1, 3, [f32s(3 * N_WIDE, 1, LANES), f32s(PAD, samples), f32s(PAD, variants)],
         [vmem(PAD, samples), vmem(24, variants), vmem(PAD, samples), vmem(24, variants)],
     )(idx, dosage, near_got, own_f)
     wide_got = exchange(slots, WIDE, WIDE_1)
@@ -417,7 +427,7 @@
     )(idx, wide_got)
     line_got = exchange(line_slots, LINE, LINE_1)
     (wide_slots,) = call(
-        line_sums_kernel, 1, 2, [f32s(N_WIDE, 4, LANES)], [vmem(12, LANES), vmem(12, LANES)]
+        line_sums_kernel, 1, 2, [f32s(3 * N_WIDE, 1, LANES)], [vmem(12, LANES), vmem(12, LANES)]
     )(idx, line_got, own_sum)
     wide_got = exchange(wide_slots, WIDE, WIDE_2)
     near_slots, own_sum, own_q, own_f = call(

time: 111 us -> 111 us (level)
  no operation moved by 1% of the time
where the time goes in v12:
time: 111 us; the launch traced here: 110 us
  blocking collectives  102 us (92%)
  Pallas kernels  6.53 us (6%)
    all_to_all x7, blocking collectives, exchange(): return lax.all_to_all(x, axes, 0, 0, tiled=True, axis_index_groups=order)  102 us
    pallas_call x8, Pallas kernels, placed(): return run(*args)  6.53 us

profile of v12, /device:TPU:1, one launch (start us, length us, event | category | flops | bytes accessed | tf_op | source)
XLA Modules:
  0.0 110.3 jit_solution(3337304209790603079)
XLA Ops:
  0.6 0.0 copy-start.2
  0.7 0.0 copy-start.1
  0.7 0.7 copy-done.2
  1.3 0.0 copy-done.1
  1.4 0.1 shard_map.50
  1.5 21.3 %all_to_all.35.far_in = f32[48,2,128]{2,1,0:T(2,128)S(1)} all-to-all(f32[48,2,128]{2,1,0:T(2,128)S(1)} %get-tuple-element.17), channel_id=1, replica_groups={{2,0,18,16,34,32,50,48,66,64,82,80,98,96,114,112},{3,1,19,17,35,33,51,4..., dimensions={0} | all-to-all | bytes 98304 | tf_op jit(solution)/shard_map/all_to_all | solution.py:405
  22.8 0.1 shard_map.51
  22.9 0.0 copy-start
  22.9 13.7 %all_to_all.36.near_in = f32[96,4,128]{2,1,0:T(4,128)S(1)} all-to-all(f32[96,4,128]{2,1,0:T(4,128)S(1)} %get-tuple-element.19), channel_id=1, replica_groups={{265,264,269,268,257,256,261,260,393,392,397,396,385,384,389,388,9,8,13..., dimensions={0} | all-to-all | bytes 393216 | tf_op jit(solution)/shard_map/all_to_all | solution.py:405
  36.6 0.0 copy-done
  36.6 2.6 %shard_map.52 = (f32[192,1,128]{2,1,0:T(1,128)S(1)}, f32[16,1024]{1,0:T(8,128)S(1)}, f32[16,512]{1,0:T(8,128)S(1)}) custom-call(s32[1]{0:T(128)} %bitcast.idx, s32[64,512]{1,0:T(8,128)S(1)} %copy-done, f32[96,4,128]{2,1,0:T(4,128)S(1)} %all_to_all.36.near_in, f32[3,4,128]{2,1,0:T(4,128)S(1)} %get-tuple-element.20.own_f_in), custom_call_target="tpu_custom_call" | custom-call | tf_op jit(solution)/shard_map/pallas_call | solution.py:395
  39.2 12.7 %all_to_all.37.wide_in = f32[192,1,128]{2,1,0:T(1,128)S(1)} all-to-all(f32[192,1,128]{2,1,0:T(1,128)S(1)} %get-tuple-element.21), channel_id=1, replica_groups={{265,264,269,268,257,256,261,260,281,280,285,284,273,272,277,276,393,39..., dimensions={0} | all-to-all | bytes 196608 | tf_op jit(solution)/shard_map/all_to_all | solution.py:405
  51.8 0.1 shard_map.53
  52.0 14.2 %all_to_all.38.line_in = f32[24,4,128]{2,1,0:T(4,128)S(1)} all-to-all(f32[24,4,128]{2,1,0:T(4,128)S(1)} %get-tuple-element.22), channel_id=1, replica_groups={{2,0,34,32,66,64,98,96},{3,1,35,33,67,65,99,97},{6,4,38,36,70,68,102,10..., dimensions={0} | all-to-all | bytes 98304 | tf_op jit(solution)/shard_map/all_to_all | solution.py:405
  66.2 0.1 shard_map.54
  66.3 12.5 %all_to_all.39.wide_in = f32[192,1,128]{2,1,0:T(1,128)S(1)} all-to-all(f32[192,1,128]{2,1,0:T(1,128)S(1)} %shard_map.54), channel_id=1, replica_groups={{265,264,269,268,257,256,261,260,281,280,285,284,273,272,277,276,393,39..., dimensions={0} | all-to-all | bytes 196608 | tf_op jit(solution)/shard_map/all_to_all | solution.py:405
  78.8 2.5 %shard_map.55 = (f32[32,24,128]{2,1,0:T(8,128)S(1)}, f32[16,128]{1,0:T(8,128)S(1)}, f32[6,128]{1,0:T(8,128)S(1)}, f32[4,128]{1,0:T(4,128)S(1)}) custom-call(s32[1]{0:T(128)} %bitcast.idx, s32[64,512]{1,0:T(8,128)S(1)} %copy-done, f32[192,1,128]{2,1,0:T(1,128)S(1)} %all_to_all.39.wide_in, f32[16,1024]{1,0:T(8,128)S(1)} %get-tuple-element.24.q_in, ...), custom_call_target="tpu_custom_call" | custom-call | tf_op jit(solution)/shard_map/pallas_call | solution.py:395
  81.4 13.7 %all_to_all.40.near_in = f32[32,24,128]{2,1,0:T(8,128)S(1)} all-to-all(f32[32,24,128]{2,1,0:T(8,128)S(1)} %get-tuple-element.26), channel_id=1, replica_groups={{265,264,269,268,257,256,261,260,393,392,397,396,385,384,389,388,9,8,13..., dimensions={0} | all-to-all | bytes 786432 | tf_op jit(solution)/shard_map/all_to_all | solution.py:405
  95.1 0.1 shard_map.56
  95.2 14.3 %all_to_all.41.far_in = f32[48,2,128]{2,1,0:T(2,128)S(1)} all-to-all(f32[48,2,128]{2,1,0:T(2,128)S(1)} %get-tuple-element.28), channel_id=1, replica_groups={{2,0,18,16,34,32,50,48,66,64,82,80,98,96,114,112},{3,1,19,17,35,33,51,4..., dimensions={0} | all-to-all | bytes 98304 | tf_op jit(solution)/shard_map/all_to_all | solution.py:405
  109.5 0.8 shard_map.57
Async XLA Ops:
  0.6 0.7 copy-start.2
  0.7 0.7 copy-start.1
  22.9 13.7 %copy-start = (s32[64,512]{1,0:T(8,128)S(1)}, s32[64,512]{1,0:T(8,128)}, u32[]{:S(2)}) copy-start(s32[64,512]{1,0:T(8,128)} %dosage_ref.3) | copy-start | bytes 393220

commit v13 on v12

--- a/solution.py
+++ b/solution.py
@@ -441,7 +441,7 @@
     )
     far_got = exchange(far_slots, FAR, FAR_2)
     return tuple(
-        call(last_kernel, 1, 4, [f32s(*shares_init.shape), f32s(*freqs_init.shape)], [], False)(
+        call(last_kernel, 1, 4, [f32s(*shares_init.shape), f32s(*freqs_init.shape)], [])(
             idx, far_got, own_sum, own_q, own_f
         )
     )

time: 111 us -> 111 us (level)
  local copies, waits for them, and re-layouts: 0.7 us -> 1.91 us
    unnamed x6 -> x8, local copies, waits for them, and re-layouts: 0.7 us -> 1.91 us
where the time goes in v13:
time: 111 us
  blocking collectives  102 us (92%)
  Pallas kernels  5.92 us (5%)
  local copies, waits for them, and re-layouts  1.91 us (2%)
    all_to_all x7, blocking collectives, exchange(): return lax.all_to_all(x, axes, 0, 0, tiled=True, axis_index_groups=order)  102 us
    pallas_call x8, Pallas kernels, placed(): return run(*args)  5.92 us

profile of v13, /device:TPU:1, one launch (start us, length us, event | category | flops | bytes accessed | tf_op | source)
XLA Modules:
  0.0 110.9 jit_solution(9664137575440279806)
XLA Ops:
  0.6 0.0 copy-start.2
  0.7 0.0 copy-start.1
  0.7 0.7 copy-done.2
  1.3 0.0 copy-done.1
  1.4 0.1 shard_map.50
  1.5 21.3 %all_to_all.35.far_in = f32[48,2,128]{2,1,0:T(2,128)S(1)} all-to-all(f32[48,2,128]{2,1,0:T(2,128)S(1)} %get-tuple-element.17), channel_id=1, replica_groups={{2,0,18,16,34,32,50,48,66,64,82,80,98,96,114,112},{3,1,19,17,35,33,51,4..., dimensions={0} | all-to-all | bytes 98304 | tf_op jit(solution)/shard_map/all_to_all | solution.py:405
  22.8 0.1 shard_map.51
  22.9 0.0 copy-start
  22.9 13.7 %all_to_all.36.near_in = f32[96,4,128]{2,1,0:T(4,128)S(1)} all-to-all(f32[96,4,128]{2,1,0:T(4,128)S(1)} %get-tuple-element.19), channel_id=1, replica_groups={{265,264,269,268,257,256,261,260,393,392,397,396,385,384,389,388,9,8,13..., dimensions={0} | all-to-all | bytes 393216 | tf_op jit(solution)/shard_map/all_to_all | solution.py:405
  36.6 0.0 copy-done
  36.6 2.6 %shard_map.52 = (f32[192,1,128]{2,1,0:T(1,128)S(1)}, f32[16,1024]{1,0:T(8,128)S(1)}, f32[16,512]{1,0:T(8,128)S(1)}) custom-call(s32[1]{0:T(128)} %bitcast.idx, s32[64,512]{1,0:T(8,128)S(1)} %copy-done, f32[96,4,128]{2,1,0:T(4,128)S(1)} %all_to_all.36.near_in, f32[3,4,128]{2,1,0:T(4,128)S(1)} %get-tuple-element.20.own_f_in), custom_call_target="tpu_custom_call" | custom-call | tf_op jit(solution)/shard_map/pallas_call | solution.py:395
  39.2 12.7 %all_to_all.37.wide_in = f32[192,1,128]{2,1,0:T(1,128)S(1)} all-to-all(f32[192,1,128]{2,1,0:T(1,128)S(1)} %get-tuple-element.21), channel_id=1, replica_groups={{265,264,269,268,257,256,261,260,281,280,285,284,273,272,277,276,393,39..., dimensions={0} | all-to-all | bytes 196608 | tf_op jit(solution)/shard_map/all_to_all | solution.py:405
  51.8 0.1 shard_map.53
  52.0 14.2 %all_to_all.38.line_in = f32[24,4,128]{2,1,0:T(4,128)S(1)} all-to-all(f32[24,4,128]{2,1,0:T(4,128)S(1)} %get-tuple-element.22), channel_id=1, replica_groups={{2,0,34,32,66,64,98,96},{3,1,35,33,67,65,99,97},{6,4,38,36,70,68,102,10..., dimensions={0} | all-to-all | bytes 98304 | tf_op jit(solution)/shard_map/all_to_all | solution.py:405
  66.2 0.1 shard_map.54
  66.3 12.5 %all_to_all.39.wide_in = f32[192,1,128]{2,1,0:T(1,128)S(1)} all-to-all(f32[192,1,128]{2,1,0:T(1,128)S(1)} %shard_map.54), channel_id=1, replica_groups={{265,264,269,268,257,256,261,260,281,280,285,284,273,272,277,276,393,39..., dimensions={0} | all-to-all | bytes 196608 | tf_op jit(solution)/shard_map/all_to_all | solution.py:405
  78.8 2.5 %shard_map.55 = (f32[32,24,128]{2,1,0:T(8,128)S(1)}, f32[16,128]{1,0:T(8,128)S(1)}, f32[6,128]{1,0:T(8,128)S(1)}, f32[4,128]{1,0:T(4,128)S(1)}) custom-call(s32[1]{0:T(128)} %bitcast.idx, s32[64,512]{1,0:T(8,128)S(1)} %copy-done, f32[192,1,128]{2,1,0:T(1,128)S(1)} %all_to_all.39.wide_in, f32[16,1024]{1,0:T(8,128)S(1)} %get-tuple-element.24.q_in, ...), custom_call_target="tpu_custom_call" | custom-call | tf_op jit(solution)/shard_map/pallas_call | solution.py:395
  81.4 13.7 %all_to_all.40.near_in = f32[32,24,128]{2,1,0:T(8,128)S(1)} all-to-all(f32[32,24,128]{2,1,0:T(8,128)S(1)} %get-tuple-element.26), channel_id=1, replica_groups={{265,264,269,268,257,256,261,260,393,392,397,396,385,384,389,388,9,8,13..., dimensions={0} | all-to-all | bytes 786432 | tf_op jit(solution)/shard_map/all_to_all | solution.py:405
  95.1 0.1 shard_map.56
  95.2 14.3 %all_to_all.41.far_in = f32[48,2,128]{2,1,0:T(2,128)S(1)} all-to-all(f32[48,2,128]{2,1,0:T(2,128)S(1)} %get-tuple-element.28), channel_id=1, replica_groups={{2,0,18,16,34,32,50,48,66,64,82,80,98,96,114,112},{3,1,19,17,35,33,51,4..., dimensions={0} | all-to-all | bytes 98304 | tf_op jit(solution)/shard_map/all_to_all | solution.py:405
  109.5 0.2 shard_map.57
  109.7 0.6 copy.5
  110.3 0.6 copy.6
Async XLA Ops:
  0.6 0.7 copy-start.2
  0.7 0.7 copy-start.1
  22.9 13.7 %copy-start = (s32[64,512]{1,0:T(8,128)S(1)}, s32[64,512]{1,0:T(8,128)}, u32[]{:S(2)}) copy-start(s32[64,512]{1,0:T(8,128)} %dosage_ref.3) | copy-start | bytes 393220

commit v14 on v12

--- a/solution.py
+++ b/solution.py
@@ -378,7 +378,7 @@
     return pltpu.VMEM(shape, f32)
 
 
-def call(kernel, scalars, n_in, outs, scratch, kept=True):
+def call(kernel, scalars, n_in, outs, scratch, kept=True, ready=True):
     spec = pl.BlockSpec(memory_space=pltpu.VMEM)
     run = pl.pallas_call(
         kernel,
@@ -394,7 +394,7 @@
         )
         return run(*args)
 
-    return placed
+    return placed if ready else run
 
 
 def exchange(x, axes, first):
@@ -409,7 +409,7 @@
     idx = lax.axis_index(AXES).astype(jnp.int32).reshape(1)
     samples, variants = 16 * dosage.shape[0], dosage.shape[1]
     pairs = f32s(3 * N_FAR, 2, LANES)
-    far_slots, own_q = call(first_kernel, 1, 2, [pairs, f32s(8, LANES)], [vmem(8, LANES)])(
+    far_slots, own_q = call(first_kernel, 1, 2, [pairs, f32s(8, LANES)], [vmem(8, LANES)], ready=False)(
         idx, shares_init, freqs_init
     )
     far_got = exchange(far_slots, FAR, FAR_1)

time: 111 us -> 111 us (level)
    pallas_call x8 -> x7, Pallas kernels: 6.53 us -> 6.39 us  [placed(): return run(*args)]
where the time goes in v14:
time: 111 us; the launch traced here: 110 us
  blocking collectives  102 us (92%)
  Pallas kernels  7.24 us (7%)
    all_to_all x7, blocking collectives, exchange(): return lax.all_to_all(x, axes, 0, 0, tiled=True, axis_index_groups=order)  102 us
    pallas_call x7, Pallas kernels, placed(): return run(*args)  6.39 us

profile of v14, /device:TPU:1, one launch (start us, length us, event | category | flops | bytes accessed | tf_op | source)
XLA Modules:
  0.0 110.3 jit_solution(12882671518500808327)
XLA Ops:
  0.6 0.9 shard_map.50
  1.5 21.3 %all_to_all.35.far_in = f32[48,2,128]{2,1,0:T(2,128)S(1)} all-to-all(f32[48,2,128]{2,1,0:T(2,128)S(1)} %get-tuple-element.17), channel_id=1, replica_groups={{2,0,18,16,34,32,50,48,66,64,82,80,98,96,114,112},{3,1,19,17,35,33,51,4..., dimensions={0} | all-to-all | bytes 98304 | tf_op jit(solution)/shard_map/all_to_all | solution.py:405
  22.8 0.1 shard_map.51
  22.9 0.0 copy-start
  22.9 13.7 %all_to_all.36.near_in = f32[96,4,128]{2,1,0:T(4,128)S(1)} all-to-all(f32[96,4,128]{2,1,0:T(4,128)S(1)} %get-tuple-element.19), channel_id=1, replica_groups={{265,264,269,268,257,256,261,260,393,392,397,396,385,384,389,388,9,8,13..., dimensions={0} | all-to-all | bytes 393216 | tf_op jit(solution)/shard_map/all_to_all | solution.py:405
  36.6 0.0 copy-done
  36.6 2.6 %shard_map.52 = (f32[192,1,128]{2,1,0:T(1,128)S(1)}, f32[16,1024]{1,0:T(8,128)S(1)}, f32[16,512]{1,0:T(8,128)S(1)}) custom-call(s32[1]{0:T(128)} %bitcast.idx, s32[64,512]{1,0:T(8,128)S(1)} %copy-done, f32[96,4,128]{2,1,0:T(4,128)S(1)} %all_to_all.36.near_in, f32[3,4,128]{2,1,0:T(4,128)S(1)} %get-tuple-element.20.own_f_in), custom_call_target="tpu_custom_call" | custom-call | tf_op jit(solution)/shard_map/pallas_call | solution.py:395
  39.2 12.7 %all_to_all.37.wide_in = f32[192,1,128]{2,1,0:T(1,128)S(1)} all-to-all(f32[192,1,128]{2,1,0:T(1,128)S(1)} %get-tuple-element.21), channel_id=1, replica_groups={{265,264,269,268,257,256,261,260,281,280,285,284,273,272,277,276,393,39..., dimensions={0} | all-to-all | bytes 196608 | tf_op jit(solution)/shard_map/all_to_all | solution.py:405
  51.8 0.1 shard_map.53
  52.0 14.2 %all_to_all.38.line_in = f32[24,4,128]{2,1,0:T(4,128)S(1)} all-to-all(f32[24,4,128]{2,1,0:T(4,128)S(1)} %get-tuple-element.22), channel_id=1, replica_groups={{2,0,34,32,66,64,98,96},{3,1,35,33,67,65,99,97},{6,4,38,36,70,68,102,10..., dimensions={0} | all-to-all | bytes 98304 | tf_op jit(solution)/shard_map/all_to_all | solution.py:405
  66.2 0.1 shard_map.54
  66.3 12.5 %all_to_all.39.wide_in = f32[192,1,128]{2,1,0:T(1,128)S(1)} all-to-all(f32[192,1,128]{2,1,0:T(1,128)S(1)} %shard_map.54), channel_id=1, replica_groups={{265,264,269,268,257,256,261,260,281,280,285,284,273,272,277,276,393,39..., dimensions={0} | all-to-all | bytes 196608 | tf_op jit(solution)/shard_map/all_to_all | solution.py:405
  78.8 2.5 %shard_map.55 = (f32[32,24,128]{2,1,0:T(8,128)S(1)}, f32[16,128]{1,0:T(8,128)S(1)}, f32[6,128]{1,0:T(8,128)S(1)}, f32[4,128]{1,0:T(4,128)S(1)}) custom-call(s32[1]{0:T(128)} %bitcast.idx, s32[64,512]{1,0:T(8,128)S(1)} %copy-done, f32[192,1,128]{2,1,0:T(1,128)S(1)} %all_to_all.39.wide_in, f32[16,1024]{1,0:T(8,128)S(1)} %get-tuple-element.24.q_in, ...), custom_call_target="tpu_custom_call" | custom-call | tf_op jit(solution)/shard_map/pallas_call | solution.py:395
  81.4 13.7 %all_to_all.40.near_in = f32[32,24,128]{2,1,0:T(8,128)S(1)} all-to-all(f32[32,24,128]{2,1,0:T(8,128)S(1)} %get-tuple-element.26), channel_id=1, replica_groups={{265,264,269,268,257,256,261,260,393,392,397,396,385,384,389,388,9,8,13..., dimensions={0} | all-to-all | bytes 786432 | tf_op jit(solution)/shard_map/all_to_all | solution.py:405
  95.1 0.1 shard_map.56
  95.2 14.3 %all_to_all.41.far_in = f32[48,2,128]{2,1,0:T(2,128)S(1)} all-to-all(f32[48,2,128]{2,1,0:T(2,128)S(1)} %get-tuple-element.28), channel_id=1, replica_groups={{2,0,18,16,34,32,50,48,66,64,82,80,98,96,114,112},{3,1,19,17,35,33,51,4..., dimensions={0} | all-to-all | bytes 98304 | tf_op jit(solution)/shard_map/all_to_all | solution.py:405
  109.5 0.8 shard_map.57
Async XLA Ops:
  22.9 13.7 %copy-start = (s32[64,512]{1,0:T(8,128)S(1)}, s32[64,512]{1,0:T(8,128)}, u32[]{:S(2)}) copy-start(s32[64,512]{1,0:T(8,128)} %dosage_ref.3) | copy-start | bytes 393220
